TPU v7x, 32 devices: a whole 2x2x4 slice. The times are simulated.
32 devices in a mesh: tok: 16 (over z, x, core), grp: 2 (over y).
Axes of the slice: x: 2, y: 2, z: 4, core: 2. Of those that a mesh axis runs over, the one named last changes fastest.
Arguments:
- queries: bfloat16 [2, 2048, 3072], P('grp', 'tok'), may hold values from -20 to 20, as said below
- keys: bfloat16 [2, 2048, 3072], P('grp', 'tok'), may hold values from -20 to 20, as said below
- values: bfloat16 [2, 2048, 3072], P('grp', 'tok'), may hold values from -10 to 10, as said below
- next_latent: bfloat16 [2, 2048, 3072], P('grp', 'tok'), may hold values from -20 to 20, as said below
- clip_blocks: int32 [2, 4], P('grp'), may hold values from 1 to 8, 16 in all within a row
- valid_counts: int32 [2, 16], P('grp'), may hold values from 32 to 128
- group_ids: int32 [2, 4], P('grp'), may hold values from 0 to 3
- rewards: float32 [2, 4], P('grp'), may hold values from -6 to 6
Outputs:
- velocity: bfloat16 [2, 2048, 3072], P('grp', 'tok')
- loss: float32 [], replicated
Inputs may be any that keep to these rules, and one draw needn't show every extreme that they name: queries drawn within the range. keys drawn within the range. values drawn within the range. `next_latent`: next latents drawn within the range.
All inputs are finite; a program needn't handle non-finite values.
Results may differ from a plain program's by a relative error of at most 0.0034.
Values may be sent and summed in bfloat16 or wider, within the bound.
No kernel may reach another device: no remote copies, remote signals or barrier semaphores. Data moves between devices by JAX's collectives and lax.ppermute only.
A program may use at most 128 MiB of HBM per device.

v0:
```python
import math

import jax
import jax.numpy as jnp
from jax import lax
from jax.sharding import PartitionSpec as P

D = 3072
HEADS = 24
HEAD = 128
BLK = 128
MAXB = 8
GROUPS = 4


masked_score = -1e30


def passed_along(value, axis, steps):
    count = lax.axis_size(axis)
    first, last = (max(0, -steps), min(count, count - steps))
    return lax.ppermute(value, axis, [(source, source + steps) for source in range(first, last)])


def block_clips(clip_row, total_blocks):
    ends = jnp.cumsum(clip_row)
    positions = jnp.arange(total_blocks, dtype=jnp.int32)
    return jnp.sum((ends[None, :] <= positions[:, None]).astype(jnp.int32), axis=1)


def advantages(reward_row, group_row):
    member = (group_row[:, None] == jnp.arange(GROUPS, dtype=jnp.int32)[None, :]).astype(
        jnp.float32
    )
    totals = jnp.sum(member * reward_row[:, None], axis=0)
    counts = jnp.sum(member, axis=0)
    means = totals / jnp.maximum(counts, 1.0)
    return reward_row - jnp.sum(member * means[None, :], axis=1)


def clip_tokens(block_clip, valid_row, clips):
    member = (block_clip[:, None] == jnp.arange(clips, dtype=jnp.int32)[None, :]).astype(
        jnp.float32
    )
    return jnp.sum(member * valid_row.astype(jnp.float32)[:, None], axis=0)


def attend(query_block, key_rows, value_rows, allowed):
    width = query_block.shape[0]
    count = key_rows.shape[0]
    query_heads = query_block.reshape(width, HEADS, HEAD)
    key_heads = key_rows.reshape(count, HEADS, HEAD)
    value_heads = value_rows.reshape(count, HEADS, HEAD)
    scores = jnp.einsum(
        "qhd,khd->hqk", query_heads, key_heads, preferred_element_type=jnp.float32
    ) * (1.0 / math.sqrt(HEAD))
    scores = jnp.where(allowed[None, None, :], scores, masked_score)
    top = jnp.max(scores, axis=-1, keepdims=True)
    expo = jnp.exp(scores - top)
    probs = (expo / jnp.sum(expo, axis=-1, keepdims=True)).astype(jnp.bfloat16)
    mixed = jnp.einsum("hqk,khd->qhd", probs, value_heads, preferred_element_type=jnp.float32)
    return mixed.reshape(width, HEADS * HEAD)


def on_device(queries, keys, values, next_latent, clip_blocks, valid_counts, group_ids, rewards):
    query_rows = queries[0]
    rows = query_rows.shape[0]
    blocks_dev = rows // BLK
    devices = lax.axis_size("tok")
    own_index = lax.axis_index("tok")
    valid_row = valid_counts[0]
    total_blocks = valid_row.shape[0]
    block_clip = block_clips(clip_blocks[0], total_blocks)
    reach = (MAXB + blocks_dev - 2) // blocks_dev
    packed = jnp.stack([keys[0], values[0]])
    pieces = [(0, packed)]
    upward = packed
    downward = packed
    for distance in range(1, reach + 1):
        upward = passed_along(upward, "tok", 1)
        downward = passed_along(downward, "tok", -1)
        pieces.append((distance, upward))
        pieces.append((-distance, downward))
    slots = jnp.arange(BLK, dtype=jnp.int32)
    key_list = []
    value_list = []
    clip_list = []
    live_list = []
    for offset, piece in pieces:
        source = own_index - offset
        block_ids = source * blocks_dev + jnp.arange(blocks_dev, dtype=jnp.int32)
        inside = (source >= 0) & (source < devices)
        safe_ids = jnp.clip(block_ids, 0, total_blocks - 1)
        clips_here = jnp.where(inside, jnp.take(block_clip, safe_ids), -1)
        counts_here = jnp.where(inside, jnp.take(valid_row, safe_ids), 0)
        key_list.append(piece[0])
        value_list.append(piece[1])
        clip_list.append(jnp.repeat(clips_here, BLK, total_repeat_length=blocks_dev * BLK))
        live_list.append((slots[None, :] < counts_here[:, None]).reshape(-1))
    key_all = jnp.concatenate(key_list, axis=0)
    value_all = jnp.concatenate(value_list, axis=0)
    key_clip = jnp.concatenate(clip_list, axis=0)
    key_live = jnp.concatenate(live_list, axis=0)
    own_ids = own_index * blocks_dev + jnp.arange(blocks_dev, dtype=jnp.int32)
    own_clip = jnp.take(block_clip, own_ids[0])
    allowed = (key_clip == own_clip) & key_live
    mixed = attend(query_rows, key_all, value_all, allowed)
    live = slots < jnp.take(valid_row, own_ids[0])
    outputs = jnp.where(live[:, None], mixed, 0.0).astype(jnp.bfloat16)
    diff = next_latent[0].astype(jnp.float32) - outputs.astype(jnp.float32)
    token_err = jnp.sum(diff * diff, axis=-1).reshape(blocks_dev, BLK)
    own_valid = jnp.take(valid_row, own_ids)
    block_err = jnp.sum(
        token_err * (slots[None, :] < own_valid[:, None]).astype(jnp.float32), axis=1
    )
    adv = advantages(rewards[0], group_ids[0])
    tokens_of = clip_tokens(block_clip, valid_row, clip_blocks.shape[1])
    own_clips = jnp.take(block_clip, own_ids)
    terms = jnp.take(adv, own_clips) * block_err / (2.0 * D * jnp.take(tokens_of, own_clips))
    total = lax.psum(jnp.sum(terms), ("tok", "grp"))
    return (outputs[None], total)


def solution(mesh):
    return jax.shard_map(
        on_device,
        mesh=mesh,
        in_specs=(
            P("grp", "tok", None),
            P("grp", "tok", None),
            P("grp", "tok", None),
            P("grp", "tok", None),
            P("grp", None),
            P("grp", None),
            P("grp", None),
            P("grp", None),
        ),
        out_specs=(P("grp", "tok", None), P()),
        check_vma=False,
    )
```

profile of v0, /device:TPU:0, one launch (start us, length us, event | category | flops | bytes accessed | tf_op | source)
XLA Modules:
  0.0 368.5 jit_solution(5354640992449593383)
XLA Ops:
  0.6 1.5 copy.52
  2.1 1.5 copy.53
  3.7 1.3 pad_maximum_fusion
  4.9 3.6 collective-permute-start
  8.6 1.3 collective-permute-start.1
  10.6 2.0 constant_dynamic-slice_fusion
  37.6 2.2 copy.76
  49.0 5.1 %collective-permute-start.2 = (bf16[2,128,3072]{1,2,0:T(8,128)(2,1)}, bf16[2,128,3072]{1,2,0:T(8,128)(2,1)}, u32[]{:S(2)}, u32[]{:S(2)}) collective-permute-start(bf16[2,128,3072]{1,2,0:T(8,128)(2,1)} %collective-permute-done), channel_id=1, source_target_pairs={{0,2},{2,4},{4,6},{6,8},{8,10},{10,12},{12,14},{14,16},{16,18},{18... | collective-permute-start | bytes 4718600 | tf_op jit(solution)/shard_map/ppermute | solution.py:22
  54.1 1.5 fusion.53
  55.5 1.3 collective-permute-start.3
  56.8 2.4 fusion.52
  59.6 1.5 copy.58
  65.2 27.0 %collective-permute-start.4 = (bf16[2,128,3072]{1,2,0:T(8,128)(2,1)}, bf16[2,128,3072]{1,2,0:T(8,128)(2,1)}, u32[]{:S(2)}, u32[]{:S(2)}) collective-permute-start(bf16[2,128,3072]{1,2,0:T(8,128)(2,1)} %collective-permute-done.2), channel_id=1, source_target_pairs={{0,2},{2,4},{4,6},{6,8},{8,10},{10,12},{12,14},{14,16},{16,18},{18... | collective-permute-start | bytes 4718600 | tf_op jit(solution)/shard_map/ppermute | solution.py:22
  92.2 1.5 fusion.51
  93.7 1.3 collective-permute-start.5
  95.0 2.4 fusion.50
  97.8 1.5 copy.60
  99.3 1.1 constant_dynamic-update-slice_fusion.11
  103.4 44.5 %collective-permute-start.6 = (bf16[2,128,3072]{1,2,0:T(8,128)(2,1)}, bf16[2,128,3072]{1,2,0:T(8,128)(2,1)}, u32[]{:S(2)}, u32[]{:S(2)}) collective-permute-start(bf16[2,128,3072]{1,2,0:T(8,128)(2,1)} %collective-permute-done.4), channel_id=1, source_target_pairs={{0,2},{2,4},{4,6},{6,8},{8,10},{10,12},{12,14},{14,16},{16,18},{18... | collective-permute-start | bytes 4718600 | tf_op jit(solution)/shard_map/ppermute | solution.py:22
  147.9 1.5 fusion.49
  149.4 1.3 collective-permute-start.7
  150.7 2.4 fusion.48
  153.5 1.5 copy.62
  159.1 11.0 %collective-permute-start.8 = (bf16[2,128,3072]{1,2,0:T(8,128)(2,1)}, bf16[2,128,3072]{1,2,0:T(8,128)(2,1)}, u32[]{:S(2)}, u32[]{:S(2)}) collective-permute-start(bf16[2,128,3072]{1,2,0:T(8,128)(2,1)} %collective-permute-done.6), channel_id=1, source_target_pairs={{0,2},{2,4},{4,6},{6,8},{8,10},{10,12},{12,14},{14,16},{16,18},{18... | collective-permute-start | bytes 4718600 | tf_op jit(solution)/shard_map/ppermute | solution.py:22
  170.0 1.5 fusion.47
  171.5 1.5 collective-permute-start.9
  173.0 2.4 fusion.46
  175.7 1.5 copy.64
  179.3 1.1 constant_dynamic-update-slice_fusion.23
  181.4 27.5 %collective-permute-start.10 = (bf16[2,128,3072]{1,2,0:T(8,128)(2,1)}, bf16[2,128,3072]{1,2,0:T(8,128)(2,1)}, u32[]{:S(2)}, u32[]{:S(2)}) collective-permute-start(bf16[2,128,3072]{1,2,0:T(8,128)(2,1)} %collective-permute-done.8), channel_id=1, source_target_pairs={{0,2},{2,4},{4,6},{6,8},{8,10},{10,12},{12,14},{14,16},{16,18},{18... | collective-permute-start | bytes 4718600 | tf_op jit(solution)/shard_map/ppermute | solution.py:22
  208.9 1.5 fusion.45
  210.4 1.3 collective-permute-start.11
  211.7 2.4 fusion.44
  214.4 1.5 copy.66
  220.0 27.8 %collective-permute-start.12 = (bf16[2,128,3072]{1,2,0:T(8,128)(2,1)}, bf16[2,128,3072]{1,2,0:T(8,128)(2,1)}, u32[]{:S(2)}, u32[]{:S(2)}) collective-permute-start(bf16[2,128,3072]{1,2,0:T(8,128)(2,1)} %collective-permute-done.10), channel_id=1, source_target_pairs={{0,2},{2,4},{4,6},{6,8},{8,10},{10,12},{12,14},{14,16},{16,18},{18... | collective-permute-start | bytes 4718600 | tf_op jit(solution)/shard_map/ppermute | solution.py:22
  247.8 1.5 fusion.43
  249.3 1.3 collective-permute-start.13
  250.6 2.4 fusion.42
  253.3 1.5 copy.68
  254.9 1.1 constant_dynamic-update-slice_fusion.3
  255.9 1.2 constant_dynamic-update-slice_fusion.2
  259.1 1.5 fusion.41
  261.0 2.4 fusion.40
  263.4 1.5 copy.70
  268.9 12.8 %fusion.55 = f32[24,128]{1,0:T(8,128)S(1)} fusion(pred[1920]{0:T(1024)(128)(4,1)S(1)} %compare_and_fusion, bf16[1920,24,128]{2,0,1:T(8,128)(2,1)} %constant_dynamic-update-slice_fusion.16, bf16[128,24,128]{2,1,0:T(8,128)(2,1)} %bitcast.191), kind=kOutput, calls=%fused_computation.134 | convolution fusion | flops 1533544320 | bytes 12597120 | tf_op jit(solution)/shard_map/sub | solution.py:59
  281.7 15.5 %fusion.8 = bf16[24,128,128]{2,1,0:T(8,128)(2,1)S(1)} fusion(bf16[1920,24,128]{0,2,1:T(8,128)(2,1)} %constant_dynamic-update-slice_fusion, f32[24,128]{1,0:T(8,128)S(1)} %fusion.55, pred[1920]{0:T(1024)(128)(4,1)S(1)} %compare_and_fusion, bf16[1920,24,128]{2,0,1:T(8,128)(2,1)} %constant_dynamic-update-slice_fusion.16, bf16[128,24,128]{2,1,0:T(8,128)(2,1)S(1)} %bitcast.192), kind=kOutput, calls=%fused_computation.10 | convolution fusion | flops 3049395200 | bytes 25180032 | tf_op jit(solution)/shard_map/hqk,khd->qhd/dot_general | solution.py:61
  297.8 1.1 select_convert_fusion.1
  300.7 67.8 %psum.7 = f32[]{:T(128)} all-reduce(f32[]{:T(128)} %bitcast.125), channel_id=1, replica_groups=mesh['tok'=16,'grp'=2] {'tok','grp'}, use_global_device_ids=true, to_apply=%region_10.12 | all-reduce | flops 1 | bytes 8 | tf_op jit(solution)/shard_map/psum | solution.py:120
  (116 shorter events, 40.5 us)
Async XLA Ops:
  4.9 44.0 %collective-permute-start = (bf16[2,128,3072]{1,2,0:T(8,128)(2,1)}, bf16[2,128,3072]{1,2,0:T(8,128)(2,1)}, u32[]{:S(2)}, u32[]{:S(2)}) collective-permute-start(bf16[2,128,3072]{1,2,0:T(8,128)(2,1)} %pad_maximum_fusion), channel_id=1, source_target_pairs={{0,2},{2,4},{4,6},{6,8},{8,10},{10,12},{12,14},{14,16},{16,18},{18... | collective-permute-start | bytes 4718600 | tf_op jit(solution)/shard_map/ppermute | solution.py:22
  8.6 47.0 %collective-permute-start.1 = (bf16[2,128,3072]{1,2,0:T(8,128)(2,1)}, bf16[2,128,3072]{1,2,0:T(8,128)(2,1)}, u32[]{:S(2)}, u32[]{:S(2)}) collective-permute-start(bf16[2,128,3072]{1,2,0:T(8,128)(2,1)} %pad_maximum_fusion), channel_id=1, source_target_pairs={{2,0},{4,2},{6,4},{8,6},{10,8},{12,10},{14,12},{16,14},{18,16},{20... | collective-permute-start | bytes 4718600 | tf_op jit(solution)/shard_map/ppermute | solution.py:22
  49.0 16.3 %collective-permute-start.2 = (bf16[2,128,3072]{1,2,0:T(8,128)(2,1)}, bf16[2,128,3072]{1,2,0:T(8,128)(2,1)}, u32[]{:S(2)}, u32[]{:S(2)}) collective-permute-start(bf16[2,128,3072]{1,2,0:T(8,128)(2,1)} %collective-permute-done), channel_id=1, source_target_pairs={{0,2},{2,4},{4,6},{6,8},{8,10},{10,12},{12,14},{14,16},{16,18},{18... | collective-permute-start | bytes 4718600 | tf_op jit(solution)/shard_map/ppermute | solution.py:22
  55.5 38.2 %collective-permute-start.3 = (bf16[2,128,3072]{1,2,0:T(8,128)(2,1)}, bf16[2,128,3072]{1,2,0:T(8,128)(2,1)}, u32[]{:S(2)}, u32[]{:S(2)}) collective-permute-start(bf16[2,128,3072]{1,2,0:T(8,128)(2,1)} %collective-permute-done.1), channel_id=1, source_target_pairs={{2,0},{4,2},{6,4},{8,6},{10,8},{12,10},{14,12},{16,14},{18,16},{20... | collective-permute-start | bytes 4718600 | tf_op jit(solution)/shard_map/ppermute | solution.py:22
  65.2 38.2 %collective-permute-start.4 = (bf16[2,128,3072]{1,2,0:T(8,128)(2,1)}, bf16[2,128,3072]{1,2,0:T(8,128)(2,1)}, u32[]{:S(2)}, u32[]{:S(2)}) collective-permute-start(bf16[2,128,3072]{1,2,0:T(8,128)(2,1)} %collective-permute-done.2), channel_id=1, source_target_pairs={{0,2},{2,4},{4,6},{6,8},{8,10},{10,12},{12,14},{14,16},{16,18},{18... | collective-permute-start | bytes 4718600 | tf_op jit(solution)/shard_map/ppermute | solution.py:22
  93.7 55.7 %collective-permute-start.5 = (bf16[2,128,3072]{1,2,0:T(8,128)(2,1)}, bf16[2,128,3072]{1,2,0:T(8,128)(2,1)}, u32[]{:S(2)}, u32[]{:S(2)}) collective-permute-start(bf16[2,128,3072]{1,2,0:T(8,128)(2,1)} %collective-permute-done.3), channel_id=1, source_target_pairs={{2,0},{4,2},{6,4},{8,6},{10,8},{12,10},{14,12},{16,14},{18,16},{20... | collective-permute-start | bytes 4718600 | tf_op jit(solution)/shard_map/ppermute | solution.py:22
  103.4 55.7 %collective-permute-start.6 = (bf16[2,128,3072]{1,2,0:T(8,128)(2,1)}, bf16[2,128,3072]{1,2,0:T(8,128)(2,1)}, u32[]{:S(2)}, u32[]{:S(2)}) collective-permute-start(bf16[2,128,3072]{1,2,0:T(8,128)(2,1)} %collective-permute-done.4), channel_id=1, source_target_pairs={{0,2},{2,4},{4,6},{6,8},{8,10},{10,12},{12,14},{14,16},{16,18},{18... | collective-permute-start | bytes 4718600 | tf_op jit(solution)/shard_map/ppermute | solution.py:22
  149.4 22.1 %collective-permute-start.7 = (bf16[2,128,3072]{1,2,0:T(8,128)(2,1)}, bf16[2,128,3072]{1,2,0:T(8,128)(2,1)}, u32[]{:S(2)}, u32[]{:S(2)}) collective-permute-start(bf16[2,128,3072]{1,2,0:T(8,128)(2,1)} %collective-permute-done.5), channel_id=1, source_target_pairs={{2,0},{4,2},{6,4},{8,6},{10,8},{12,10},{14,12},{16,14},{18,16},{20... | collective-permute-start | bytes 4718600 | tf_op jit(solution)/shard_map/ppermute | solution.py:22
  159.1 22.3 %collective-permute-start.8 = (bf16[2,128,3072]{1,2,0:T(8,128)(2,1)}, bf16[2,128,3072]{1,2,0:T(8,128)(2,1)}, u32[]{:S(2)}, u32[]{:S(2)}) collective-permute-start(bf16[2,128,3072]{1,2,0:T(8,128)(2,1)} %collective-permute-done.6), channel_id=1, source_target_pairs={{0,2},{2,4},{4,6},{6,8},{8,10},{10,12},{12,14},{14,16},{16,18},{18... | collective-permute-start | bytes 4718600 | tf_op jit(solution)/shard_map/ppermute | solution.py:22
  171.5 38.8 %collective-permute-start.9 = (bf16[2,128,3072]{1,2,0:T(8,128)(2,1)}, bf16[2,128,3072]{1,2,0:T(8,128)(2,1)}, u32[]{:S(2)}, u32[]{:S(2)}) collective-permute-start(bf16[2,128,3072]{1,2,0:T(8,128)(2,1)} %collective-permute-done.7), channel_id=1, source_target_pairs={{2,0},{4,2},{6,4},{8,6},{10,8},{12,10},{14,12},{16,14},{18,16},{20... | collective-permute-start | bytes 4718600 | tf_op jit(solution)/shard_map/ppermute | solution.py:22
  181.4 38.7 %collective-permute-start.10 = (bf16[2,128,3072]{1,2,0:T(8,128)(2,1)}, bf16[2,128,3072]{1,2,0:T(8,128)(2,1)}, u32[]{:S(2)}, u32[]{:S(2)}) collective-permute-start(bf16[2,128,3072]{1,2,0:T(8,128)(2,1)} %collective-permute-done.8), channel_id=1, source_target_pairs={{0,2},{2,4},{4,6},{6,8},{8,10},{10,12},{12,14},{14,16},{16,18},{18... | collective-permute-start | bytes 4718600 | tf_op jit(solution)/shard_map/ppermute | solution.py:22
  210.4 38.9 %collective-permute-start.11 = (bf16[2,128,3072]{1,2,0:T(8,128)(2,1)}, bf16[2,128,3072]{1,2,0:T(8,128)(2,1)}, u32[]{:S(2)}, u32[]{:S(2)}) collective-permute-start(bf16[2,128,3072]{1,2,0:T(8,128)(2,1)} %collective-permute-done.9), channel_id=1, source_target_pairs={{2,0},{4,2},{6,4},{8,6},{10,8},{12,10},{14,12},{16,14},{18,16},{20... | collective-permute-start | bytes 4718600 | tf_op jit(solution)/shard_map/ppermute | solution.py:22
  220.0 39.1 %collective-permute-start.12 = (bf16[2,128,3072]{1,2,0:T(8,128)(2,1)}, bf16[2,128,3072]{1,2,0:T(8,128)(2,1)}, u32[]{:S(2)}, u32[]{:S(2)}) collective-permute-start(bf16[2,128,3072]{1,2,0:T(8,128)(2,1)} %collective-permute-done.10), channel_id=1, source_target_pairs={{0,2},{2,4},{4,6},{6,8},{8,10},{10,12},{12,14},{14,16},{16,18},{18... | collective-permute-start | bytes 4718600 | tf_op jit(solution)/shard_map/ppermute | solution.py:22
  249.3 11.7 %collective-permute-start.13 = (bf16[2,128,3072]{1,2,0:T(8,128)(2,1)}, bf16[2,128,3072]{1,2,0:T(8,128)(2,1)}, u32[]{:S(2)}, u32[]{:S(2)}) collective-permute-start(bf16[2,128,3072]{1,2,0:T(8,128)(2,1)} %collective-permute-done.11), channel_id=1, source_target_pairs={{2,0},{4,2},{6,4},{8,6},{10,8},{12,10},{14,12},{16,14},{18,16},{20... | collective-permute-start | bytes 4718600 | tf_op jit(solution)/shard_map/ppermute | solution.py:22
  268.9 12.8 %copy-start = (bf16[16,8,24,128]{3,2,1,0:T(8,128)(2,1)S(1)}, bf16[16,8,24,128]{3,2,1,0:T(8,128)(2,1)}, u32[]{:S(2)}) copy-start(bf16[16,8,24,128]{3,2,1,0:T(8,128)(2,1)} %copy.76) | copy-start | bytes 2359300
  281.7 17.2 %copy-start.1 = (bf16[1,128,3072]{2,1,0:T(8,128)(2,1)S(1)}, bf16[1,128,3072]{2,1,0:T(8,128)(2,1)}, u32[]{:S(2)}) copy-start(bf16[1,128,3072]{2,1,0:T(8,128)(2,1)} %param.73) | copy-start | bytes 2359300
where the time goes:
time: 370 us; the launch traced here: 369 us
  starting transfers between devices  156 us (42%)
  local copies, waits for them, and re-layouts  84.2 us (23%)
  blocking collectives  67.8 us (18%)
  matrix products  28.3 us (8%)
  between operations  24.8 us (7%)
  other arithmetic  7.51 us (2%)
    ppermute x14, starting transfers between devices, passed_along(): lax.ppermute(value, axis, [(source, source + steps) for source in range(f...  156 us
    psum x1, blocking collectives, on_device(): total = lax.psum(jnp.sum(terms), ('tok', 'grp'))  67.8 us
    unnamed x63, local copies, waits for them, and re-layouts  37.1 us
    slice x14, local copies, waits for them, and re-layouts, on_device(): key_list.append(piece[0])  26.8 us
    dot_general x1, matrix products, attend(): jnp.einsum('hqk,khd->qhd', probs, value_heads, preferred_element_type=jnp...  15.5 us
    concatenate x16, local copies, waits for them, and re-layouts, on_device(): key_all = jnp.concatenate(key_list, axis=0)  14.6 us
    sub x1, matrix products, attend(): expo = jnp.exp(scores - top)  12.8 us
  transfers between devices with their start and end apart: 14, of which 0 were waited for; matrix products, arithmetic and copies ran while one was open for 21% of the time, Pallas kernels for 0%

commit v1 on v0

v1 whole, which is shorter than its diff:
```python
import functools
import math

import jax
import jax.numpy as jnp
from jax import lax
from jax.experimental import pallas as pl
from jax.experimental.pallas import tpu as pltpu
from jax.sharding import PartitionSpec as P

HEADS = 24
HEAD = 128
BLK = 128
MAXB = 8
GROUPS = 4
LEVEL = MAXB // 2
REACH = MAXB - 1

masked_score = -1e30


def passed_along(value, axis, steps):
    count = lax.axis_size(axis)
    first, last = (max(0, -steps), min(count, count - steps))
    return lax.ppermute(value, axis, [(source, source + steps) for source in range(first, last)])


def advantages(reward_row, group_row):
    member = (group_row[:, None] == jnp.arange(GROUPS, dtype=jnp.int32)[None, :]).astype(
        jnp.float32
    )
    totals = jnp.sum(member * reward_row[:, None], axis=0)
    counts = jnp.sum(member, axis=0)
    means = totals / jnp.maximum(counts, 1.0)
    return reward_row - jnp.sum(member * means[None, :], axis=1)


def kernel_body(pieces, heads, start_ref, live_ref, weight_ref, bias_ref, *refs):
    parts = len(pieces)
    q_hbm, n_hbm = refs[0], refs[1]
    k_parts, v_parts = refs[2 : 2 + parts], refs[2 + parts : 2 + 2 * parts]
    out_ref, err_ref = refs[2 + 2 * parts], refs[3 + 2 * parts]
    q_buf, n_buf, k_buf, v_buf, sems = refs[4 + 2 * parts :]
    copies = [
        pltpu.make_async_copy(q_hbm, q_buf, sems.at[0]),
        pltpu.make_async_copy(n_hbm, n_buf, sems.at[1]),
    ]
    for index, (first, count) in enumerate(pieces):
        rows = pl.ds(first * BLK, count * BLK)
        copies.append(
            pltpu.make_async_copy(k_parts[index], k_buf.at[rows], sems.at[2 + 2 * index])
        )
        copies.append(
            pltpu.make_async_copy(v_parts[index], v_buf.at[rows], sems.at[3 + 2 * index])
        )
    for copy in copies:
        copy.start()
    for copy in copies:
        copy.wait()
    factor = math.log2(math.e) / math.sqrt(HEAD)
    err_ref[...] = jnp.zeros_like(err_ref)

    def one_block(block, carry):
        rows = pl.ds(pl.multiple_of(block * BLK, BLK), BLK)
        window = pl.ds(pl.multiple_of(start_ref[block] * BLK, BLK), MAXB * BLK)
        bias = bias_ref[pl.ds(block, 1), :]
        live = lax.broadcasted_iota(jnp.int32, (BLK, HEAD), 0) < live_ref[block]
        block_err = jnp.zeros((BLK, HEAD), jnp.float32)
        for head in range(heads):
            columns = slice(head * HEAD, (head + 1) * HEAD)
            scores = lax.dot_general(
                q_buf[rows, columns],
                k_buf[window, columns],
                (((1,), (1,)), ((), ())),
                preferred_element_type=jnp.float32,
            )
            scores = scores + bias
            top = jnp.max(scores, axis=-1, keepdims=True)
            expo = jnp.exp2((scores - top) * factor)
            probs = (expo * (1.0 / jnp.sum(expo, axis=-1, keepdims=True))).astype(jnp.bfloat16)
            mixed = lax.dot_general(
                probs,
                v_buf[window, columns],
                (((1,), (0,)), ((), ())),
                preferred_element_type=jnp.float32,
            )
            result = jnp.where(live, mixed, 0.0).astype(jnp.bfloat16)
            out_ref[rows, columns] = result
            diff = n_buf[rows, columns].astype(jnp.float32) - result.astype(jnp.float32)
            block_err = block_err + diff * diff
        block_err = jnp.where(live, block_err, 0.0)
        err_ref[...] += weight_ref[block] * jnp.sum(
            block_err.reshape(BLK // 8, 8, HEAD), axis=0
        )
        return carry

    lax.fori_loop(0, LEVEL, one_block, 0)


def attend(pieces, start, live, weight, bias, q, n, k_parts, v_parts):
    total = sum(count for _, count in pieces)
    width = q.shape[1]
    smem = pl.BlockSpec(memory_space=pltpu.SMEM)
    vmem = pl.BlockSpec(memory_space=pltpu.VMEM)
    hbm = pl.BlockSpec(memory_space=pl.ANY)
    parts = len(pieces)
    return pl.pallas_call(
        functools.partial(kernel_body, pieces, width // HEAD),
        out_shape=(
            jax.ShapeDtypeStruct(q.shape, jnp.bfloat16),
            jax.ShapeDtypeStruct((8, HEAD), jnp.float32),
        ),
        in_specs=[smem, smem, smem, vmem] + [hbm] * (2 + 2 * parts),
        out_specs=(vmem, vmem),
        scratch_shapes=[
            pltpu.VMEM(q.shape, jnp.bfloat16),
            pltpu.VMEM(q.shape, jnp.bfloat16),
            pltpu.VMEM((total * BLK, width), jnp.bfloat16),
            pltpu.VMEM((total * BLK, width), jnp.bfloat16),
            pltpu.SemaphoreType.DMA((2 + 2 * parts,)),
        ],
        compiler_params=pltpu.CompilerParams(vmem_limit_bytes=48 * 1024 * 1024),
        name="window_attention",
    )(start, live, weight, bias, q, n, *k_parts, *v_parts)


def on_device(queries, keys, values, next_latent, clip_blocks, valid_counts, group_ids, rewards):
    devices = lax.axis_size("tok")
    own_index = lax.axis_index("tok")
    width = queries.shape[2]
    levels = [list(range(first, first + LEVEL)) for first in range(0, devices, LEVEL)]

    def exchange(value):
        return lax.all_to_all(value, "tok", 1, 0, axis_index_groups=levels, tiled=True)

    valid_row = valid_counts[0]
    clip_row = clip_blocks[0]
    total_blocks = valid_row.shape[0]
    ends = jnp.cumsum(clip_row)
    starts = ends - clip_row
    positions = jnp.arange(total_blocks, dtype=jnp.int32)
    member = (starts[None, :] <= positions[:, None]) & (positions[:, None] < ends[None, :])
    tokens_of = jnp.sum(jnp.where(member, valid_row[:, None], 0), axis=0).astype(jnp.float32)
    clip_weight = advantages(rewards[0], group_ids[0]) / (2.0 * width * tokens_of)
    level_first = own_index // LEVEL * LEVEL
    own_ids = level_first + jnp.arange(LEVEL, dtype=jnp.int32)
    own_member = (starts[None, :] <= own_ids[:, None]) & (own_ids[:, None] < ends[None, :])
    own_start = jnp.sum(jnp.where(own_member, starts[None, :], 0), axis=1)
    own_count = jnp.sum(jnp.where(own_member, clip_row[None, :], 0), axis=1)
    own_weight = jnp.sum(jnp.where(own_member, clip_weight[None, :], 0.0), axis=1)
    own_live = jnp.take(valid_row, own_ids)
    near_ids = own_start[:, None] + jnp.arange(MAXB, dtype=jnp.int32)[None, :]
    near_live = jnp.take(valid_row, jnp.minimum(near_ids, total_blocks - 1))
    near_live = jnp.where(jnp.arange(MAXB)[None, :] < own_count[:, None], near_live, 0)
    slots = jnp.arange(BLK, dtype=jnp.int32)
    bias = jnp.where(slots[None, None, :] < near_live[:, :, None], 0.0, masked_score)
    bias = bias.astype(jnp.float32).reshape(LEVEL, MAXB * BLK)
    start = own_start - (level_first - REACH)

    def gathered(value):
        own = exchange(value[0])
        found = [(REACH, LEVEL, own)]
        upward = downward = own
        held = LEVEL
        for distance in range(1, -(-REACH // LEVEL) + 1):
            count = min(LEVEL, REACH - (distance - 1) * LEVEL)
            upward = passed_along(upward[(held - count) * BLK :], "tok", LEVEL)
            downward = passed_along(downward[: count * BLK], "tok", -LEVEL)
            held = count
            up_first = max(0, REACH - distance * LEVEL)
            found.append((up_first, count, upward))
            found.append((REACH + distance * LEVEL, count, downward))
        return found

    key_found = gathered(keys)
    value_found = gathered(values)
    q = exchange(queries[0])
    n = exchange(next_latent[0])
    pieces = tuple((first, count) for first, count, _ in key_found)
    out, err = attend(
        pieces,
        start,
        own_live,
        own_weight,
        bias,
        q,
        n,
        [piece for _, _, piece in key_found],
        [piece for _, _, piece in value_found],
    )
    velocity = lax.all_to_all(out, "tok", 0, 1, axis_index_groups=levels, tiled=True)
    share = jnp.sum(err)
    everyone = devices * lax.axis_size("grp")
    spread = jnp.full((everyone, HEAD), share)
    total = jnp.sum(lax.all_to_all(spread, ("tok", "grp"), 0, 0, tiled=True)[:, 0])
    return (velocity[None], total)


def solution(mesh):
    return jax.shard_map(
        on_device,
        mesh=mesh,
        in_specs=(
            P("grp", "tok", None),
            P("grp", "tok", None),
            P("grp", "tok", None),
            P("grp", "tok", None),
            P("grp", None),
            P("grp", None),
            P("grp", None),
            P("grp", None),
        ),
        out_specs=(P("grp", "tok", None), P()),
        check_vma=False,
    )
```

time: 370 us -> 145 us (0.39)
  starting transfers between devices: 156 us -> 44.9 us
  local copies, waits for them, and re-layouts: 84.2 us -> 27.4 us
  blocking collectives: 67.8 us -> 15 us
  waiting for transfers between devices: 0.04 us -> 36.5 us
  matrix products: 28.3 us -> 0 us
  between operations: 24.8 us -> 0.85 us
  Pallas kernels: 0 us -> 15.4 us
    ppermute x14 -> x8, starting transfers between devices: 156 us -> 26.5 us  [passed_along(): lax.ppermute(value, axis, [(source, source + steps) for source in range(f...]
    psum x1 -> x0, blocking collectives: 67.8 us -> none  [on_device(): total = lax.psum(jnp.sum(terms), ('tok', 'grp'))]
    unnamed x63 -> x21, local copies, waits for them, and re-layouts: 37.1 us -> 3.3 us
    all_to_all x0 -> x5, waiting for transfers between devices: none -> 30.3 us  [the longest x4 19.3 us: exchange(): lax.all_to_all(value, 'tok', 1, 0, axis_index_groups=levels, tiled=True)]
    slice x14 -> x4, local copies, waits for them, and re-layouts: 26.8 us -> 7.67 us  [the longest x2 3.84 us: gathered(): downward = passed_along(downward[:count * BLK], 'tok', -LEVEL)]
    all_to_all x0 -> x5, starting transfers between devices: none -> 18.3 us  [the longest x4 14.8 us: exchange(): lax.all_to_all(value, 'tok', 1, 0, axis_index_groups=levels, tiled=True)]
    concatenate x19 -> x0, local copies, waits for them, and re-layouts: 15.8 us -> none  [the longest x16 14.6 us: on_device(): key_all = jnp.concatenate(key_list, axis=0)]
    dot_general x1 -> x0, matrix products: 15.5 us -> none  [attend(): jnp.einsum('hqk,khd->qhd', probs, value_heads, preferred_element_type=jnp...]
  transfers between devices with their start and end apart: 14 -> 13, of which waited for: 0 -> 6; matrix products, arithmetic and copies ran while one was open for 21% -> 11% of each run, Pallas kernels for 0% -> 0%
where the time goes in v1:
time: 145 us; the launch traced here: 144 us
  starting transfers between devices  44.9 us (31%)
  waiting for transfers between devices  36.5 us (25%)
  local copies, waits for them, and re-layouts  27.4 us (19%)
  Pallas kernels  15.4 us (11%)
  blocking collectives  15 us (10%)
  other arithmetic  4.08 us (3%)
    ppermute x8, starting transfers between devices, passed_along(): lax.ppermute(value, axis, [(source, source + steps) for source in range(f...  26.5 us
    all_to_all x4, waiting for transfers between devices, exchange(): lax.all_to_all(value, 'tok', 1, 0, axis_index_groups=levels, tiled=True)  19.3 us
    pallas_call x1, Pallas kernels, attend(): pl.pallas_call(functools.partial(kernel_body, pieces, width // HEAD), out...  15.4 us
    all_to_all x1, blocking collectives, on_device(): lax.all_to_all(spread, ('tok', 'grp'), 0, 0, tiled=True)[:, 0]  15 us
    all_to_all x4, starting transfers between devices, exchange(): lax.all_to_all(value, 'tok', 1, 0, axis_index_groups=levels, tiled=True)  14.8 us
    all_to_all x8, local copies, waits for them, and re-layouts, exchange(): lax.all_to_all(value, 'tok', 1, 0, axis_index_groups=levels, tiled=True)  12.2 us
    all_to_all x1, waiting for transfers between devices, on_device(): lax.all_to_all(out, 'tok', 0, 1, axis_index_groups=levels, tiled=True)  11 us
    ppermute x8, waiting for transfers between devices, passed_along(): lax.ppermute(value, axis, [(source, source + steps) for source in range(f...  6.21 us
  transfers between devices with their start and end apart: 13, of which 6 were waited for; matrix products, arithmetic and copies ran while one was open for 11% of the time, Pallas kernels for 0%

profile of v1, /device:TPU:0, one launch (start us, length us, event | category | flops | bytes accessed | tf_op | source)
XLA Modules:
  0.0 144.1 jit_solution(15084157526921616276)
XLA Ops:
  0.6 2.0 %all_to_all.86 = bf16[128,4,768]{2,1,0:T(4,128)(2,1)S(1)} reshape(bf16[1,128,3072]{2,1,0:T(8,128)(2,1)} %param.10) | data formatting | bytes 1572864 | tf_op jit(solution)/shard_map/all_to_all | solution.py:134
  2.6 1.0 copy.28
  3.6 4.4 %all-to-all-start.3 = ((bf16[128,4,768]{2,0,1:T(8,128)(2,1)}), bf16[128,4,768]{2,0,1:T(8,128)(2,1)S(1)}, u32[]{:S(2)}, u32[]{:S(2)}) async-start(bf16[128,4,768]{2,0,1:T(8,128)(2,1)} %copy.28), calls=%async_computation.3 | async-start | bytes 1572864 | tf_op jit(solution)/shard_map/all_to_all | solution.py:134
  8.0 0.7 copy-done.7
  8.7 0.6 copy-done.8
  9.6 0.6 all_to_all.82
  10.1 1.0 copy.27
  11.1 0.2 select_reduce_fusion.3
  11.3 8.3 %all-to-all-done.3 = bf16[128,4,768]{2,0,1:T(8,128)(2,1)S(1)} async-done(((bf16[128,4,768]{2,0,1:T(8,128)(2,1)}), bf16[128,4,768]{2,0,1:T(8,128)(2,1)S(1)}, u32[]{:S(2)}, u32[]{:S(2)}) %all-to-all-start.3) | async-done | bytes 786464 | tf_op jit(solution)/shard_map/all_to_all | solution.py:134
  19.6 3.5 %all-to-all-start.2 = ((bf16[128,4,768]{2,0,1:T(8,128)(2,1)}), bf16[128,4,768]{2,0,1:T(8,128)(2,1)S(1)}, u32[]{:S(2)}, u32[]{:S(2)}) async-start(bf16[128,4,768]{2,0,1:T(8,128)(2,1)} %copy.27), calls=%async_computation.2 | async-start | bytes 1572864 | tf_op jit(solution)/shard_map/all_to_all | solution.py:134
  23.1 2.0 %all_to_all.74 = bf16[128,4,768]{2,1,0:T(4,128)(2,1)S(1)} reshape(bf16[1,128,3072]{2,1,0:T(8,128)(2,1)} %param.8) | data formatting | bytes 1572864 | tf_op jit(solution)/shard_map/all_to_all | solution.py:134
  25.1 1.0 copy.25
  26.1 0.7 copy-done.4
  26.7 0.2 select_reduce_fusion.2
  26.9 0.7 select_reduce_fusion.1
  27.6 1.3 collective-permute-start.5
  28.9 5.7 %collective-permute-start.4 = (bf16[512,768]{1,0:T(8,128)(2,1)S(1)}, bf16[512,768]{1,0:T(8,128)(2,1)}, u32[]{:S(2)}, u32[]{:S(2)}) collective-permute-start(bf16[512,768]{1,0:T(8,128)(2,1)S(1)} %bitcast.60), channel_id=1, source_target_pairs={{0,8},{2,10},{4,12},{6,14},{8,16},{10,18},{12,20},{14,22},{16,24},... | collective-permute-start | bytes 2359304 | tf_op jit(solution)/shard_map/ppermute | solution.py:25
  34.7 3.5 %all-to-all-start = ((bf16[128,4,768]{2,0,1:T(8,128)(2,1)}), bf16[128,4,768]{2,0,1:T(8,128)(2,1)S(1)}, u32[]{:S(2)}, u32[]{:S(2)}) async-start(bf16[128,4,768]{2,0,1:T(8,128)(2,1)} %copy.25), calls=%async_computation | async-start | bytes 1572864 | tf_op jit(solution)/shard_map/all_to_all | solution.py:134
  38.2 1.3 collective-permute-start.1
  39.5 5.7 %collective-permute-start = (bf16[512,768]{1,0:T(8,128)(2,1)S(1)}, bf16[512,768]{1,0:T(8,128)(2,1)}, u32[]{:S(2)}, u32[]{:S(2)}) collective-permute-start(bf16[512,768]{1,0:T(8,128)(2,1)S(1)} %bitcast.52), channel_id=1, source_target_pairs={{0,8},{2,10},{4,12},{6,14},{8,16},{10,18},{12,20},{14,22},{16,24},... | collective-permute-start | bytes 2359304 | tf_op jit(solution)/shard_map/ppermute | solution.py:25
  45.5 0.7 gather_fusion.1
  46.3 0.6 gather_fusion
  47.0 2.7 %all_to_all.78 = bf16[128,4,768]{2,1,0:T(4,128)(2,1)} reshape(bf16[1,128,3072]{2,1,0:T(8,128)(2,1)} %param.11) | data formatting | bytes 1572864 | tf_op jit(solution)/shard_map/all_to_all | solution.py:134
  49.6 2.1 %copy.26 = bf16[128,4,768]{2,0,1:T(8,128)(2,1)} copy(bf16[128,4,768]{2,1,0:T(4,128)(2,1)} %all_to_all.78) | data formatting | bytes 1572864 | tf_op jit(solution)/shard_map/all_to_all | solution.py:134
  51.8 1.9 %slice.27 = bf16[384,768]{1,0:T(8,128)(2,1)} slice(bf16[512,768]{1,0:T(8,128)(2,1)} %collective-permute-done.5.refs_9_), slice={[0:384], [0:768]} | slice | bytes 1179648 | tf_op jit(solution)/shard_map/slice | solution.py:168
  53.7 1.3 collective-permute-start.7
  55.0 1.9 %slice.26 = bf16[384,768]{1,0:T(8,128)(2,1)} slice(bf16[512,768]{1,0:T(8,128)(2,1)} %collective-permute-done.4.refs_8_), slice={[128:512], [0:768]} | slice | bytes 1179648 | tf_op jit(solution)/shard_map/slice | solution.py:167
  56.9 4.6 %collective-permute-start.6 = (bf16[384,768]{1,0:T(8,128)(2,1)}, bf16[384,768]{1,0:T(8,128)(2,1)S(1)}, u32[]{:S(2)}, u32[]{:S(2)}) collective-permute-start(bf16[384,768]{1,0:T(8,128)(2,1)} %slice.26), channel_id=1, source_target_pairs={{0,8},{2,10},{4,12},{6,14},{8,16},{10,18},{12,20},{14,22},{16,24},... | collective-permute-start | bytes 1769480 | tf_op jit(solution)/shard_map/ppermute | solution.py:25
  61.5 5.6 %collective-permute-done.1.refs_4_ = bf16[512,768]{1,0:T(8,128)(2,1)} collective-permute-done((bf16[512,768]{1,0:T(8,128)(2,1)S(1)}, bf16[512,768]{1,0:T(8,128)(2,1)}, u32[]{:S(2)}, u32[]{:S(2)}) %collective-permute-start.1) | collective-permute-done | bytes 786464 | tf_op jit(solution)/shard_map/ppermute | solution.py:25
  67.1 1.9 %slice.25 = bf16[384,768]{1,0:T(8,128)(2,1)} slice(bf16[512,768]{1,0:T(8,128)(2,1)} %collective-permute-done.1.refs_4_), slice={[0:384], [0:768]} | slice | bytes 1179648 | tf_op jit(solution)/shard_map/slice | solution.py:168
  69.0 1.3 collective-permute-start.3
  70.3 1.9 %slice.24 = bf16[384,768]{1,0:T(8,128)(2,1)} slice(bf16[512,768]{1,0:T(8,128)(2,1)} %collective-permute-done.refs_3_), slice={[128:512], [0:768]} | slice | bytes 1179648 | tf_op jit(solution)/shard_map/slice | solution.py:167
  72.3 5.4 %collective-permute-start.2 = (bf16[384,768]{1,0:T(8,128)(2,1)}, bf16[384,768]{1,0:T(8,128)(2,1)}, u32[]{:S(2)}, u32[]{:S(2)}) collective-permute-start(bf16[384,768]{1,0:T(8,128)(2,1)} %slice.24), channel_id=1, source_target_pairs={{0,8},{2,10},{4,12},{6,14},{8,16},{10,18},{12,20},{14,22},{16,24},... | collective-permute-start | bytes 1769480 | tf_op jit(solution)/shard_map/ppermute | solution.py:25
  77.7 3.5 %all-to-all-start.1 = ((bf16[128,4,768]{2,0,1:T(8,128)(2,1)}), bf16[128,4,768]{2,0,1:T(8,128)(2,1)S(1)}, u32[]{:S(2)}, u32[]{:S(2)}) async-start(bf16[128,4,768]{2,0,1:T(8,128)(2,1)} %copy.26), calls=%async_computation.1 | async-start | bytes 1572864 | tf_op jit(solution)/shard_map/all_to_all | solution.py:134
  81.2 0.5 and_select_fusion
  81.8 11.0 %all-to-all-done.1 = bf16[128,4,768]{2,0,1:T(8,128)(2,1)S(1)} async-done(((bf16[128,4,768]{2,0,1:T(8,128)(2,1)}), bf16[128,4,768]{2,0,1:T(8,128)(2,1)S(1)}, u32[]{:S(2)}, u32[]{:S(2)}) %all-to-all-start.1) | async-done | bytes 786464 | tf_op jit(solution)/shard_map/all_to_all | solution.py:134
  92.8 0.6 collective-permute-done.2.refs_5_
  93.4 0.6 copy-done.1
  94.0 15.4 %window_attention.1 = (bf16[512,768]{1,0:T(8,128)(2,1)}, f32[8,128]{1,0:T(8,128)S(1)}) custom-call(s32[4]{0:T(128)S(1)} %copy-done.3, s32[4]{0:T(128)S(1)} %copy-done.2, f32[4]{0:T(128)S(1)} %copy-done.1, f32[4,1024]{1,0:T(4,128)S(1)} %fusion.bias_ref, bf16[512,768]{1,0:T(8,128)(2,1)S(1)} %bitcast.54, bf16[512,768]{1,0:T(8,128)(2,1)S(1)} %bitcast.55, ...), custom_call_target="tpu_custom_call" | custom-call | tf_op jit(solution)/shard_map/window_attention/pallas_call | solution.py:107
  109.5 0.6 copy-done
  110.1 1.3 reduce_sum.91
  111.3 0.7 broadcast_in_dim.95
  112.0 15.0 %all_to_all.101 = f32[32,1,128]{2,1,0:T(1,128)S(1)} all-to-all(f32[32,1,128]{2,1,0:T(1,128)S(1)} %broadcast_in_dim.95), channel_id=1, replica_groups=mesh['tok'=16,'grp'=2] {'tok','grp'}, dimensions={0} | all-to-all | bytes 32768 | tf_op jit(solution)/shard_map/all_to_all | solution.py:195
  127.0 3.5 %all-to-all-start.4 = ((bf16[4,128,768]{2,1,0:T(8,128)(2,1)}), bf16[4,128,768]{2,1,0:T(8,128)(2,1)S(1)}, u32[]{:S(2)}, u32[]{:S(2)}) async-start(bf16[4,128,768]{2,1,0:T(8,128)(2,1)} %bitcast.23), calls=%async_computation.4 | async-start | bytes 1572864 | tf_op jit(solution)/shard_map/all_to_all | solution.py:191
  130.5 0.6 slice_reduce_fusion
  131.1 11.0 %all-to-all-done.4 = bf16[4,128,768]{2,1,0:T(8,128)(2,1)S(1)} async-done(((bf16[4,128,768]{2,1,0:T(8,128)(2,1)}), bf16[4,128,768]{2,1,0:T(8,128)(2,1)S(1)}, u32[]{:S(2)}, u32[]{:S(2)}) %all-to-all-start.4) | async-done | bytes 786464 | tf_op jit(solution)/shard_map/all_to_all | solution.py:191
  142.1 0.6 copy.29
  142.7 1.5 %broadcast_in_dim.94 = bf16[1,128,3072]{2,1,0:T(8,128)(2,1)} reshape(bf16[128,4,768]{2,1,0:T(4,128)(2,1)S(1)} %copy.29) | data formatting | bytes 1572864 | tf_op jit(solution)/shard_map/broadcast_in_dim | solution.py:196
  (40 shorter events, 1.0 us)
Async XLA Ops:
  3.6 6.0 %copy-start.6 = (bf16[1,128,3072]{2,1,0:T(8,128)(2,1)S(1)}, bf16[1,128,3072]{2,1,0:T(8,128)(2,1)}, u32[]{:S(2)}) copy-start(bf16[1,128,3072]{2,1,0:T(8,128)(2,1)} %param.9) | copy-start | bytes 2359300
  3.6 16.0 %all-to-all-start.3 = ((bf16[128,4,768]{2,0,1:T(8,128)(2,1)}), bf16[128,4,768]{2,0,1:T(8,128)(2,1)S(1)}, u32[]{:S(2)}, u32[]{:S(2)}) async-start(bf16[128,4,768]{2,0,1:T(8,128)(2,1)} %copy.28), calls=%async_computation.3 | async-start | bytes 1572864 | tf_op jit(solution)/shard_map/all_to_all | solution.py:134
  8.0 0.7 copy-start.7
  8.0 0.7 copy-start.9
  8.7 0.7 copy-start.8
  19.6 9.3 %copy-start.5 = (bf16[128,4,768]{2,0,1:T(8,128)(2,1)}, bf16[128,4,768]{2,0,1:T(8,128)(2,1)S(1)}, u32[]{:S(2)}) copy-start(bf16[128,4,768]{2,0,1:T(8,128)(2,1)S(1)} %all-to-all-done.3) | copy-start | bytes 2359300
  19.6 15.1 %all-to-all-start.2 = ((bf16[128,4,768]{2,0,1:T(8,128)(2,1)}), bf16[128,4,768]{2,0,1:T(8,128)(2,1)S(1)}, u32[]{:S(2)}, u32[]{:S(2)}) async-start(bf16[128,4,768]{2,0,1:T(8,128)(2,1)} %copy.27), calls=%async_computation.2 | async-start | bytes 1572864 | tf_op jit(solution)/shard_map/all_to_all | solution.py:134
  26.0 0.7 copy-start.4
  27.6 24.2 %collective-permute-start.5 = (bf16[512,768]{1,0:T(8,128)(2,1)S(1)}, bf16[512,768]{1,0:T(8,128)(2,1)}, u32[]{:S(2)}, u32[]{:S(2)}) collective-permute-start(bf16[512,768]{1,0:T(8,128)(2,1)S(1)} %bitcast.59), channel_id=1, source_target_pairs={{8,0},{10,2},{12,4},{14,6},{16,8},{18,10},{20,12},{22,14},{24,16},... | collective-permute-start | bytes 2359304 | tf_op jit(solution)/shard_map/ppermute | solution.py:25
  28.9 26.1 %collective-permute-start.4 = (bf16[512,768]{1,0:T(8,128)(2,1)S(1)}, bf16[512,768]{1,0:T(8,128)(2,1)}, u32[]{:S(2)}, u32[]{:S(2)}) collective-permute-start(bf16[512,768]{1,0:T(8,128)(2,1)S(1)} %bitcast.60), channel_id=1, source_target_pairs={{0,8},{2,10},{4,12},{6,14},{8,16},{10,18},{12,20},{14,22},{16,24},... | collective-permute-start | bytes 2359304 | tf_op jit(solution)/shard_map/ppermute | solution.py:25
  34.7 43.0 %all-to-all-start = ((bf16[128,4,768]{2,0,1:T(8,128)(2,1)}), bf16[128,4,768]{2,0,1:T(8,128)(2,1)S(1)}, u32[]{:S(2)}, u32[]{:S(2)}) async-start(bf16[128,4,768]{2,0,1:T(8,128)(2,1)} %copy.25), calls=%async_computation | async-start | bytes 1572864 | tf_op jit(solution)/shard_map/all_to_all | solution.py:134
  38.2 28.9 %collective-permute-start.1 = (bf16[512,768]{1,0:T(8,128)(2,1)S(1)}, bf16[512,768]{1,0:T(8,128)(2,1)}, u32[]{:S(2)}, u32[]{:S(2)}) collective-permute-start(bf16[512,768]{1,0:T(8,128)(2,1)S(1)} %bitcast.51), channel_id=1, source_target_pairs={{8,0},{10,2},{12,4},{14,6},{16,8},{18,10},{20,12},{22,14},{24,16},... | collective-permute-start | bytes 2359304 | tf_op jit(solution)/shard_map/ppermute | solution.py:25
  39.5 30.9 %collective-permute-start = (bf16[512,768]{1,0:T(8,128)(2,1)S(1)}, bf16[512,768]{1,0:T(8,128)(2,1)}, u32[]{:S(2)}, u32[]{:S(2)}) collective-permute-start(bf16[512,768]{1,0:T(8,128)(2,1)S(1)} %bitcast.52), channel_id=1, source_target_pairs={{0,8},{2,10},{4,12},{6,14},{8,16},{10,18},{12,20},{14,22},{16,24},... | collective-permute-start | bytes 2359304 | tf_op jit(solution)/shard_map/ppermute | solution.py:25
  53.7 39.0 %collective-permute-start.7 = (bf16[384,768]{1,0:T(8,128)(2,1)}, bf16[384,768]{1,0:T(8,128)(2,1)S(1)}, u32[]{:S(2)}, u32[]{:S(2)}) collective-permute-start(bf16[384,768]{1,0:T(8,128)(2,1)} %slice.27), channel_id=1, source_target_pairs={{8,0},{10,2},{12,4},{14,6},{16,8},{18,10},{20,12},{22,14},{24,16},... | collective-permute-start | bytes 1769480 | tf_op jit(solution)/shard_map/ppermute | solution.py:25
  56.9 35.8 %collective-permute-start.6 = (bf16[384,768]{1,0:T(8,128)(2,1)}, bf16[384,768]{1,0:T(8,128)(2,1)S(1)}, u32[]{:S(2)}, u32[]{:S(2)}) collective-permute-start(bf16[384,768]{1,0:T(8,128)(2,1)} %slice.26), channel_id=1, source_target_pairs={{0,8},{2,10},{4,12},{6,14},{8,16},{10,18},{12,20},{14,22},{16,24},... | collective-permute-start | bytes 1769480 | tf_op jit(solution)/shard_map/ppermute | solution.py:25
  69.0 23.7 %collective-permute-start.3 = (bf16[384,768]{1,0:T(8,128)(2,1)}, bf16[384,768]{1,0:T(8,128)(2,1)}, u32[]{:S(2)}, u32[]{:S(2)}) collective-permute-start(bf16[384,768]{1,0:T(8,128)(2,1)} %slice.25), channel_id=1, source_target_pairs={{8,0},{10,2},{12,4},{14,6},{16,8},{18,10},{20,12},{22,14},{24,16},... | collective-permute-start | bytes 1769480 | tf_op jit(solution)/shard_map/ppermute | solution.py:25
  72.3 21.1 %collective-permute-start.2 = (bf16[384,768]{1,0:T(8,128)(2,1)}, bf16[384,768]{1,0:T(8,128)(2,1)}, u32[]{:S(2)}, u32[]{:S(2)}) collective-permute-start(bf16[384,768]{1,0:T(8,128)(2,1)} %slice.24), channel_id=1, source_target_pairs={{0,8},{2,10},{4,12},{6,14},{8,16},{10,18},{12,20},{14,22},{16,24},... | collective-permute-start | bytes 1769480 | tf_op jit(solution)/shard_map/ppermute | solution.py:25
  77.7 15.1 %all-to-all-start.1 = ((bf16[128,4,768]{2,0,1:T(8,128)(2,1)}), bf16[128,4,768]{2,0,1:T(8,128)(2,1)S(1)}, u32[]{:S(2)}, u32[]{:S(2)}) async-start(bf16[128,4,768]{2,0,1:T(8,128)(2,1)} %copy.26), calls=%async_computation.1 | async-start | bytes 1572864 | tf_op jit(solution)/shard_map/all_to_all | solution.py:134
  93.4 0.7 copy-start.1
  93.4 0.7 copy-start.2
  93.4 0.7 copy-start.3
  109.5 0.6 copy-start
  127.0 15.1 %all-to-all-start.4 = ((bf16[4,128,768]{2,1,0:T(8,128)(2,1)}), bf16[4,128,768]{2,1,0:T(8,128)(2,1)S(1)}, u32[]{:S(2)}, u32[]{:S(2)}) async-start(bf16[4,128,768]{2,1,0:T(8,128)(2,1)} %bitcast.23), calls=%async_computation.4 | async-start | bytes 1572864 | tf_op jit(solution)/shard_map/all_to_all | solution.py:191

commit v2 on v1

v2 whole, which is shorter than its diff:
```python
import functools
import math

import jax
import jax.numpy as jnp
from jax import lax
from jax.experimental import pallas as pl
from jax.experimental.pallas import tpu as pltpu
from jax.sharding import PartitionSpec as P


HEAD = 128
BLK = 128
MAXB = 8
GROUPS = 4
LEVEL = MAXB // 2
REACH = MAXB - 1
CHUNKS = (1, 1)

masked_score = -1e30


def passed_along(value, axis, steps):
    count = lax.axis_size(axis)
    first, last = (max(0, -steps), min(count, count - steps))
    return lax.ppermute(value, axis, [(source, source + steps) for source in range(first, last)])


def advantages(reward_row, group_row):
    member = (group_row[:, None] == jnp.arange(GROUPS, dtype=jnp.int32)[None, :]).astype(
        jnp.float32
    )
    totals = jnp.sum(member * reward_row[:, None], axis=0)
    counts = jnp.sum(member, axis=0)
    means = totals / jnp.maximum(counts, 1.0)
    return reward_row - jnp.sum(member * means[None, :], axis=1)


def moved(copies):
    for copy in copies:
        copy.start()
    for copy in copies:
        copy.wait()


def pack_body(spans, first_ref, second_ref, *refs):
    outs, sems = refs[:-1], refs[-1]
    share = first_ref.shape[2] // LEVEL
    copies = []
    for out_ref, (low, high) in zip(outs, spans):
        for part in range(LEVEL):
            for side, ref in enumerate((first_ref, second_ref)):
                copies.append(
                    pltpu.make_async_copy(
                        ref.at[0, :, pl.ds(part * share + low, high - low)],
                        out_ref.at[part, :, pl.ds(side * (high - low), high - low)],
                        sems.at[len(copies)],
                    )
                )
    moved(copies)


def packed(first, second, spans):
    rows = first.shape[1]
    hbm = pl.BlockSpec(memory_space=pl.ANY)
    return pl.pallas_call(
        functools.partial(pack_body, spans),
        out_shape=[
            jax.ShapeDtypeStruct((LEVEL, rows, 2 * (high - low)), first.dtype)
            for low, high in spans
        ],
        in_specs=[hbm, hbm],
        out_specs=[hbm] * len(spans),
        scratch_shapes=[pltpu.SemaphoreType.DMA((2 * LEVEL * len(spans),))],
    )(first, second)


def unpack_body(spans, place_ref, *refs):
    parts, out_ref, sems = refs[:-2], refs[-2], refs[-1]
    share = out_ref.shape[2] // LEVEL
    own = place_ref[1]
    copies = []
    for index, (low, high) in enumerate(spans):
        for step in range(LEVEL):
            first = pl.multiple_of(jnp.bitwise_xor(own, step) * share + low, HEAD)
            copies.append(
                pltpu.make_async_copy(
                    parts[index * LEVEL + step],
                    out_ref.at[0, :, pl.ds(first, high - low)],
                    sems.at[len(copies)],
                )
            )
    moved(copies)


def unpacked(place, outs, spans, width):
    hbm = pl.BlockSpec(memory_space=pl.ANY)
    return pl.pallas_call(
        functools.partial(unpack_body, spans),
        out_shape=jax.ShapeDtypeStruct((1, outs[0].shape[0], width), outs[0].dtype),
        in_specs=[pl.BlockSpec(memory_space=pltpu.SMEM)] + [hbm] * len(outs),
        out_specs=hbm,
        scratch_shapes=[pltpu.SemaphoreType.DMA((len(outs),))],
        name="unpack",
    )(place, *outs)


def kernel_body(
    pieces, heads, first_head, place_ref, clip_ref, valid_ref, weight_ref, *refs
):
    parts = len(pieces)
    width = heads * HEAD
    qn_hbm = refs[0]
    kv_parts = refs[1 : 1 + parts]
    out_refs = refs[1 + parts : 1 + parts + LEVEL]
    err_ref, q_buf, n_buf, kv_buf, sems = refs[1 + parts + LEVEL :]
    half = qn_hbm.shape[1] // 2
    copies = [
        pltpu.make_async_copy(
            qn_hbm.at[:, pl.ds(first_head * HEAD, width)], q_buf, sems.at[0]
        ),
        pltpu.make_async_copy(
            qn_hbm.at[:, pl.ds(half + first_head * HEAD, width)], n_buf, sems.at[1]
        ),
    ]
    for index, (first, count) in enumerate(pieces):
        rows = pl.ds(first * BLK, count * BLK)
        copies.append(
            pltpu.make_async_copy(kv_parts[index], kv_buf.at[rows], sems.at[2 + index])
        )
    moved(copies)
    factor = math.log2(math.e) / math.sqrt(HEAD)
    err_ref[...] = jnp.zeros_like(err_ref)
    level_first, own = place_ref[0], place_ref[1]
    last_block = valid_ref.shape[1] - 1
    slots = lax.broadcasted_iota(jnp.int32, (1, BLK), 1)

    for step in range(LEVEL):
        block = jnp.bitwise_xor(own, step)
        own_id = level_first + block
        clip_start = clip_count = clip_first = jnp.int32(0)
        for clip in range(clip_ref.shape[1]):
            blocks = clip_ref[0, clip]
            mine = (own_id >= clip_first) & (own_id < clip_first + blocks)
            clip_start = jnp.where(mine, clip_first, clip_start)
            clip_count = jnp.where(mine, blocks, clip_count)
            clip_first = clip_first + blocks
        bias = []
        for near in range(MAXB):
            live = valid_ref[0, jnp.minimum(clip_start + near, last_block)]
            live = jnp.where(near < clip_count, live, 0)
            bias.append(jnp.where(slots < live, 0.0, masked_score).astype(jnp.float32))
        bias = jnp.concatenate(bias, axis=1)
        rows = pl.ds(pl.multiple_of(block * BLK, BLK), BLK)
        window_first = clip_start - (level_first - REACH)
        window = pl.ds(pl.multiple_of(window_first * BLK, BLK), MAXB * BLK)
        own_live = lax.broadcasted_iota(jnp.int32, (BLK, HEAD), 0) < valid_ref[0, own_id]
        block_err = jnp.zeros((BLK, HEAD), jnp.float32)
        for head in range(heads):
            columns = slice(head * HEAD, (head + 1) * HEAD)
            scores = lax.dot_general(
                q_buf[rows, columns],
                kv_buf[window, columns],
                (((1,), (1,)), ((), ())),
                preferred_element_type=jnp.float32,
            )
            scores = scores + bias
            top = jnp.max(scores, axis=-1, keepdims=True)
            expo = jnp.exp2((scores - top) * factor)
            probs = (expo * (1.0 / jnp.sum(expo, axis=-1, keepdims=True))).astype(jnp.bfloat16)
            mixed = lax.dot_general(
                probs,
                kv_buf[window, width + head * HEAD : width + (head + 1) * HEAD],
                (((1,), (0,)), ((), ())),
                preferred_element_type=jnp.float32,
            )
            result = jnp.where(own_live, mixed, 0.0).astype(jnp.bfloat16)
            out_refs[step][:, columns] = result
            diff = n_buf[rows, columns].astype(jnp.float32) - result.astype(jnp.float32)
            block_err = block_err + diff * diff
        block_err = jnp.where(own_live, block_err, 0.0)
        err_ref[...] += weight_ref[block] * jnp.sum(
            block_err.reshape(BLK // 8, 8, HEAD), axis=0
        )


def attend(pieces, first_head, tables, qn, kv_parts):
    total = sum(count for _, count in pieces)
    width = kv_parts[0].shape[1] // 2
    block_rows = qn.shape[0]
    smem = pl.BlockSpec(memory_space=pltpu.SMEM)
    vmem = pl.BlockSpec(memory_space=pltpu.VMEM)
    hbm = pl.BlockSpec(memory_space=pl.ANY)
    parts = len(pieces)
    units = LEVEL * (width // HEAD)
    return pl.pallas_call(
        functools.partial(kernel_body, pieces, width // HEAD, first_head),
        out_shape=[jax.ShapeDtypeStruct((BLK, width), jnp.bfloat16)] * LEVEL
        + [jax.ShapeDtypeStruct((8, HEAD), jnp.float32)],
        in_specs=[smem] * len(tables) + [hbm] * (1 + parts),
        out_specs=[vmem] * (LEVEL + 1),
        scratch_shapes=[
            pltpu.VMEM((block_rows, width), jnp.bfloat16),
            pltpu.VMEM((block_rows, width), jnp.bfloat16),
            pltpu.VMEM((total * BLK, 2 * width), jnp.bfloat16),
            pltpu.SemaphoreType.DMA((2 + parts,)),
        ],
        cost_estimate=pl.CostEstimate(
            flops=units * 4 * BLK * MAXB * BLK * HEAD,
            transcendentals=units * BLK * MAXB * BLK,
            bytes_accessed=4 * (total * BLK + 2 * block_rows) * width,
        ),
        compiler_params=pltpu.CompilerParams(vmem_limit_bytes=32 * 1024 * 1024),
    )(*tables, qn, *kv_parts)


def step(queries, keys, values, next_latent, clip_blocks, valid_counts, group_ids, rewards):
    devices = lax.axis_size("tok")
    own_index = lax.axis_index("tok")
    _, width = queries.shape[1:]
    share = width // LEVEL
    levels = [list(range(first, first + LEVEL)) for first in range(0, devices, LEVEL)]
    heads = share // HEAD
    cuts = [0]
    for part in CHUNKS:
        cuts.append(cuts[-1] + heads * part // sum(CHUNKS))
    spans = [(low * HEAD, high * HEAD) for low, high in zip(cuts[:-1], cuts[1:])]

    def exchange(value):
        return lax.all_to_all(value, "tok", 0, 0, axis_index_groups=levels, tiled=True)

    def exchanged(value):
        found = exchange(value)
        return found.reshape(found.shape[0] * found.shape[1], found.shape[2])

    def gathered(own):
        found = [(REACH, LEVEL, own)]
        upward = downward = own
        held = LEVEL
        for distance in range(1, -(-REACH // LEVEL) + 1):
            count = min(LEVEL, REACH - (distance - 1) * LEVEL)
            upward = passed_along(upward[(held - count) * BLK :], "tok", LEVEL)
            downward = passed_along(downward[: count * BLK], "tok", -LEVEL)
            held = count
            found.append((max(0, REACH - distance * LEVEL), count, upward))
            found.append((REACH + distance * LEVEL, count, downward))
        return found

    own_kv = []
    for span in spans:
        parts = packed(keys, values, [span])
        own_kv += [exchanged(part) for part in parts]
    (part,) = packed(queries, next_latent, [(0, share)])
    qn = exchanged(part)

    valid_row = valid_counts[0]
    clip_row = clip_blocks[0]
    ends = jnp.cumsum(clip_row)
    starts = ends - clip_row
    positions = jnp.arange(valid_row.shape[0], dtype=jnp.int32)
    member = (starts[None, :] <= positions[:, None]) & (positions[:, None] < ends[None, :])
    tokens_of = jnp.sum(jnp.where(member, valid_row[:, None], 0), axis=0).astype(jnp.float32)
    clip_weight = advantages(rewards[0], group_ids[0]) / (2.0 * width * tokens_of)
    level_first = own_index // LEVEL * LEVEL
    own_ids = level_first + jnp.arange(LEVEL, dtype=jnp.int32)
    own_member = (starts[None, :] <= own_ids[:, None]) & (own_ids[:, None] < ends[None, :])
    own_weight = jnp.sum(jnp.where(own_member, clip_weight[None, :], 0.0), axis=1)
    place = jnp.stack([level_first, own_index - level_first])
    tables = (place, clip_blocks, valid_counts, own_weight)

    outs, errs = [], []
    for (low, high), own in zip(spans, own_kv):
        found = gathered(own)
        pieces = tuple((first, count) for first, count, _ in found)
        *out, err = attend(pieces, low // HEAD, tables, qn, [piece for _, _, piece in found])
        outs.append(out[0])
        for step in range(1, LEVEL):
            partners = [(source, source ^ step) for source in range(devices)]
            outs.append(lax.ppermute(out[step], "tok", partners))
        errs.append(err)
    velocity = unpacked(place, outs, spans, width)
    device_share = jnp.sum(sum(errs))
    everyone = devices * lax.axis_size("grp")
    spread = jnp.full((everyone, HEAD), device_share)
    total = jnp.sum(lax.all_to_all(spread, ("tok", "grp"), 0, 0, tiled=True)[:, 0])
    return (velocity, total)


def solution(mesh):
    return jax.shard_map(
        step,
        mesh=mesh,
        in_specs=(
            P("grp", "tok", None),
            P("grp", "tok", None),
            P("grp", "tok", None),
            P("grp", "tok", None),
            P("grp", None),
            P("grp", None),
            P("grp", None),
            P("grp", None),
        ),
        out_specs=(P("grp", "tok", None), P()),
        check_vma=False,
    )
```

time: 145 us -> 223 us (1.54)
  Pallas kernels: 15.4 us -> 140 us
  local copies, waits for them, and re-layouts: 27.4 us -> 11 us
  blocking collectives: 15 us -> 0 us
  waiting for transfers between devices: 36.5 us -> 21.6 us
    pallas_call x1 -> x6, Pallas kernels: 15.4 us -> 140 us  [the longest x3 98.8 us: packed(): pl.pallas_call(functools.partial(pack_body, spans), out_shape=[jax.ShapeD...]
    all_to_all x5 -> x4, waiting for transfers between devices: 30.3 us -> 3.18 us  [the longest x1 3.17 us: step(): lax.all_to_all(spread, ('tok', 'grp'), 0, 0, tiled=True)[:, 0]]
    all_to_all x1 -> x0, blocking collectives: 15 us -> none  [on_device(): lax.all_to_all(spread, ('tok', 'grp'), 0, 0, tiled=True)[:, 0]]
    all_to_all x9 -> x0, local copies, waits for them, and re-layouts: 12.8 us -> none  [the longest x8 12.2 us: exchange(): lax.all_to_all(value, 'tok', 1, 0, axis_index_groups=levels, tiled=True)]
    ppermute x8, waiting for transfers between devices: 6.21 us -> 15 us  [passed_along(): lax.ppermute(value, axis, [(source, source + steps) for source in range(f...]
    ppermute x0 -> x6, starting transfers between devices: none -> 3.98 us  [step(): outs.append(lax.ppermute(out[step], 'tok', partners))]
    ppermute x0 -> x6, waiting for transfers between devices: none -> 3.42 us  [step(): outs.append(lax.ppermute(out[step], 'tok', partners))]
    all_to_all x5 -> x4, starting transfers between devices: 18.3 us -> 15.4 us  [the longest x3 11.3 us: exchange(): lax.all_to_all(value, 'tok', 0, 0, axis_index_groups=levels, tiled=True)]
  transfers between devices with their start and end apart: 13 -> 18, of which waited for: 6 -> 7; matrix products, arithmetic and copies ran while one was open for 11% -> 5% of each run, Pallas kernels for 0% -> 40%
where the time goes in v2:
time: 223 us; the launch traced here: 222 us
  Pallas kernels  140 us (63%)
  starting transfers between devices  45.9 us (21%)
  waiting for transfers between devices  21.6 us (10%)
  local copies, waits for them, and re-layouts  11 us (5%)
    pallas_call x3, Pallas kernels, packed(): pl.pallas_call(functools.partial(pack_body, spans), out_shape=[jax.ShapeD...  98.8 us
    ppermute x8, starting transfers between devices, passed_along(): lax.ppermute(value, axis, [(source, source + steps) for source in range(f...  26.5 us
    pallas_call x1, Pallas kernels, unpacked(): pl.pallas_call(functools.partial(unpack_body, spans), out_shape=jax.Shape...  25.7 us
    pallas_call x2, Pallas kernels, attend(): pl.pallas_call(functools.partial(kernel_body, pieces, width // HEAD, firs...  15.9 us
    ppermute x8, waiting for transfers between devices, passed_along(): lax.ppermute(value, axis, [(source, source + steps) for source in range(f...  15 us
    all_to_all x3, starting transfers between devices, exchange(): lax.all_to_all(value, 'tok', 0, 0, axis_index_groups=levels, tiled=True)  11.3 us
  transfers between devices with their start and end apart: 18, of which 7 were waited for; matrix products, arithmetic and copies ran while one was open for 5% of the time, Pallas kernels for 40%

profile of v2, /device:TPU:0, one launch (start us, length us, event | category | flops | bytes accessed | tf_op | source)
XLA Modules:
  0.0 221.9 jit_solution(4992516016907080762)
XLA Ops:
  0.6 25.0 %shard_map.96 = bf16[4,128,768]{2,1,0:T(8,128)(2,1)} custom-call(bf16[1,128,3072]{2,1,0:T(8,128)(2,1)} %first_ref.5, bf16[1,128,3072]{2,1,0:T(8,128)(2,1)} %second_ref.5), custom_call_target="tpu_custom_call" | custom-call | tf_op jit(solution)/shard_map/pallas_call | solution.py:66
  25.6 4.2 %all-to-all-start.1 = ((bf16[4,128,768]{2,1,0:T(8,128)(2,1)}), bf16[4,128,768]{2,1,0:T(8,128)(2,1)S(1)}, u32[]{:S(2)}, u32[]{:S(2)}) async-start(bf16[4,128,768]{2,1,0:T(8,128)(2,1)} %shard_map.96), calls=%async_computation.1 | async-start | bytes 1572864 | tf_op jit(solution)/shard_map/all_to_all | solution.py:230
  29.9 25.0 %shard_map.98 = bf16[4,128,768]{2,1,0:T(8,128)(2,1)} custom-call(bf16[1,128,3072]{2,1,0:T(8,128)(2,1)} %first_ref.5, bf16[1,128,3072]{2,1,0:T(8,128)(2,1)} %second_ref.5), custom_call_target="tpu_custom_call" | custom-call | tf_op jit(solution)/shard_map/pallas_call | solution.py:66
  54.9 0.0 all-to-all-done.1
  54.9 3.5 %all-to-all-start.2 = ((bf16[4,128,768]{2,1,0:T(8,128)(2,1)}), bf16[4,128,768]{2,1,0:T(8,128)(2,1)S(1)}, u32[]{:S(2)}, u32[]{:S(2)}) async-start(bf16[4,128,768]{2,1,0:T(8,128)(2,1)} %shard_map.98), calls=%async_computation.2 | async-start | bytes 1572864 | tf_op jit(solution)/shard_map/all_to_all | solution.py:230
  58.4 5.1 %collective-permute-start = (bf16[512,768]{1,0:T(8,128)(2,1)S(1)}, bf16[512,768]{1,0:T(8,128)(2,1)}, u32[]{:S(2)}, u32[]{:S(2)}) collective-permute-start(bf16[512,768]{1,0:T(8,128)(2,1)S(1)} %bitcast.34), channel_id=1, source_target_pairs={{0,8},{2,10},{4,12},{6,14},{8,16},{10,18},{12,20},{14,22},{16,24},... | collective-permute-start | bytes 2359304 | tf_op jit(solution)/shard_map/ppermute | solution.py:26
  63.6 1.3 collective-permute-start.1
  64.9 0.2 reduce-window.4
  65.0 48.8 %shard_map.95 = bf16[4,128,1536]{2,1,0:T(8,128)(2,1)} custom-call(bf16[1,128,3072]{2,1,0:T(8,128)(2,1)} %first_ref.3, bf16[1,128,3072]{2,1,0:T(8,128)(2,1)} %second_ref.3), custom_call_target="tpu_custom_call" | custom-call | tf_op jit(solution)/shard_map/pallas_call | solution.py:66
  113.9 0.0 copy-start.11
  113.9 0.0 copy-start.12
  113.9 0.0 all-to-all-done.2
  113.9 3.6 %all-to-all-start = ((bf16[4,128,1536]{2,1,0:T(8,128)(2,1)}), bf16[4,128,1536]{2,1,0:T(8,128)(2,1)S(1)}, u32[]{:S(2)}, u32[]{:S(2)}) async-start(bf16[4,128,1536]{2,1,0:T(8,128)(2,1)} %shard_map.95), calls=%async_computation | async-start | bytes 3145728 | tf_op jit(solution)/shard_map/all_to_all | solution.py:230
  117.5 5.4 %collective-permute-start.7 = (bf16[512,768]{1,0:T(8,128)(2,1)S(1)}, bf16[512,768]{1,0:T(8,128)(2,1)}, u32[]{:S(2)}, u32[]{:S(2)}) collective-permute-start(bf16[512,768]{1,0:T(8,128)(2,1)S(1)} %bitcast.31), channel_id=1, source_target_pairs={{0,8},{2,10},{4,12},{6,14},{8,16},{10,18},{12,20},{14,22},{16,24},... | collective-permute-start | bytes 2359304 | tf_op jit(solution)/shard_map/ppermute | solution.py:26
  122.9 1.3 collective-permute-start.8
  124.2 0.1 convert_reduce_fusion
  124.3 0.2 select_reduce_fusion.2
  124.5 1.9 slice.20
  126.4 5.5 %collective-permute-start.2 = (bf16[384,768]{1,0:T(8,128)(2,1)}, bf16[384,768]{1,0:T(8,128)(2,1)}, u32[]{:S(2)}, u32[]{:S(2)}) collective-permute-start(bf16[384,768]{1,0:T(8,128)(2,1)} %slice.20), channel_id=1, source_target_pairs={{0,8},{2,10},{4,12},{6,14},{8,16},{10,18},{12,20},{14,22},{16,24},... | collective-permute-start | bytes 1769480 | tf_op jit(solution)/shard_map/ppermute | solution.py:26
  132.0 2.0 slice.21
  133.9 1.3 collective-permute-start.3
  135.2 4.7 %collective-permute-done.7.refs_2_ = bf16[512,768]{1,0:T(8,128)(2,1)} collective-permute-done((bf16[512,768]{1,0:T(8,128)(2,1)S(1)}, bf16[512,768]{1,0:T(8,128)(2,1)}, u32[]{:S(2)}, u32[]{:S(2)}) %collective-permute-start.7) | collective-permute-done | bytes 786464 | tf_op jit(solution)/shard_map/ppermute | solution.py:26
  140.0 1.9 slice.22
  141.9 5.3 %collective-permute-start.9 = (bf16[384,768]{1,0:T(8,128)(2,1)}, bf16[384,768]{1,0:T(8,128)(2,1)}, u32[]{:S(2)}, u32[]{:S(2)}) collective-permute-start(bf16[384,768]{1,0:T(8,128)(2,1)} %slice.22), channel_id=1, source_target_pairs={{0,8},{2,10},{4,12},{6,14},{8,16},{10,18},{12,20},{14,22},{16,24},... | collective-permute-start | bytes 1769480 | tf_op jit(solution)/shard_map/ppermute | solution.py:26
  147.2 2.0 slice.23
  149.2 1.3 collective-permute-start.10
  150.4 0.1 pad_add_fusion.place_ref
  150.5 0.2 select_reduce_fusion.1
  150.7 0.2 select_reduce_fusion.weight_ref
  150.9 1.8 collective-permute-done.2.refs_4_
  152.7 5.3 %collective-permute-done.3.refs_5_ = bf16[384,768]{1,0:T(8,128)(2,1)} collective-permute-done((bf16[384,768]{1,0:T(8,128)(2,1)}, bf16[384,768]{1,0:T(8,128)(2,1)}, u32[]{:S(2)}, u32[]{:S(2)}) %collective-permute-start.3) | collective-permute-done | bytes 589856 | tf_op jit(solution)/shard_map/ppermute | solution.py:26
  158.0 8.0 %shard_map.97 = (bf16[128,384]{1,0:T(8,128)(2,1)S(1)}, bf16[128,384]{1,0:T(8,128)(2,1)S(1)}, bf16[128,384]{1,0:T(8,128)(2,1)S(1)}, bf16[128,384]{1,0:T(8,128)(2,1)S(1)}, f32[8,128]{1,0:T(8,128)S(1)}) custom-call(s32[2]{0:T(128)S(1)} %pad_add_fusion.place_ref, s32[1,4]{1,0:T(1,128)S(1)} %copy-done.4, s32[1,16]{1,0:T(1,128)S(1)} %copy-done.3, ...), custom_call_target="tpu_custom_call" | custom-call | flops 805306368 | bytes 5111808 | tf_op jit(solution)/shard_map/pallas_call | solution.py:196
  165.9 0.6 copy-done
  166.6 3.2 %collective-permute-done.10.refs_5_ = bf16[384,768]{1,0:T(8,128)(2,1)} collective-permute-done((bf16[384,768]{1,0:T(8,128)(2,1)}, bf16[384,768]{1,0:T(8,128)(2,1)}, u32[]{:S(2)}, u32[]{:S(2)}) %collective-permute-start.10) | collective-permute-done | bytes 589856 | tf_op jit(solution)/shard_map/ppermute | solution.py:26
  169.8 8.0 %shard_map.99 = (bf16[128,384]{1,0:T(8,128)(2,1)S(1)}, bf16[128,384]{1,0:T(8,128)(2,1)S(1)}, bf16[128,384]{1,0:T(8,128)(2,1)S(1)}, bf16[128,384]{1,0:T(8,128)(2,1)S(1)}, f32[8,128]{1,0:T(8,128)S(1)}) custom-call(s32[2]{0:T(128)S(1)} %pad_add_fusion.place_ref, s32[1,4]{1,0:T(1,128)S(1)} %copy-done.4, s32[1,16]{1,0:T(1,128)S(1)} %copy-done.3, ...), custom_call_target="tpu_custom_call" | custom-call | flops 805306368 | bytes 5111808 | tf_op jit(solution)/shard_map/pallas_call | solution.py:196
  177.8 0.6 copy-done.1
  178.4 0.6 add_reduce_fusion
  179.0 1.3 broadcast_in_dim.45
  180.3 4.1 %all-to-all-start.3 = ((f32[32,1,128]{2,1,0:T(1,128)}), f32[32,1,128]{2,1,0:T(1,128)S(1)}, u32[]{:S(2)}, u32[]{:S(2)}) async-start(f32[32,1,128]{2,1,0:T(1,128)} %broadcast_in_dim.45), calls=%async_computation.3 | async-start | bytes 32768 | tf_op jit(solution)/shard_map/all_to_all | solution.py:285
  184.4 1.8 collective-permute-start.5
  186.2 0.4 collective-permute-start.11
  186.6 1.8 collective-permute-start.12
  188.4 3.2 %all-to-all-done.3 = f32[32,1,128]{2,1,0:T(1,128)S(1)} async-done(((f32[32,1,128]{2,1,0:T(1,128)}), f32[32,1,128]{2,1,0:T(1,128)S(1)}, u32[]{:S(2)}, u32[]{:S(2)}) %all-to-all-start.3) | async-done | bytes 16416 | tf_op jit(solution)/shard_map/all_to_all | solution.py:285
  191.5 0.6 slice_reduce_fusion
  192.2 1.9 collective-permute-done.12.refs_6_
  194.0 1.5 collective-permute-done.13.refs_7_
  195.6 0.6 copy-done.10
  196.2 25.7 %unpack.1 = bf16[1,128,3072]{2,1,0:T(8,128)(2,1)} custom-call(s32[2]{0:T(128)} %copy-done.2, bf16[128,384]{1,0:T(8,128)(2,1)} %copy-done, bf16[128,384]{1,0:T(8,128)(2,1)} %copy-done.5, bf16[128,384]{1,0:T(8,128)(2,1)} %copy-done.6, bf16[128,384]{1,0:T(8,128)(2,1)} %copy-done.7, bf16[128,384]{1,0:T(8,128)(2,1)} %copy-done.1, bf16[128,384]{1,0:T(8,128)(2,1)} %copy-done.8, ...), custom_call_target="tpu_custom_call" | custom-call | tf_op jit(solution)/shard_map/unpack/pallas_call | solution.py:98
  (37 shorter events, 0.1 us)
Async XLA Ops:
  25.6 29.3 %all-to-all-start.1 = ((bf16[4,128,768]{2,1,0:T(8,128)(2,1)}), bf16[4,128,768]{2,1,0:T(8,128)(2,1)S(1)}, u32[]{:S(2)}, u32[]{:S(2)}) async-start(bf16[4,128,768]{2,1,0:T(8,128)(2,1)} %shard_map.96), calls=%async_computation.1 | async-start | bytes 1572864 | tf_op jit(solution)/shard_map/all_to_all | solution.py:230
  29.9 35.0 %copy-start.4 = (s32[1,4]{1,0:T(1,128)S(1)}, s32[1,4]{1,0:T(1,128)}, u32[]{:S(2)}) copy-start(s32[1,4]{1,0:T(1,128)} %clip_ref.3) | copy-start | bytes 52
  54.9 59.0 %all-to-all-start.2 = ((bf16[4,128,768]{2,1,0:T(8,128)(2,1)}), bf16[4,128,768]{2,1,0:T(8,128)(2,1)S(1)}, u32[]{:S(2)}, u32[]{:S(2)}) async-start(bf16[4,128,768]{2,1,0:T(8,128)(2,1)} %shard_map.98), calls=%async_computation.2 | async-start | bytes 1572864 | tf_op jit(solution)/shard_map/all_to_all | solution.py:230
  58.4 66.1 %collective-permute-start = (bf16[512,768]{1,0:T(8,128)(2,1)S(1)}, bf16[512,768]{1,0:T(8,128)(2,1)}, u32[]{:S(2)}, u32[]{:S(2)}) collective-permute-start(bf16[512,768]{1,0:T(8,128)(2,1)S(1)} %bitcast.34), channel_id=1, source_target_pairs={{0,8},{2,10},{4,12},{6,14},{8,16},{10,18},{12,20},{14,22},{16,24},... | collective-permute-start | bytes 2359304 | tf_op jit(solution)/shard_map/ppermute | solution.py:26
  63.6 68.4 %collective-permute-start.1 = (bf16[512,768]{1,0:T(8,128)(2,1)S(1)}, bf16[512,768]{1,0:T(8,128)(2,1)}, u32[]{:S(2)}, u32[]{:S(2)}) collective-permute-start(bf16[512,768]{1,0:T(8,128)(2,1)S(1)} %bitcast.35), channel_id=1, source_target_pairs={{8,0},{10,2},{12,4},{14,6},{16,8},{18,10},{20,12},{22,14},{24,16},... | collective-permute-start | bytes 2359304 | tf_op jit(solution)/shard_map/ppermute | solution.py:26
  113.9 10.3 %copy-start.11 = (f32[1,4]{1,0:T(1,128)S(1)}, f32[1,4]{1,0:T(1,128)}, u32[]{:S(2)}) copy-start(f32[1,4]{1,0:T(1,128)} %param.15) | copy-start | bytes 52
  113.9 10.3 %copy-start.12 = (s32[1,4]{1,0:T(1,128)S(1)}, s32[1,4]{1,0:T(1,128)}, u32[]{:S(2)}) copy-start(s32[1,4]{1,0:T(1,128)} %param.14) | copy-start | bytes 52
  113.9 37.0 %all-to-all-start = ((bf16[4,128,1536]{2,1,0:T(8,128)(2,1)}), bf16[4,128,1536]{2,1,0:T(8,128)(2,1)S(1)}, u32[]{:S(2)}, u32[]{:S(2)}) async-start(bf16[4,128,1536]{2,1,0:T(8,128)(2,1)} %shard_map.95), calls=%async_computation | async-start | bytes 3145728 | tf_op jit(solution)/shard_map/all_to_all | solution.py:230
  117.5 22.5 %collective-permute-start.7 = (bf16[512,768]{1,0:T(8,128)(2,1)S(1)}, bf16[512,768]{1,0:T(8,128)(2,1)}, u32[]{:S(2)}, u32[]{:S(2)}) collective-permute-start(bf16[512,768]{1,0:T(8,128)(2,1)S(1)} %bitcast.31), channel_id=1, source_target_pairs={{0,8},{2,10},{4,12},{6,14},{8,16},{10,18},{12,20},{14,22},{16,24},... | collective-permute-start | bytes 2359304 | tf_op jit(solution)/shard_map/ppermute | solution.py:26
  122.9 24.3 %collective-permute-start.8 = (bf16[512,768]{1,0:T(8,128)(2,1)S(1)}, bf16[512,768]{1,0:T(8,128)(2,1)}, u32[]{:S(2)}, u32[]{:S(2)}) collective-permute-start(bf16[512,768]{1,0:T(8,128)(2,1)S(1)} %bitcast.32), channel_id=1, source_target_pairs={{8,0},{10,2},{12,4},{14,6},{16,8},{18,10},{20,12},{22,14},{24,16},... | collective-permute-start | bytes 2359304 | tf_op jit(solution)/shard_map/ppermute | solution.py:26
  126.4 24.1 %copy-start.3 = (s32[1,16]{1,0:T(1,128)S(1)}, s32[1,16]{1,0:T(1,128)}, u32[]{:S(2)}) copy-start(s32[1,16]{1,0:T(1,128)} %valid_ref.3) | copy-start | bytes 196
  126.4 26.2 %collective-permute-start.2 = (bf16[384,768]{1,0:T(8,128)(2,1)}, bf16[384,768]{1,0:T(8,128)(2,1)}, u32[]{:S(2)}, u32[]{:S(2)}) collective-permute-start(bf16[384,768]{1,0:T(8,128)(2,1)} %slice.20), channel_id=1, source_target_pairs={{0,8},{2,10},{4,12},{6,14},{8,16},{10,18},{12,20},{14,22},{16,24},... | collective-permute-start | bytes 1769480 | tf_op jit(solution)/shard_map/ppermute | solution.py:26
  133.9 24.0 %collective-permute-start.3 = (bf16[384,768]{1,0:T(8,128)(2,1)}, bf16[384,768]{1,0:T(8,128)(2,1)}, u32[]{:S(2)}, u32[]{:S(2)}) collective-permute-start(bf16[384,768]{1,0:T(8,128)(2,1)} %slice.21), channel_id=1, source_target_pairs={{8,0},{10,2},{12,4},{14,6},{16,8},{18,10},{20,12},{22,14},{24,16},... | collective-permute-start | bytes 1769480 | tf_op jit(solution)/shard_map/ppermute | solution.py:26
  141.9 24.7 %collective-permute-start.9 = (bf16[384,768]{1,0:T(8,128)(2,1)}, bf16[384,768]{1,0:T(8,128)(2,1)}, u32[]{:S(2)}, u32[]{:S(2)}) collective-permute-start(bf16[384,768]{1,0:T(8,128)(2,1)} %slice.22), channel_id=1, source_target_pairs={{0,8},{2,10},{4,12},{6,14},{8,16},{10,18},{12,20},{14,22},{16,24},... | collective-permute-start | bytes 1769480 | tf_op jit(solution)/shard_map/ppermute | solution.py:26
  149.2 20.7 %collective-permute-start.10 = (bf16[384,768]{1,0:T(8,128)(2,1)}, bf16[384,768]{1,0:T(8,128)(2,1)}, u32[]{:S(2)}, u32[]{:S(2)}) collective-permute-start(bf16[384,768]{1,0:T(8,128)(2,1)} %slice.23), channel_id=1, source_target_pairs={{8,0},{10,2},{12,4},{14,6},{16,8},{18,10},{20,12},{22,14},{24,16},... | collective-permute-start | bytes 1769480 | tf_op jit(solution)/shard_map/ppermute | solution.py:26
  150.5 19.3 %copy-start.2 = (s32[2]{0:T(128)}, s32[2]{0:T(128)S(1)}, u32[]{:S(2)}) copy-start(s32[2]{0:T(128)S(1)} %pad_add_fusion.place_ref) | copy-start | bytes 28
  165.9 0.7 copy-start
  166.6 21.8 %collective-permute-start.4 = (bf16[128,384]{1,0:T(8,128)(2,1)S(1)}, bf16[128,384]{1,0:T(8,128)(2,1)S(1)}, u32[]{:S(2)}, u32[]{:S(2)}) collective-permute-start(bf16[128,384]{1,0:T(8,128)(2,1)S(1)} %get-tuple-element.13), channel_id=1, source_target_pairs={{0,2},{2,0},{4,6},{6,4},{8,10},{10,8},{12,14},{14,12},{16,18},{18,... | collective-permute-start | bytes 294920 | tf_op jit(solution)/shard_map/ppermute | solution.py:279
  177.8 0.6 copy-start.1
  180.3 11.3 %all-to-all-start.3 = ((f32[32,1,128]{2,1,0:T(1,128)}), f32[32,1,128]{2,1,0:T(1,128)S(1)}, u32[]{:S(2)}, u32[]{:S(2)}) async-start(f32[32,1,128]{2,1,0:T(1,128)} %broadcast_in_dim.45), calls=%async_computation.3 | async-start | bytes 32768 | tf_op jit(solution)/shard_map/all_to_all | solution.py:285
  184.4 7.8 %collective-permute-start.5 = (bf16[128,384]{1,0:T(8,128)(2,1)S(1)}, bf16[128,384]{1,0:T(8,128)(2,1)S(1)}, u32[]{:S(2)}, u32[]{:S(2)}) collective-permute-start(bf16[128,384]{1,0:T(8,128)(2,1)S(1)} %get-tuple-element.14), channel_id=1, source_target_pairs={{0,4},{2,6},{4,0},{6,2},{8,12},{10,14},{12,8},{14,10},{16,20},{18,... | collective-permute-start | bytes 294920 | tf_op jit(solution)/shard_map/ppermute | solution.py:279
  186.2 5.9 %collective-permute-start.6 = (bf16[128,384]{1,0:T(8,128)(2,1)S(1)}, bf16[128,384]{1,0:T(8,128)(2,1)S(1)}, u32[]{:S(2)}, u32[]{:S(2)}) collective-permute-start(bf16[128,384]{1,0:T(8,128)(2,1)S(1)} %get-tuple-element.15), channel_id=1, source_target_pairs={{0,6},{2,4},{4,2},{6,0},{8,14},{10,12},{12,10},{14,8},{16,22},{18,... | collective-permute-start | bytes 294920 | tf_op jit(solution)/shard_map/ppermute | solution.py:279
  186.2 5.9 %collective-permute-start.11 = (bf16[128,384]{1,0:T(8,128)(2,1)S(1)}, bf16[128,384]{1,0:T(8,128)(2,1)S(1)}, u32[]{:S(2)}, u32[]{:S(2)}) collective-permute-start(bf16[128,384]{1,0:T(8,128)(2,1)S(1)} %get-tuple-element.17), channel_id=1, source_target_pairs={{0,2},{2,0},{4,6},{6,4},{8,10},{10,8},{12,14},{14,12},{16,18},{18,... | collective-permute-start | bytes 294920 | tf_op jit(solution)/shard_map/ppermute | solution.py:279
  186.6 7.5 %collective-permute-start.12 = (bf16[128,384]{1,0:T(8,128)(2,1)S(1)}, bf16[128,384]{1,0:T(8,128)(2,1)S(1)}, u32[]{:S(2)}, u32[]{:S(2)}) collective-permute-start(bf16[128,384]{1,0:T(8,128)(2,1)S(1)} %get-tuple-element.18), channel_id=1, source_target_pairs={{0,4},{2,6},{4,0},{6,2},{8,12},{10,14},{12,8},{14,10},{16,20},{18,... | collective-permute-start | bytes 294920 | tf_op jit(solution)/shard_map/ppermute | solution.py:279
  188.4 7.2 %copy-start.5 = (bf16[128,384]{1,0:T(8,128)(2,1)}, bf16[128,384]{1,0:T(8,128)(2,1)S(1)}, u32[]{:S(2)}) copy-start(bf16[128,384]{1,0:T(8,128)(2,1)S(1)} %collective-permute-done.4.refs_1_) | copy-start | bytes 294916
  188.4 7.2 %collective-permute-start.13 = (bf16[128,384]{1,0:T(8,128)(2,1)S(1)}, bf16[128,384]{1,0:T(8,128)(2,1)S(1)}, u32[]{:S(2)}, u32[]{:S(2)}) collective-permute-start(bf16[128,384]{1,0:T(8,128)(2,1)S(1)} %get-tuple-element.19), channel_id=1, source_target_pairs={{0,6},{2,4},{4,2},{6,0},{8,14},{10,12},{12,10},{14,8},{16,22},{18,... | collective-permute-start | bytes 294920 | tf_op jit(solution)/shard_map/ppermute | solution.py:279
  192.1 3.4 %copy-start.6 = (bf16[128,384]{1,0:T(8,128)(2,1)}, bf16[128,384]{1,0:T(8,128)(2,1)S(1)}, u32[]{:S(2)}) copy-start(bf16[128,384]{1,0:T(8,128)(2,1)S(1)} %collective-permute-done.5.refs_2_) | copy-start | bytes 294916
  192.2 3.4 %copy-start.7 = (bf16[128,384]{1,0:T(8,128)(2,1)}, bf16[128,384]{1,0:T(8,128)(2,1)S(1)}, u32[]{:S(2)}) copy-start(bf16[128,384]{1,0:T(8,128)(2,1)S(1)} %collective-permute-done.6.refs_3_) | copy-start | bytes 294916
  192.2 3.4 %copy-start.8 = (bf16[128,384]{1,0:T(8,128)(2,1)}, bf16[128,384]{1,0:T(8,128)(2,1)S(1)}, u32[]{:S(2)}) copy-start(bf16[128,384]{1,0:T(8,128)(2,1)S(1)} %collective-permute-done.11.refs_5_) | copy-start | bytes 294916
  194.0 1.6 copy-start.9
  195.6 0.6 copy-start.10

commit v3 on v2

--- a/solution.py
+++ b/solution.py
@@ -43,64 +43,42 @@
         copy.wait()
 
 
-def pack_body(spans, first_ref, second_ref, *refs):
-    outs, sems = refs[:-1], refs[-1]
+def pack_body(low, high, first_ref, second_ref, out_ref):
     share = first_ref.shape[2] // LEVEL
-    copies = []
-    for out_ref, (low, high) in zip(outs, spans):
-        for part in range(LEVEL):
-            for side, ref in enumerate((first_ref, second_ref)):
-                copies.append(
-                    pltpu.make_async_copy(
-                        ref.at[0, :, pl.ds(part * share + low, high - low)],
-                        out_ref.at[part, :, pl.ds(side * (high - low), high - low)],
-                        sems.at[len(copies)],
-                    )
-                )
-    moved(copies)
-
-
-def packed(first, second, spans):
-    rows = first.shape[1]
-    hbm = pl.BlockSpec(memory_space=pl.ANY)
+    span = high - low
+    for part in range(LEVEL):
+        for side, ref in enumerate((first_ref, second_ref)):
+            out_ref[part, :, side * span : (side + 1) * span] = ref[
+                0, :, part * share + low : part * share + high
+            ]
+
+
+def packed(first, second, low, high):
+    vmem = pl.BlockSpec(memory_space=pltpu.VMEM)
     return pl.pallas_call(
-        functools.partial(pack_body, spans),
-        out_shape=[
-            jax.ShapeDtypeStruct((LEVEL, rows, 2 * (high - low)), first.dtype)
-            for low, high in spans
-        ],
-        in_specs=[hbm, hbm],
-        out_specs=[hbm] * len(spans),
-        scratch_shapes=[pltpu.SemaphoreType.DMA((2 * LEVEL * len(spans),))],
+        functools.partial(pack_body, low, high),
+        out_shape=jax.ShapeDtypeStruct((LEVEL, first.shape[1], 2 * (high - low)), first.dtype),
+        in_specs=[vmem, vmem],
+        out_specs=vmem,
     )(first, second)
 
 
 def unpack_body(spans, place_ref, *refs):
-    parts, out_ref, sems = refs[:-2], refs[-2], refs[-1]
+    parts, out_ref = refs[:-1], refs[-1]
     share = out_ref.shape[2] // LEVEL
-    own = place_ref[1]
-    copies = []
     for index, (low, high) in enumerate(spans):
         for step in range(LEVEL):
-            first = pl.multiple_of(jnp.bitwise_xor(own, step) * share + low, HEAD)
-            copies.append(
-                pltpu.make_async_copy(
-                    parts[index * LEVEL + step],
-                    out_ref.at[0, :, pl.ds(first, high - low)],
-                    sems.at[len(copies)],
-                )
-            )
-    moved(copies)
+            first = pl.multiple_of(jnp.bitwise_xor(place_ref[1], step) * share + low, HEAD)
+            out_ref[0, :, pl.ds(first, high - low)] = parts[index * LEVEL + step][...]
 
 
 def unpacked(place, outs, spans, width):
-    hbm = pl.BlockSpec(memory_space=pl.ANY)
+    vmem = pl.BlockSpec(memory_space=pltpu.VMEM)
     return pl.pallas_call(
         functools.partial(unpack_body, spans),
         out_shape=jax.ShapeDtypeStruct((1, outs[0].shape[0], width), outs[0].dtype),
-        in_specs=[pl.BlockSpec(memory_space=pltpu.SMEM)] + [hbm] * len(outs),
-        out_specs=hbm,
-        scratch_shapes=[pltpu.SemaphoreType.DMA((len(outs),))],
+        in_specs=[pl.BlockSpec(memory_space=pltpu.SMEM)] + [vmem] * len(outs),
+        out_specs=vmem,
         name="unpack",
     )(place, *outs)
 
@@ -247,10 +225,10 @@
         return found
 
     own_kv = []
-    for span in spans:
-        parts = packed(keys, values, [span])
-        own_kv += [exchanged(part) for part in parts]
-    (part,) = packed(queries, next_latent, [(0, share)])
+    for low, high in spans:
+        part = packed(keys, values, low, high)
+        own_kv.append(exchanged(part))
+    part = packed(queries, next_latent, 0, share)
     qn = exchanged(part)
 
     valid_row = valid_counts[0]

time: 223 us -> 121 us (0.54)
  Pallas kernels: 140 us -> 25.4 us
  waiting for transfers between devices: 21.6 us -> 35 us
    pallas_call x3, Pallas kernels: 98.8 us -> 7.29 us  [packed(): pl.pallas_call(functools.partial(pack_body, low, high), out_shape=jax.Sha...]
    pallas_call x1, Pallas kernels: 25.7 us -> 2.17 us  [unpacked(): pl.pallas_call(functools.partial(unpack_body, spans), out_shape=jax.Shape...]
    all_to_all x3, waiting for transfers between devices: 0.01 us -> 11.7 us  [exchange(): lax.all_to_all(value, 'tok', 0, 0, axis_index_groups=levels, tiled=True)]
  transfers between devices with their start and end apart: 18 -> 18, of which waited for: 7 -> 10; matrix products, arithmetic and copies ran while one was open for 5% -> 9% of each run, Pallas kernels for 40% -> 17%
where the time goes in v3:
time: 121 us; the launch traced here: 120 us
  starting transfers between devices  45.4 us (38%)
  waiting for transfers between devices  35 us (29%)
  Pallas kernels  25.4 us (21%)
  local copies, waits for them, and re-layouts  11 us (9%)
  other arithmetic  2.12 us (2%)
    ppermute x8, starting transfers between devices, passed_along(): lax.ppermute(value, axis, [(source, source + steps) for source in range(f...  26 us
    ppermute x8, waiting for transfers between devices, passed_along(): lax.ppermute(value, axis, [(source, source + steps) for source in range(f...  16.8 us
    pallas_call x2, Pallas kernels, attend(): pl.pallas_call(functools.partial(kernel_body, pieces, width // HEAD, firs...  15.9 us
    all_to_all x3, waiting for transfers between devices, exchange(): lax.all_to_all(value, 'tok', 0, 0, axis_index_groups=levels, tiled=True)  11.7 us
    all_to_all x3, starting transfers between devices, exchange(): lax.all_to_all(value, 'tok', 0, 0, axis_index_groups=levels, tiled=True)  11.3 us
    pallas_call x3, Pallas kernels, packed(): pl.pallas_call(functools.partial(pack_body, low, high), out_shape=jax.Sha...  7.29 us
    all_to_all x1, starting transfers between devices, step(): lax.all_to_all(spread, ('tok', 'grp'), 0, 0, tiled=True)[:, 0]  4.1 us
    ppermute x6, starting transfers between devices, step(): outs.append(lax.ppermute(out[step], 'tok', partners))  3.98 us
  transfers between devices with their start and end apart: 18, of which 10 were waited for; matrix products, arithmetic and copies ran while one was open for 9% of the time, Pallas kernels for 17%

profile of v3, /device:TPU:0, one launch (start us, length us, event | category | flops | bytes accessed | tf_op | source)
XLA Modules:
  0.0 119.7 jit_solution(12041866521961580578)
XLA Ops:
  0.6 2.3 %shard_map.96 = bf16[4,128,768]{2,1,0:T(8,128)(2,1)} custom-call(bf16[1,128,3072]{2,1,0:T(8,128)(2,1)} %first_ref.5, bf16[1,128,3072]{2,1,0:T(8,128)(2,1)} %second_ref.5), custom_call_target="tpu_custom_call" | custom-call | tf_op jit(solution)/shard_map/pallas_call | solution.py:58
  2.9 4.2 %all-to-all-start.1 = ((bf16[4,128,768]{2,1,0:T(8,128)(2,1)}), bf16[4,128,768]{2,1,0:T(8,128)(2,1)S(1)}, u32[]{:S(2)}, u32[]{:S(2)}) async-start(bf16[4,128,768]{2,1,0:T(8,128)(2,1)} %shard_map.96), calls=%async_computation.1 | async-start | bytes 1572864 | tf_op jit(solution)/shard_map/all_to_all | solution.py:208
  7.2 2.3 %shard_map.98 = bf16[4,128,768]{2,1,0:T(8,128)(2,1)} custom-call(bf16[1,128,3072]{2,1,0:T(8,128)(2,1)} %first_ref.5, bf16[1,128,3072]{2,1,0:T(8,128)(2,1)} %second_ref.5), custom_call_target="tpu_custom_call" | custom-call | tf_op jit(solution)/shard_map/pallas_call | solution.py:58
  9.5 9.3 %all-to-all-done.1 = bf16[4,128,768]{2,1,0:T(8,128)(2,1)S(1)} async-done(((bf16[4,128,768]{2,1,0:T(8,128)(2,1)}), bf16[4,128,768]{2,1,0:T(8,128)(2,1)S(1)}, u32[]{:S(2)}, u32[]{:S(2)}) %all-to-all-start.1) | async-done | bytes 786464 | tf_op jit(solution)/shard_map/all_to_all | solution.py:208
  18.8 3.5 %all-to-all-start.2 = ((bf16[4,128,768]{2,1,0:T(8,128)(2,1)}), bf16[4,128,768]{2,1,0:T(8,128)(2,1)S(1)}, u32[]{:S(2)}, u32[]{:S(2)}) async-start(bf16[4,128,768]{2,1,0:T(8,128)(2,1)} %shard_map.98), calls=%async_computation.2 | async-start | bytes 1572864 | tf_op jit(solution)/shard_map/all_to_all | solution.py:208
  22.3 5.1 %collective-permute-start = (bf16[512,768]{1,0:T(8,128)(2,1)S(1)}, bf16[512,768]{1,0:T(8,128)(2,1)}, u32[]{:S(2)}, u32[]{:S(2)}) collective-permute-start(bf16[512,768]{1,0:T(8,128)(2,1)S(1)} %bitcast.34), channel_id=1, source_target_pairs={{0,8},{2,10},{4,12},{6,14},{8,16},{10,18},{12,20},{14,22},{16,24},... | collective-permute-start | bytes 2359304 | tf_op jit(solution)/shard_map/ppermute | solution.py:26
  27.4 1.3 %collective-permute-start.1 = (bf16[512,768]{1,0:T(8,128)(2,1)S(1)}, bf16[512,768]{1,0:T(8,128)(2,1)}, u32[]{:S(2)}, u32[]{:S(2)}) collective-permute-start(bf16[512,768]{1,0:T(8,128)(2,1)S(1)} %bitcast.35), channel_id=1, source_target_pairs={{8,0},{10,2},{12,4},{14,6},{16,8},{18,10},{20,12},{22,14},{24,16},... | collective-permute-start | bytes 2359304 | tf_op jit(solution)/shard_map/ppermute | solution.py:26
  28.7 0.2 reduce-window.4
  28.9 2.6 %shard_map.95 = bf16[4,128,1536]{2,1,0:T(8,128)(2,1)} custom-call(bf16[1,128,3072]{2,1,0:T(8,128)(2,1)} %first_ref.3, bf16[1,128,3072]{2,1,0:T(8,128)(2,1)} %second_ref.3), custom_call_target="tpu_custom_call" | custom-call | tf_op jit(solution)/shard_map/pallas_call | solution.py:58
  31.5 2.4 %all-to-all-done.2 = bf16[4,128,768]{2,1,0:T(8,128)(2,1)S(1)} async-done(((bf16[4,128,768]{2,1,0:T(8,128)(2,1)}), bf16[4,128,768]{2,1,0:T(8,128)(2,1)S(1)}, u32[]{:S(2)}, u32[]{:S(2)}) %all-to-all-start.2) | async-done | bytes 786464 | tf_op jit(solution)/shard_map/all_to_all | solution.py:208
  33.9 3.6 %all-to-all-start = ((bf16[4,128,1536]{2,1,0:T(8,128)(2,1)}), bf16[4,128,1536]{2,1,0:T(8,128)(2,1)S(1)}, u32[]{:S(2)}, u32[]{:S(2)}) async-start(bf16[4,128,1536]{2,1,0:T(8,128)(2,1)} %shard_map.95), calls=%async_computation | async-start | bytes 3145728 | tf_op jit(solution)/shard_map/all_to_all | solution.py:208
  37.5 5.1 %collective-permute-start.7 = (bf16[512,768]{1,0:T(8,128)(2,1)S(1)}, bf16[512,768]{1,0:T(8,128)(2,1)}, u32[]{:S(2)}, u32[]{:S(2)}) collective-permute-start(bf16[512,768]{1,0:T(8,128)(2,1)S(1)} %bitcast.31), channel_id=1, source_target_pairs={{0,8},{2,10},{4,12},{6,14},{8,16},{10,18},{12,20},{14,22},{16,24},... | collective-permute-start | bytes 2359304 | tf_op jit(solution)/shard_map/ppermute | solution.py:26
  42.5 1.3 %collective-permute-start.8 = (bf16[512,768]{1,0:T(8,128)(2,1)S(1)}, bf16[512,768]{1,0:T(8,128)(2,1)}, u32[]{:S(2)}, u32[]{:S(2)}) collective-permute-start(bf16[512,768]{1,0:T(8,128)(2,1)S(1)} %bitcast.32), channel_id=1, source_target_pairs={{8,0},{10,2},{12,4},{14,6},{16,8},{18,10},{20,12},{22,14},{24,16},... | collective-permute-start | bytes 2359304 | tf_op jit(solution)/shard_map/ppermute | solution.py:26
  43.9 0.1 convert_reduce_fusion
  44.0 0.2 select_reduce_fusion.2
  44.1 0.3 collective-permute-done.refs_2_
  44.4 1.9 %slice.20 = bf16[384,768]{1,0:T(8,128)(2,1)} slice(bf16[512,768]{1,0:T(8,128)(2,1)} %collective-permute-done.refs_2_), slice={[128:512], [0:768]} | slice | bytes 1179648 | tf_op jit(solution)/shard_map/slice | solution.py:220
  46.3 5.4 %collective-permute-start.2 = (bf16[384,768]{1,0:T(8,128)(2,1)}, bf16[384,768]{1,0:T(8,128)(2,1)}, u32[]{:S(2)}, u32[]{:S(2)}) collective-permute-start(bf16[384,768]{1,0:T(8,128)(2,1)} %slice.20), channel_id=1, source_target_pairs={{0,8},{2,10},{4,12},{6,14},{8,16},{10,18},{12,20},{14,22},{16,24},... | collective-permute-start | bytes 1769480 | tf_op jit(solution)/shard_map/ppermute | solution.py:26
  51.8 2.0 %slice.21 = bf16[384,768]{1,0:T(8,128)(2,1)} slice(bf16[512,768]{1,0:T(8,128)(2,1)} %collective-permute-done.1.refs_3_), slice={[0:384], [0:768]} | slice | bytes 1179648 | tf_op jit(solution)/shard_map/slice | solution.py:221
  53.8 1.3 %collective-permute-start.3 = (bf16[384,768]{1,0:T(8,128)(2,1)}, bf16[384,768]{1,0:T(8,128)(2,1)}, u32[]{:S(2)}, u32[]{:S(2)}) collective-permute-start(bf16[384,768]{1,0:T(8,128)(2,1)} %slice.21), channel_id=1, source_target_pairs={{8,0},{10,2},{12,4},{14,6},{16,8},{18,10},{20,12},{22,14},{24,16},... | collective-permute-start | bytes 1769480 | tf_op jit(solution)/shard_map/ppermute | solution.py:26
  55.1 6.2 %collective-permute-done.7.refs_2_ = bf16[512,768]{1,0:T(8,128)(2,1)} collective-permute-done((bf16[512,768]{1,0:T(8,128)(2,1)S(1)}, bf16[512,768]{1,0:T(8,128)(2,1)}, u32[]{:S(2)}, u32[]{:S(2)}) %collective-permute-start.7) | collective-permute-done | bytes 786464 | tf_op jit(solution)/shard_map/ppermute | solution.py:26
  61.3 1.9 %slice.22 = bf16[384,768]{1,0:T(8,128)(2,1)} slice(bf16[512,768]{1,0:T(8,128)(2,1)} %collective-permute-done.7.refs_2_), slice={[128:512], [0:768]} | slice | bytes 1179648 | tf_op jit(solution)/shard_map/slice | solution.py:220
  63.2 5.3 %collective-permute-start.9 = (bf16[384,768]{1,0:T(8,128)(2,1)}, bf16[384,768]{1,0:T(8,128)(2,1)}, u32[]{:S(2)}, u32[]{:S(2)}) collective-permute-start(bf16[384,768]{1,0:T(8,128)(2,1)} %slice.22), channel_id=1, source_target_pairs={{0,8},{2,10},{4,12},{6,14},{8,16},{10,18},{12,20},{14,22},{16,24},... | collective-permute-start | bytes 1769480 | tf_op jit(solution)/shard_map/ppermute | solution.py:26
  68.5 0.0 collective-permute-done.8.refs_3_
  68.5 2.0 %slice.23 = bf16[384,768]{1,0:T(8,128)(2,1)} slice(bf16[512,768]{1,0:T(8,128)(2,1)} %collective-permute-done.8.refs_3_), slice={[0:384], [0:768]} | slice | bytes 1179648 | tf_op jit(solution)/shard_map/slice | solution.py:221
  70.5 1.3 %collective-permute-start.10 = (bf16[384,768]{1,0:T(8,128)(2,1)}, bf16[384,768]{1,0:T(8,128)(2,1)}, u32[]{:S(2)}, u32[]{:S(2)}) collective-permute-start(bf16[384,768]{1,0:T(8,128)(2,1)} %slice.23), channel_id=1, source_target_pairs={{8,0},{10,2},{12,4},{14,6},{16,8},{18,10},{20,12},{22,14},{24,16},... | collective-permute-start | bytes 1769480 | tf_op jit(solution)/shard_map/ppermute | solution.py:26
  71.8 0.1 pad_add_fusion.place_ref
  71.9 0.2 select_reduce_fusion.1
  72.0 0.2 select_reduce_fusion.weight_ref
  72.2 1.8 %collective-permute-done.2.refs_4_ = bf16[384,768]{1,0:T(8,128)(2,1)} collective-permute-done((bf16[384,768]{1,0:T(8,128)(2,1)}, bf16[384,768]{1,0:T(8,128)(2,1)}, u32[]{:S(2)}, u32[]{:S(2)}) %collective-permute-start.2) | collective-permute-done | bytes 589856 | tf_op jit(solution)/shard_map/ppermute | solution.py:26
  74.0 5.3 %collective-permute-done.3.refs_5_ = bf16[384,768]{1,0:T(8,128)(2,1)} collective-permute-done((bf16[384,768]{1,0:T(8,128)(2,1)}, bf16[384,768]{1,0:T(8,128)(2,1)}, u32[]{:S(2)}, u32[]{:S(2)}) %collective-permute-start.3) | collective-permute-done | bytes 589856 | tf_op jit(solution)/shard_map/ppermute | solution.py:26
  79.3 8.0 %shard_map.97 = (bf16[128,384]{1,0:T(8,128)(2,1)S(1)}, bf16[128,384]{1,0:T(8,128)(2,1)S(1)}, bf16[128,384]{1,0:T(8,128)(2,1)S(1)}, bf16[128,384]{1,0:T(8,128)(2,1)S(1)}, f32[8,128]{1,0:T(8,128)S(1)}) custom-call(s32[2]{0:T(128)S(1)} %pad_add_fusion.place_ref, s32[1,4]{1,0:T(1,128)S(1)} %copy-done.4, s32[1,16]{1,0:T(1,128)S(1)} %copy-done.3, ...), custom_call_target="tpu_custom_call" | custom-call | flops 805306368 | bytes 5111808 | tf_op jit(solution)/shard_map/pallas_call | solution.py:174
  87.3 0.6 copy-done
  87.9 3.2 %collective-permute-done.10.refs_5_ = bf16[384,768]{1,0:T(8,128)(2,1)} collective-permute-done((bf16[384,768]{1,0:T(8,128)(2,1)}, bf16[384,768]{1,0:T(8,128)(2,1)}, u32[]{:S(2)}, u32[]{:S(2)}) %collective-permute-start.10) | collective-permute-done | bytes 589856 | tf_op jit(solution)/shard_map/ppermute | solution.py:26
  91.2 8.0 %shard_map.99 = (bf16[128,384]{1,0:T(8,128)(2,1)S(1)}, bf16[128,384]{1,0:T(8,128)(2,1)S(1)}, bf16[128,384]{1,0:T(8,128)(2,1)S(1)}, bf16[128,384]{1,0:T(8,128)(2,1)S(1)}, f32[8,128]{1,0:T(8,128)S(1)}) custom-call(s32[2]{0:T(128)S(1)} %pad_add_fusion.place_ref, s32[1,4]{1,0:T(1,128)S(1)} %copy-done.4, s32[1,16]{1,0:T(1,128)S(1)} %copy-done.3, ...), custom_call_target="tpu_custom_call" | custom-call | flops 805306368 | bytes 5111808 | tf_op jit(solution)/shard_map/pallas_call | solution.py:174
  99.1 0.6 copy-done.1
  99.8 0.6 add_reduce_fusion
  100.4 1.3 %broadcast_in_dim.45 = f32[32,1,128]{2,1,0:T(1,128)} broadcast(f32[]{:T(128)} %add_reduce_fusion), dimensions={} | broadcast | bytes 16388 | tf_op jit(solution)/shard_map/broadcast_in_dim | solution.py:262
  101.6 4.1 %all-to-all-start.3 = ((f32[32,1,128]{2,1,0:T(1,128)}), f32[32,1,128]{2,1,0:T(1,128)S(1)}, u32[]{:S(2)}, u32[]{:S(2)}) async-start(f32[32,1,128]{2,1,0:T(1,128)} %broadcast_in_dim.45), calls=%async_computation.3 | async-start | bytes 32768 | tf_op jit(solution)/shard_map/all_to_all | solution.py:263
  105.7 1.8 %collective-permute-start.5 = (bf16[128,384]{1,0:T(8,128)(2,1)S(1)}, bf16[128,384]{1,0:T(8,128)(2,1)S(1)}, u32[]{:S(2)}, u32[]{:S(2)}) collective-permute-start(bf16[128,384]{1,0:T(8,128)(2,1)S(1)} %get-tuple-element.14), channel_id=1, source_target_pairs={{0,4},{2,6},{4,0},{6,2},{8,12},{10,14},{12,8},{14,10},{16,20},{18,... | collective-permute-start | bytes 294920 | tf_op jit(solution)/shard_map/ppermute | solution.py:257
  107.6 0.4 collective-permute-start.11
  107.9 1.8 %collective-permute-start.12 = (bf16[128,384]{1,0:T(8,128)(2,1)S(1)}, bf16[128,384]{1,0:T(8,128)(2,1)S(1)}, u32[]{:S(2)}, u32[]{:S(2)}) collective-permute-start(bf16[128,384]{1,0:T(8,128)(2,1)S(1)} %get-tuple-element.18), channel_id=1, source_target_pairs={{0,4},{2,6},{4,0},{6,2},{8,12},{10,14},{12,8},{14,10},{16,20},{18,... | collective-permute-start | bytes 294920 | tf_op jit(solution)/shard_map/ppermute | solution.py:257
  109.7 3.2 %all-to-all-done.3 = f32[32,1,128]{2,1,0:T(1,128)S(1)} async-done(((f32[32,1,128]{2,1,0:T(1,128)}), f32[32,1,128]{2,1,0:T(1,128)S(1)}, u32[]{:S(2)}, u32[]{:S(2)}) %all-to-all-start.3) | async-done | bytes 16416 | tf_op jit(solution)/shard_map/all_to_all | solution.py:263
  112.9 0.6 slice_reduce_fusion
  113.5 1.9 %collective-permute-done.12.refs_6_ = bf16[128,384]{1,0:T(8,128)(2,1)S(1)} collective-permute-done((bf16[128,384]{1,0:T(8,128)(2,1)S(1)}, bf16[128,384]{1,0:T(8,128)(2,1)S(1)}, u32[]{:S(2)}, u32[]{:S(2)}) %collective-permute-start.12) | collective-permute-done | bytes 98336 | tf_op jit(solution)/shard_map/ppermute | solution.py:257
  115.4 1.5 %collective-permute-done.13.refs_7_ = bf16[128,384]{1,0:T(8,128)(2,1)S(1)} collective-permute-done((bf16[128,384]{1,0:T(8,128)(2,1)S(1)}, bf16[128,384]{1,0:T(8,128)(2,1)S(1)}, u32[]{:S(2)}, u32[]{:S(2)}) %collective-permute-start.13) | collective-permute-done | bytes 98336 | tf_op jit(solution)/shard_map/ppermute | solution.py:257
  117.0 0.6 copy-done.10
  117.6 2.2 %unpack.1 = bf16[1,128,3072]{2,1,0:T(8,128)(2,1)} custom-call(s32[2]{0:T(128)} %copy-done.2, bf16[128,384]{1,0:T(8,128)(2,1)} %copy-done, bf16[128,384]{1,0:T(8,128)(2,1)} %copy-done.5, bf16[128,384]{1,0:T(8,128)(2,1)} %copy-done.6, bf16[128,384]{1,0:T(8,128)(2,1)} %copy-done.7, bf16[128,384]{1,0:T(8,128)(2,1)} %copy-done.1, bf16[128,384]{1,0:T(8,128)(2,1)} %copy-done.8, ...), custom_call_target="tpu_custom_call" | custom-call | tf_op jit(solution)/shard_map/unpack/pallas_call | solution.py:77
  (37 shorter events, 0.1 us)
Async XLA Ops:
  2.9 15.9 %all-to-all-start.1 = ((bf16[4,128,768]{2,1,0:T(8,128)(2,1)}), bf16[4,128,768]{2,1,0:T(8,128)(2,1)S(1)}, u32[]{:S(2)}, u32[]{:S(2)}) async-start(bf16[4,128,768]{2,1,0:T(8,128)(2,1)} %shard_map.96), calls=%async_computation.1 | async-start | bytes 1572864 | tf_op jit(solution)/shard_map/all_to_all | solution.py:208
  7.2 21.5 %copy-start.4 = (s32[1,4]{1,0:T(1,128)S(1)}, s32[1,4]{1,0:T(1,128)}, u32[]{:S(2)}) copy-start(s32[1,4]{1,0:T(1,128)} %clip_ref.3) | copy-start | bytes 52
  18.8 15.1 %all-to-all-start.2 = ((bf16[4,128,768]{2,1,0:T(8,128)(2,1)}), bf16[4,128,768]{2,1,0:T(8,128)(2,1)S(1)}, u32[]{:S(2)}, u32[]{:S(2)}) async-start(bf16[4,128,768]{2,1,0:T(8,128)(2,1)} %shard_map.98), calls=%async_computation.2 | async-start | bytes 1572864 | tf_op jit(solution)/shard_map/all_to_all | solution.py:208
  22.3 22.1 %collective-permute-start = (bf16[512,768]{1,0:T(8,128)(2,1)S(1)}, bf16[512,768]{1,0:T(8,128)(2,1)}, u32[]{:S(2)}, u32[]{:S(2)}) collective-permute-start(bf16[512,768]{1,0:T(8,128)(2,1)S(1)} %bitcast.34), channel_id=1, source_target_pairs={{0,8},{2,10},{4,12},{6,14},{8,16},{10,18},{12,20},{14,22},{16,24},... | collective-permute-start | bytes 2359304 | tf_op jit(solution)/shard_map/ppermute | solution.py:26
  27.4 24.4 %collective-permute-start.1 = (bf16[512,768]{1,0:T(8,128)(2,1)S(1)}, bf16[512,768]{1,0:T(8,128)(2,1)}, u32[]{:S(2)}, u32[]{:S(2)}) collective-permute-start(bf16[512,768]{1,0:T(8,128)(2,1)S(1)} %bitcast.35), channel_id=1, source_target_pairs={{8,0},{10,2},{12,4},{14,6},{16,8},{18,10},{20,12},{22,14},{24,16},... | collective-permute-start | bytes 2359304 | tf_op jit(solution)/shard_map/ppermute | solution.py:26
  31.5 12.3 %copy-start.11 = (f32[1,4]{1,0:T(1,128)S(1)}, f32[1,4]{1,0:T(1,128)}, u32[]{:S(2)}) copy-start(f32[1,4]{1,0:T(1,128)} %param.15) | copy-start | bytes 52
  31.5 12.3 %copy-start.12 = (s32[1,4]{1,0:T(1,128)S(1)}, s32[1,4]{1,0:T(1,128)}, u32[]{:S(2)}) copy-start(s32[1,4]{1,0:T(1,128)} %param.14) | copy-start | bytes 52
  33.9 38.3 %all-to-all-start = ((bf16[4,128,1536]{2,1,0:T(8,128)(2,1)}), bf16[4,128,1536]{2,1,0:T(8,128)(2,1)S(1)}, u32[]{:S(2)}, u32[]{:S(2)}) async-start(bf16[4,128,1536]{2,1,0:T(8,128)(2,1)} %shard_map.95), calls=%async_computation | async-start | bytes 3145728 | tf_op jit(solution)/shard_map/all_to_all | solution.py:208
  37.5 23.8 %collective-permute-start.7 = (bf16[512,768]{1,0:T(8,128)(2,1)S(1)}, bf16[512,768]{1,0:T(8,128)(2,1)}, u32[]{:S(2)}, u32[]{:S(2)}) collective-permute-start(bf16[512,768]{1,0:T(8,128)(2,1)S(1)} %bitcast.31), channel_id=1, source_target_pairs={{0,8},{2,10},{4,12},{6,14},{8,16},{10,18},{12,20},{14,22},{16,24},... | collective-permute-start | bytes 2359304 | tf_op jit(solution)/shard_map/ppermute | solution.py:26
  42.5 26.0 %collective-permute-start.8 = (bf16[512,768]{1,0:T(8,128)(2,1)S(1)}, bf16[512,768]{1,0:T(8,128)(2,1)}, u32[]{:S(2)}, u32[]{:S(2)}) collective-permute-start(bf16[512,768]{1,0:T(8,128)(2,1)S(1)} %bitcast.32), channel_id=1, source_target_pairs={{8,0},{10,2},{12,4},{14,6},{16,8},{18,10},{20,12},{22,14},{24,16},... | collective-permute-start | bytes 2359304 | tf_op jit(solution)/shard_map/ppermute | solution.py:26
  46.3 25.5 %copy-start.3 = (s32[1,16]{1,0:T(1,128)S(1)}, s32[1,16]{1,0:T(1,128)}, u32[]{:S(2)}) copy-start(s32[1,16]{1,0:T(1,128)} %valid_ref.3) | copy-start | bytes 196
  46.3 27.7 %collective-permute-start.2 = (bf16[384,768]{1,0:T(8,128)(2,1)}, bf16[384,768]{1,0:T(8,128)(2,1)}, u32[]{:S(2)}, u32[]{:S(2)}) collective-permute-start(bf16[384,768]{1,0:T(8,128)(2,1)} %slice.20), channel_id=1, source_target_pairs={{0,8},{2,10},{4,12},{6,14},{8,16},{10,18},{12,20},{14,22},{16,24},... | collective-permute-start | bytes 1769480 | tf_op jit(solution)/shard_map/ppermute | solution.py:26
  53.8 25.5 %collective-permute-start.3 = (bf16[384,768]{1,0:T(8,128)(2,1)}, bf16[384,768]{1,0:T(8,128)(2,1)}, u32[]{:S(2)}, u32[]{:S(2)}) collective-permute-start(bf16[384,768]{1,0:T(8,128)(2,1)} %slice.21), channel_id=1, source_target_pairs={{8,0},{10,2},{12,4},{14,6},{16,8},{18,10},{20,12},{22,14},{24,16},... | collective-permute-start | bytes 1769480 | tf_op jit(solution)/shard_map/ppermute | solution.py:26
  63.2 24.7 %collective-permute-start.9 = (bf16[384,768]{1,0:T(8,128)(2,1)}, bf16[384,768]{1,0:T(8,128)(2,1)}, u32[]{:S(2)}, u32[]{:S(2)}) collective-permute-start(bf16[384,768]{1,0:T(8,128)(2,1)} %slice.22), channel_id=1, source_target_pairs={{0,8},{2,10},{4,12},{6,14},{8,16},{10,18},{12,20},{14,22},{16,24},... | collective-permute-start | bytes 1769480 | tf_op jit(solution)/shard_map/ppermute | solution.py:26
  70.5 20.7 %collective-permute-start.10 = (bf16[384,768]{1,0:T(8,128)(2,1)}, bf16[384,768]{1,0:T(8,128)(2,1)}, u32[]{:S(2)}, u32[]{:S(2)}) collective-permute-start(bf16[384,768]{1,0:T(8,128)(2,1)} %slice.23), channel_id=1, source_target_pairs={{8,0},{10,2},{12,4},{14,6},{16,8},{18,10},{20,12},{22,14},{24,16},... | collective-permute-start | bytes 1769480 | tf_op jit(solution)/shard_map/ppermute | solution.py:26
  71.8 19.3 %copy-start.2 = (s32[2]{0:T(128)}, s32[2]{0:T(128)S(1)}, u32[]{:S(2)}) copy-start(s32[2]{0:T(128)S(1)} %pad_add_fusion.place_ref) | copy-start | bytes 28
  87.3 0.7 copy-start
  87.9 21.8 %collective-permute-start.4 = (bf16[128,384]{1,0:T(8,128)(2,1)S(1)}, bf16[128,384]{1,0:T(8,128)(2,1)S(1)}, u32[]{:S(2)}, u32[]{:S(2)}) collective-permute-start(bf16[128,384]{1,0:T(8,128)(2,1)S(1)} %get-tuple-element.13), channel_id=1, source_target_pairs={{0,2},{2,0},{4,6},{6,4},{8,10},{10,8},{12,14},{14,12},{16,18},{18,... | collective-permute-start | bytes 294920 | tf_op jit(solution)/shard_map/ppermute | solution.py:257
  99.1 0.6 copy-start.1
  101.6 11.3 %all-to-all-start.3 = ((f32[32,1,128]{2,1,0:T(1,128)}), f32[32,1,128]{2,1,0:T(1,128)S(1)}, u32[]{:S(2)}, u32[]{:S(2)}) async-start(f32[32,1,128]{2,1,0:T(1,128)} %broadcast_in_dim.45), calls=%async_computation.3 | async-start | bytes 32768 | tf_op jit(solution)/shard_map/all_to_all | solution.py:263
  105.7 7.8 %collective-permute-start.5 = (bf16[128,384]{1,0:T(8,128)(2,1)S(1)}, bf16[128,384]{1,0:T(8,128)(2,1)S(1)}, u32[]{:S(2)}, u32[]{:S(2)}) collective-permute-start(bf16[128,384]{1,0:T(8,128)(2,1)S(1)} %get-tuple-element.14), channel_id=1, source_target_pairs={{0,4},{2,6},{4,0},{6,2},{8,12},{10,14},{12,8},{14,10},{16,20},{18,... | collective-permute-start | bytes 294920 | tf_op jit(solution)/shard_map/ppermute | solution.py:257
  107.6 5.9 %collective-permute-start.6 = (bf16[128,384]{1,0:T(8,128)(2,1)S(1)}, bf16[128,384]{1,0:T(8,128)(2,1)S(1)}, u32[]{:S(2)}, u32[]{:S(2)}) collective-permute-start(bf16[128,384]{1,0:T(8,128)(2,1)S(1)} %get-tuple-element.15), channel_id=1, source_target_pairs={{0,6},{2,4},{4,2},{6,0},{8,14},{10,12},{12,10},{14,8},{16,22},{18,... | collective-permute-start | bytes 294920 | tf_op jit(solution)/shard_map/ppermute | solution.py:257
  107.6 5.9 %collective-permute-start.11 = (bf16[128,384]{1,0:T(8,128)(2,1)S(1)}, bf16[128,384]{1,0:T(8,128)(2,1)S(1)}, u32[]{:S(2)}, u32[]{:S(2)}) collective-permute-start(bf16[128,384]{1,0:T(8,128)(2,1)S(1)} %get-tuple-element.17), channel_id=1, source_target_pairs={{0,2},{2,0},{4,6},{6,4},{8,10},{10,8},{12,14},{14,12},{16,18},{18,... | collective-permute-start | bytes 294920 | tf_op jit(solution)/shard_map/ppermute | solution.py:257
  107.9 7.5 %collective-permute-start.12 = (bf16[128,384]{1,0:T(8,128)(2,1)S(1)}, bf16[128,384]{1,0:T(8,128)(2,1)S(1)}, u32[]{:S(2)}, u32[]{:S(2)}) collective-permute-start(bf16[128,384]{1,0:T(8,128)(2,1)S(1)} %get-tuple-element.18), channel_id=1, source_target_pairs={{0,4},{2,6},{4,0},{6,2},{8,12},{10,14},{12,8},{14,10},{16,20},{18,... | collective-permute-start | bytes 294920 | tf_op jit(solution)/shard_map/ppermute | solution.py:257
  109.7 7.2 %copy-start.5 = (bf16[128,384]{1,0:T(8,128)(2,1)}, bf16[128,384]{1,0:T(8,128)(2,1)S(1)}, u32[]{:S(2)}) copy-start(bf16[128,384]{1,0:T(8,128)(2,1)S(1)} %collective-permute-done.4.refs_1_) | copy-start | bytes 294916
  109.7 7.2 %collective-permute-start.13 = (bf16[128,384]{1,0:T(8,128)(2,1)S(1)}, bf16[128,384]{1,0:T(8,128)(2,1)S(1)}, u32[]{:S(2)}, u32[]{:S(2)}) collective-permute-start(bf16[128,384]{1,0:T(8,128)(2,1)S(1)} %get-tuple-element.19), channel_id=1, source_target_pairs={{0,6},{2,4},{4,2},{6,0},{8,14},{10,12},{12,10},{14,8},{16,22},{18,... | collective-permute-start | bytes 294920 | tf_op jit(solution)/shard_map/ppermute | solution.py:257
  113.5 3.4 %copy-start.6 = (bf16[128,384]{1,0:T(8,128)(2,1)}, bf16[128,384]{1,0:T(8,128)(2,1)S(1)}, u32[]{:S(2)}) copy-start(bf16[128,384]{1,0:T(8,128)(2,1)S(1)} %collective-permute-done.5.refs_2_) | copy-start | bytes 294916
  113.5 3.4 %copy-start.7 = (bf16[128,384]{1,0:T(8,128)(2,1)}, bf16[128,384]{1,0:T(8,128)(2,1)S(1)}, u32[]{:S(2)}) copy-start(bf16[128,384]{1,0:T(8,128)(2,1)S(1)} %collective-permute-done.6.refs_3_) | copy-start | bytes 294916
  113.5 3.4 %copy-start.8 = (bf16[128,384]{1,0:T(8,128)(2,1)}, bf16[128,384]{1,0:T(8,128)(2,1)S(1)}, u32[]{:S(2)}) copy-start(bf16[128,384]{1,0:T(8,128)(2,1)S(1)} %collective-permute-done.11.refs_5_) | copy-start | bytes 294916
  115.4 1.6 %copy-start.9 = (bf16[128,384]{1,0:T(8,128)(2,1)}, bf16[128,384]{1,0:T(8,128)(2,1)S(1)}, u32[]{:S(2)}) copy-start(bf16[128,384]{1,0:T(8,128)(2,1)S(1)} %collective-permute-done.12.refs_6_) | copy-start | bytes 294916
  116.9 0.6 copy-start.10

commit v4 on v3

v4 whole, which is shorter than its diff:
```python
import functools
import math

import jax
import jax.numpy as jnp
from jax import lax
from jax.experimental import pallas as pl
from jax.experimental.pallas import tpu as pltpu
from jax.sharding import PartitionSpec as P


HEAD = 128
BLK = 128
MAXB = 8
GROUPS = 4
LEVEL = MAXB // 2
REACH = MAXB - 1
CHUNKS = (1, 1, 1)


masked_score = -1e30


def level_swap(value, axis, odd):
    count = lax.axis_size(axis)
    partners = [
        (source, ((source // LEVEL + odd) ^ 1) * LEVEL - odd * LEVEL + source % LEVEL)
        for source in range(count)
    ]
    return lax.ppermute(value, axis, [pair for pair in partners if 0 <= pair[1] < count])


def advantages(reward_row, group_row):
    member = (group_row[:, None] == jnp.arange(GROUPS, dtype=jnp.int32)[None, :]).astype(
        jnp.float32
    )
    totals = jnp.sum(member * reward_row[:, None], axis=0)
    counts = jnp.sum(member, axis=0)
    means = totals / jnp.maximum(counts, 1.0)
    return reward_row - jnp.sum(member * means[None, :], axis=1)


def moved(copies):
    for copy in copies:
        copy.start()
    for copy in copies:
        copy.wait()


def pack_body(spans, place_ref, first_ref, second_ref, *refs):
    out_refs, sems = refs[:-1], refs[-1]
    share = first_ref.shape[2] // LEVEL
    copies = []
    for index, out_ref in enumerate(out_refs):
        low, high = spans[index // LEVEL]
        span = high - low
        first = jnp.bitwise_xor(place_ref[1], index % LEVEL) * share + low
        for side, ref in enumerate((first_ref, second_ref)):
            copies.append(
                pltpu.make_async_copy(
                    ref.at[0, :, pl.ds(pl.multiple_of(first, HEAD), span)],
                    out_ref.at[:, pl.ds(side * span, span)],
                    sems.at[len(copies)],
                )
            )
    moved(copies)


def packed(place, first, second, spans):
    hbm = pl.BlockSpec(memory_space=pl.ANY)
    shapes = [
        jax.ShapeDtypeStruct((first.shape[1], 2 * (high - low)), first.dtype)
        for low, high in spans
        for _ in range(LEVEL)
    ]
    found = pl.pallas_call(
        functools.partial(pack_body, spans),
        out_shape=shapes,
        in_specs=[pl.BlockSpec(memory_space=pltpu.SMEM), hbm, hbm],
        out_specs=[pl.BlockSpec(memory_space=pltpu.VMEM)] * len(shapes),
        scratch_shapes=[pltpu.SemaphoreType.DMA((2 * len(shapes),))],
    )(place, first, second)
    return [found[first : first + LEVEL] for first in range(0, len(shapes), LEVEL)]


def join_body(place_ref, *refs):
    for step, ref in enumerate(refs[:-1]):
        first = jnp.bitwise_xor(place_ref[1], step) * BLK
        refs[-1][pl.ds(pl.multiple_of(first, BLK), BLK), :] = ref[...]


def joined(place, parts):
    vmem = pl.BlockSpec(memory_space=pltpu.VMEM)
    rows, width = parts[0].shape
    return pl.pallas_call(
        join_body,
        out_shape=jax.ShapeDtypeStruct((len(parts) * rows, width), parts[0].dtype),
        in_specs=[pl.BlockSpec(memory_space=pltpu.SMEM)] + [vmem] * len(parts),
        out_specs=vmem,
    )(place, *parts)


def unpack_body(spans, place_ref, *refs):
    parts, out_ref = refs[:-1], refs[-1]
    share = out_ref.shape[2] // LEVEL
    for index, (low, high) in enumerate(spans):
        for step in range(LEVEL):
            first = pl.multiple_of(jnp.bitwise_xor(place_ref[1], step) * share + low, HEAD)
            out_ref[0, :, pl.ds(first, high - low)] = parts[index * LEVEL + step][...]


def unpacked(place, outs, spans, width):
    vmem = pl.BlockSpec(memory_space=pltpu.VMEM)
    return pl.pallas_call(
        functools.partial(unpack_body, spans),
        out_shape=jax.ShapeDtypeStruct((1, outs[0].shape[0], width), outs[0].dtype),
        in_specs=[pl.BlockSpec(memory_space=pltpu.SMEM)] + [vmem] * len(outs),
        out_specs=vmem,
        name="unpack",
    )(place, *outs)


def kernel_body(heads, first_head, earlier, place_ref, clip_ref, valid_ref, weight_ref, *refs):
    earlier, refs = refs[:earlier], refs[earlier:]
    width = heads * HEAD
    qn_ref, kv_parts = refs[0], refs[1:6]
    out_refs = refs[6 : 6 + LEVEL]
    err_ref, kv_buf = refs[6 + LEVEL :]
    half = qn_ref.shape[1] // 2
    level_first, own, odd = place_ref[0], place_ref[1], place_ref[2]
    sides = (REACH + LEVEL, REACH - LEVEL)
    ends = (REACH + 2 * LEVEL, 0)
    firsts = [
        jnp.int32(REACH),
        jnp.where(odd == 0, *sides),
        jnp.where(odd == 1, *sides),
        jnp.where(odd == 0, *ends),
        jnp.where(odd == 1, *ends),
    ]
    err = jnp.zeros((8, HEAD), jnp.float32)
    for ref in earlier:
        err = err + ref[...]
    factor = math.log2(math.e) / math.sqrt(HEAD)
    last_block = valid_ref.shape[1] - 1
    slots = lax.broadcasted_iota(jnp.int32, (1, BLK), 1)
    blocks = []
    for step in range(LEVEL):
        block = jnp.bitwise_xor(own, step)
        own_id = level_first + block
        clip_start = clip_count = clip_first = jnp.int32(0)
        for clip in range(clip_ref.shape[1]):
            count = clip_ref[0, clip]
            mine = (own_id >= clip_first) & (own_id < clip_first + count)
            clip_start = jnp.where(mine, clip_first, clip_start)
            clip_count = jnp.where(mine, count, clip_count)
            clip_first = clip_first + count
        bias = []
        for near in range(MAXB):
            live = valid_ref[0, jnp.minimum(clip_start + near, last_block)]
            live = jnp.where(near < clip_count, live, 0)
            bias.append(jnp.where(slots < live, 0.0, masked_score).astype(jnp.float32))
        window_first = clip_start - (level_first - REACH)
        blocks.append(
            (
                pl.ds(pl.multiple_of(block * BLK, BLK), BLK),
                pl.ds(pl.multiple_of(window_first * BLK, BLK), MAXB * BLK),
                jnp.concatenate(bias, axis=1),
                valid_ref[0, own_id],
                weight_ref[block],
            )
        )
    for head in range(heads):
        columns = slice(head * HEAD, (head + 1) * HEAD)
        other = slice(width + head * HEAD, width + (head + 1) * HEAD)
        own_columns = slice((first_head + head) * HEAD, (first_head + head + 1) * HEAD)
        own_other = slice(half + own_columns.start, half + own_columns.stop)
        for ref, first in zip(kv_parts, firsts):
            rows = pl.ds(pl.multiple_of(first * BLK, BLK), ref.shape[0])
            kv_buf[rows, columns] = ref[:, columns]
            kv_buf[rows, other] = ref[:, other]
        for step, (rows, window, bias, live, weight) in enumerate(blocks):
            scores = lax.dot_general(
                qn_ref[rows, own_columns],
                kv_buf[window, columns],
                (((1,), (1,)), ((), ())),
                preferred_element_type=jnp.float32,
            )
            scores = scores + bias
            top = jnp.max(scores, axis=-1, keepdims=True)
            expo = jnp.exp2((scores - top) * factor)
            probs = (expo * (1.0 / jnp.sum(expo, axis=-1, keepdims=True))).astype(jnp.bfloat16)
            mixed = lax.dot_general(
                probs,
                kv_buf[window, other],
                (((1,), (0,)), ((), ())),
                preferred_element_type=jnp.float32,
            )
            own_live = lax.broadcasted_iota(jnp.int32, (BLK, HEAD), 0) < live
            result = jnp.where(own_live, mixed, 0.0).astype(jnp.bfloat16)
            out_refs[step][:, columns] = result
            diff = qn_ref[rows, own_other].astype(jnp.float32) - result.astype(jnp.float32)
            block_err = jnp.where(own_live, diff * diff, 0.0)
            err = err + weight * jnp.sum(block_err.reshape(BLK // 8, 8, HEAD), axis=0)
    if err_ref.shape[0] != err.shape[0]:
        err = jnp.broadcast_to(jnp.sum(err, keepdims=True), err_ref.shape)
    err_ref[...] = err


def attend(first_head, tables, earlier, spread, qn, kv_parts):
    width = kv_parts[0].shape[1] // 2
    heads = width // HEAD
    total = sum(part.shape[0] for part in kv_parts)
    smem = pl.BlockSpec(memory_space=pltpu.SMEM)
    vmem = pl.BlockSpec(memory_space=pltpu.VMEM)
    units = LEVEL * heads
    return pl.pallas_call(
        functools.partial(kernel_body, heads, first_head, len(earlier)),
        out_shape=[jax.ShapeDtypeStruct((BLK, width), jnp.bfloat16)] * LEVEL
        + [jax.ShapeDtypeStruct((spread, HEAD), jnp.float32)],
        in_specs=[smem] * len(tables) + [vmem] * (len(earlier) + 1 + len(kv_parts)),
        out_specs=[vmem] * (LEVEL + 1),
        scratch_shapes=[
            pltpu.VMEM((total, 2 * width), jnp.bfloat16),
        ],
        cost_estimate=pl.CostEstimate(
            flops=units * 4 * BLK * MAXB * BLK * HEAD,
            transcendentals=units * BLK * MAXB * BLK,
            bytes_accessed=4 * (total + 2 * qn.shape[0]) * width,
        ),
        compiler_params=pltpu.CompilerParams(vmem_limit_bytes=24 * 1024 * 1024),
    )(*tables, *earlier, qn, *kv_parts)


def step(queries, keys, values, next_latent, clip_blocks, valid_counts, group_ids, rewards):
    devices = lax.axis_size("tok")
    own_index = lax.axis_index("tok")
    _, width = queries.shape[1:]
    share = width // LEVEL
    heads = share // HEAD
    cuts = [0]
    for part in CHUNKS:
        cuts.append(cuts[-1] + heads * part // sum(CHUNKS))
    spans = [(low * HEAD, high * HEAD) for low, high in zip(cuts[:-1], cuts[1:])]

    def swapped(parts):
        found = [parts[0]]
        for step in range(1, LEVEL):
            partners = [(source, source ^ step) for source in range(devices)]
            found.append(lax.ppermute(parts[step], "tok", partners))
        return found

    level = own_index // LEVEL
    level_first = level * LEVEL
    odd = level % 2
    place = jnp.stack([level_first, own_index - level_first, odd])

    def gathered(own):
        reached = (REACH - LEVEL) * BLK
        upper = LEVEL * BLK - reached
        first = [level_swap(own, "tok", side) for side in (0, 1)]
        starts = (jnp.where(odd == 0, upper, 0), jnp.where(odd == 1, upper, 0))
        second = [
            level_swap(lax.dynamic_slice_in_dim(value, start, reached, 0), "tok", side)
            for side, (value, start) in enumerate(zip(first[::-1], starts))
        ]
        return [own, *first, *second]

    own_kv = []
    packs = packed(place, keys, values, spans[:1])
    packs += packed(place, keys, values, spans[1:])
    for parts in packs:
        parts = swapped(parts)
        own_kv.append(joined(place, parts))
    (parts,) = packed(place, queries, next_latent, [(0, share)])
    parts = swapped(parts)
    qn = joined(place, parts)

    valid_row = valid_counts[0]
    clip_row = clip_blocks[0]
    ends = jnp.cumsum(clip_row)
    starts = ends - clip_row
    positions = jnp.arange(valid_row.shape[0], dtype=jnp.int32)
    member = (starts[None, :] <= positions[:, None]) & (positions[:, None] < ends[None, :])
    tokens_of = jnp.sum(jnp.where(member, valid_row[:, None], 0), axis=0).astype(jnp.float32)
    clip_weight = advantages(rewards[0], group_ids[0]) / (2.0 * width * tokens_of)
    own_ids = level_first + jnp.arange(LEVEL, dtype=jnp.int32)
    own_member = (starts[None, :] <= own_ids[:, None]) & (own_ids[:, None] < ends[None, :])
    own_weight = jnp.sum(jnp.where(own_member, clip_weight[None, :], 0.0), axis=1)
    tables = (place, clip_blocks, valid_counts, own_weight)

    everyone = devices * lax.axis_size("grp")
    outs, errs = [], []
    for index, ((low, high), own) in enumerate(zip(spans, own_kv)):
        found = gathered(own)
        *out, err = attend(
            low // HEAD, tables, errs[-1:], everyone if index == len(spans) - 1 else 8, qn, found
        )
        outs += swapped(out)
        errs.append(err)
    velocity = unpacked(place, outs, spans, width)
    total = jnp.sum(lax.all_to_all(errs[-1], ("tok", "grp"), 0, 0, tiled=True)[:, 0])
    return (velocity, total)


def solution(mesh):
    return jax.shard_map(
        step,
        mesh=mesh,
        in_specs=(
            P("grp", "tok", None),
            P("grp", "tok", None),
            P("grp", "tok", None),
            P("grp", "tok", None),
            P("grp", None),
            P("grp", None),
            P("grp", None),
            P("grp", None),
        ),
        out_specs=(P("grp", "tok", None), P()),
        check_vma=False,
    )
```

time: 121 us -> 119 us (0.983)
  waiting for transfers between devices: 35 us -> 8.17 us
  starting transfers between devices: 45.4 us -> 58.4 us
  Pallas kernels: 25.4 us -> 36.8 us
    ppermute x14 -> x33, starting transfers between devices: 30 us -> 52 us  [the longest x12 36.7 us: level_swap(): lax.ppermute(value, axis, [pair for pair in partners if 0 <= pair[1] < co...]
    ppermute x14 -> x33, waiting for transfers between devices: 20.2 us -> 4.94 us  [the longest x21 2.47 us: swapped(): found.append(lax.ppermute(parts[step], 'tok', partners))]
    all_to_all x4 -> x1, waiting for transfers between devices: 14.8 us -> 3.23 us  [step(): lax.all_to_all(errs[-1], ('tok', 'grp'), 0, 0, tiled=True)[:, 0]]
    pallas_call x5 -> x10, Pallas kernels: 23.2 us -> 34.7 us  [the longest x3 17 us: attend(): pl.pallas_call(functools.partial(kernel_body, heads, first_head, len(earl...]
    all_to_all x4 -> x1, starting transfers between devices: 15.4 us -> 6.4 us  [step(): lax.all_to_all(errs[-1], ('tok', 'grp'), 0, 0, tiled=True)[:, 0]]
    slice x4 -> x0, local copies, waits for them, and re-layouts: 7.78 us -> none  [the longest x2 3.95 us: gathered(): downward = passed_along(downward[:count * BLK], 'tok', -LEVEL)]
    unnamed x26 -> x88, local copies, waits for them, and re-layouts: 1.93 us -> 7.43 us
    dynamic_slice x0 -> x6, local copies, waits for them, and re-layouts: none -> 3.89 us  [gathered(): lax.dynamic_slice_in_dim(value, start, reached, 0)]
  transfers between devices with their start and end apart: 18 -> 34, of which waited for: 10 -> 4; matrix products, arithmetic and copies ran while one was open for 9% -> 5% of each run, Pallas kernels for 17% -> 27%
where the time goes in v4:
time: 119 us; the launch traced here: 118 us
  starting transfers between devices  58.4 us (49%)
  Pallas kernels  36.8 us (31%)
  local copies, waits for them, and re-layouts  11.3 us (9%)
  waiting for transfers between devices  8.17 us (7%)
  other arithmetic  2.52 us (2%)
    ppermute x12, starting transfers between devices, level_swap(): lax.ppermute(value, axis, [pair for pair in partners if 0 <= pair[1] < co...  36.7 us
    pallas_call x3, Pallas kernels, attend(): pl.pallas_call(functools.partial(kernel_body, heads, first_head, len(earl...  17 us
    ppermute x21, starting transfers between devices, swapped(): found.append(lax.ppermute(parts[step], 'tok', partners))  15.4 us
    pallas_call x3, Pallas kernels, packed(): pl.pallas_call(functools.partial(pack_body, spans), out_shape=shapes, in_...  9.16 us
    pallas_call x4, Pallas kernels, joined(): pl.pallas_call(join_body, out_shape=jax.ShapeDtypeStruct((len(parts) * ro...  8.52 us
    unnamed x88, local copies, waits for them, and re-layouts  7.43 us
    all_to_all x1, starting transfers between devices, step(): lax.all_to_all(errs[-1], ('tok', 'grp'), 0, 0, tiled=True)[:, 0]  6.4 us
    dynamic_slice x6, local copies, waits for them, and re-layouts, gathered(): lax.dynamic_slice_in_dim(value, start, reached, 0)  3.89 us
  transfers between devices with their start and end apart: 34, of which 4 were waited for; matrix products, arithmetic and copies ran while one was open for 5% of the time, Pallas kernels for 27%

profile of v4, /device:TPU:0, one launch (start us, length us, event | category | flops | bytes accessed | tf_op | source)
XLA Modules:
  0.0 118.4 jit_solution(5393549662365904200)
XLA Ops:
  1.2 2.7 %shard_map.97 = (bf16[128,512]{1,0:T(8,128)(2,1)}, bf16[128,512]{1,0:T(8,128)(2,1)}, bf16[128,512]{1,0:T(8,128)(2,1)}, bf16[128,512]{1,0:T(8,128)(2,1)}) custom-call(s32[3]{0:T(128)} %pad_add_fusion.place_ref, bf16[1,128,3072]{2,1,0:T(8,128)(2,1)} %first_ref.5, bf16[1,128,3072]{2,1,0:T(8,128)(2,1)} %second_ref.5), custom_call_target="tpu_custom_call" | custom-call | tf_op jit(solution)/shard_map/pallas_call | solution.py:76
  4.5 2.6 %collective-permute-start.4 = (bf16[128,512]{1,0:T(8,128)(2,1)}, bf16[128,512]{1,0:T(8,128)(2,1)S(1)}, u32[]{:S(2)}, u32[]{:S(2)}) collective-permute-start(bf16[128,512]{1,0:T(8,128)(2,1)} %get-tuple-element.39), channel_id=1, source_target_pairs={{0,4},{2,6},{4,0},{6,2},{8,12},{10,14},{12,8},{14,10},{16,20},{18,... | collective-permute-start | bytes 393224 | tf_op jit(solution)/shard_map/ppermute | solution.py:249
  7.1 3.1 %shard_map.100 = (bf16[128,512]{1,0:T(8,128)(2,1)}, bf16[128,512]{1,0:T(8,128)(2,1)}, bf16[128,512]{1,0:T(8,128)(2,1)}, bf16[128,512]{1,0:T(8,128)(2,1)}, bf16[1...) custom-call(s32[3]{0:T(128)} %pad_add_fusion.place_ref, ...), custom_call_target="tpu_custom_call" | custom-call | tf_op jit(solution)/shard_map/pallas_call | solution.py:76
  10.4 1.9 %collective-permute-start.14 = (bf16[128,512]{1,0:T(8,128)(2,1)}, bf16[128,512]{1,0:T(8,128)(2,1)S(1)}, u32[]{:S(2)}, u32[]{:S(2)}) collective-permute-start(bf16[128,512]{1,0:T(8,128)(2,1)} %get-tuple-element.48), channel_id=1, source_target_pairs={{0,4},{2,6},{4,0},{6,2},{8,12},{10,14},{12,8},{14,10},{16,20},{18,... | collective-permute-start | bytes 393224 | tf_op jit(solution)/shard_map/ppermute | solution.py:249
  12.9 1.2 %collective-permute-done.5.refs_3_ = bf16[128,512]{1,0:T(8,128)(2,1)S(1)} collective-permute-done((bf16[128,512]{1,0:T(8,128)(2,1)}, bf16[128,512]{1,0:T(8,128)(2,1)S(1)}, u32[]{:S(2)}, u32[]{:S(2)}) %collective-permute-start.5) | collective-permute-done | bytes 131104 | tf_op jit(solution)/shard_map/ppermute | solution.py:249
  14.1 1.3 %collective-permute-start.24 = (bf16[128,512]{1,0:T(8,128)(2,1)}, bf16[128,512]{1,0:T(8,128)(2,1)S(1)}, u32[]{:S(2)}, u32[]{:S(2)}) collective-permute-start(bf16[128,512]{1,0:T(8,128)(2,1)} %get-tuple-element.57), channel_id=1, source_target_pairs={{0,4},{2,6},{4,0},{6,2},{8,12},{10,14},{12,8},{14,10},{16,20},{18,... | collective-permute-start | bytes 393224 | tf_op jit(solution)/shard_map/ppermute | solution.py:249
  15.4 1.9 %shard_map.98.refs_1_ = bf16[512,512]{1,0:T(8,128)(2,1)} custom-call(s32[3]{0:T(128)} %pad_add_fusion.place_ref, bf16[128,512]{1,0:T(8,128)(2,1)} %get-tuple-element.37.refs_0_, bf16[128,512]{1,0:T(8,128)(2,1)} %copy-done.23, bf16[128,512]{1,0:T(8,128)(2,1)} %copy-done.24, bf16[128,512]{1,0:T(8,128)(2,1)} %copy-done.26), custom_call_target="tpu_custom_call" | custom-call | tf_op jit(solution)/shard_map/pallas_call | solution.py:95
  17.3 1.1 collective-permute-start.25
  18.5 1.6 %collective-permute-start.6 = (bf16[512,512]{1,0:T(8,128)(2,1)}, bf16[512,512]{1,0:T(8,128)(2,1)S(1)}, u32[]{:S(2)}, u32[]{:S(2)}) collective-permute-start(bf16[512,512]{1,0:T(8,128)(2,1)} %shard_map.98.refs_1_), channel_id=1, source_target_pairs={{0,8},{2,10},{4,12},{6,14},{8,0},{10,2},{12,4},{14,6},{16,24},{18,... | collective-permute-start | bytes 1572872 | tf_op jit(solution)/shard_map/ppermute | solution.py:30
  20.1 0.7 collective-permute-start.7
  20.8 1.9 %shard_map.101.refs_2_ = bf16[512,512]{1,0:T(8,128)(2,1)} custom-call(s32[3]{0:T(128)} %pad_add_fusion.place_ref, bf16[128,512]{1,0:T(8,128)(2,1)} %get-tuple-element.46.refs_0_, bf16[128,512]{1,0:T(8,128)(2,1)} %copy-done.20, bf16[128,512]{1,0:T(8,128)(2,1)} %copy-done.22, bf16[128,512]{1,0:T(8,128)(2,1)} %copy-done.25), custom_call_target="tpu_custom_call" | custom-call | tf_op jit(solution)/shard_map/pallas_call | solution.py:95
  22.7 0.7 collective-permute-start.17
  23.5 5.7 %collective-permute-start.16 = (bf16[512,512]{1,0:T(8,128)(2,1)}, bf16[512,512]{1,0:T(8,128)(2,1)S(1)}, u32[]{:S(2)}, u32[]{:S(2)}) collective-permute-start(bf16[512,512]{1,0:T(8,128)(2,1)} %shard_map.101.refs_2_), channel_id=1, source_target_pairs={{0,8},{2,10},{4,12},{6,14},{8,0},{10,2},{12,4},{14,6},{16,24},{18,... | collective-permute-start | bytes 1572872 | tf_op jit(solution)/shard_map/ppermute | solution.py:30
  29.2 0.6 copy-done.27
  29.9 1.9 %shard_map.103.refs_2_ = bf16[512,512]{1,0:T(8,128)(2,1)} custom-call(s32[3]{0:T(128)} %pad_add_fusion.place_ref, bf16[128,512]{1,0:T(8,128)(2,1)} %get-tuple-element.55.refs_0_, bf16[128,512]{1,0:T(8,128)(2,1)} %copy-done.19, bf16[128,512]{1,0:T(8,128)(2,1)} %copy-done.21, bf16[128,512]{1,0:T(8,128)(2,1)} %copy-done.27), custom_call_target="tpu_custom_call" | custom-call | tf_op jit(solution)/shard_map/pallas_call | solution.py:95
  31.8 0.8 collective-permute-start.27
  33.2 3.4 %shard_map.95 = (bf16[128,1536]{1,0:T(8,128)(2,1)}, bf16[128,1536]{1,0:T(8,128)(2,1)}, bf16[128,1536]{1,0:T(8,128)(2,1)}, bf16[128,1536]{1,0:T(8,128)(2,1)}) custom-call(s32[3]{0:T(128)} %pad_add_fusion.place_ref, bf16[1,128,3072]{2,1,0:T(8,128)(2,1)} %first_ref.3, bf16[1,128,3072]{2,1,0:T(8,128)(2,1)} %second_ref.3), custom_call_target="tpu_custom_call" | custom-call | tf_op jit(solution)/shard_map/pallas_call | solution.py:76
  37.0 3.2 %collective-permute-start.26 = (bf16[512,512]{1,0:T(8,128)(2,1)S(1)}, bf16[512,512]{1,0:T(8,128)(2,1)S(1)}, u32[]{:S(2)}, u32[]{:S(2)}) collective-permute-start(bf16[512,512]{1,0:T(8,128)(2,1)S(1)} %copy-done.3), channel_id=1, source_target_pairs={{0,8},{2,10},{4,12},{6,14},{8,0},{10,2},{12,4},{14,6},{16,24},{18,... | collective-permute-start | bytes 1572872 | tf_op jit(solution)/shard_map/ppermute | solution.py:30
  40.3 1.2 collective-permute-start.1
  41.5 0.8 constant_dynamic-slice_fusion.3
  42.3 2.4 %collective-permute-done.16.refs_3_ = bf16[512,512]{1,0:T(8,128)(2,1)S(1)} collective-permute-done((bf16[512,512]{1,0:T(8,128)(2,1)}, bf16[512,512]{1,0:T(8,128)(2,1)S(1)}, u32[]{:S(2)}, u32[]{:S(2)}) %collective-permute-start.16) | collective-permute-done | bytes 524320 | tf_op jit(solution)/shard_map/ppermute | solution.py:30
  44.8 15.5 %collective-permute-start.8 = (bf16[384,512]{1,0:T(8,128)(2,1)S(1)}, bf16[384,512]{1,0:T(8,128)(2,1)S(1)}, u32[]{:S(2)}, u32[]{:S(2)}) collective-permute-start(bf16[384,512]{1,0:T(8,128)(2,1)S(1)} %constant_dynamic-slice_fusion.5), channel_id=1, source_target_pairs={{0,8},{2,10},{4,12},{6,14},{8,0},{10,2},{12,4},{14,6},{16,24},{18,... | collective-permute-start | bytes 1179656 | tf_op jit(solution)/shard_map/ppermute | solution.py:30
  60.4 0.8 constant_dynamic-slice_fusion.4
  61.1 0.8 constant_dynamic-slice_fusion.2
  61.9 0.8 constant_dynamic-slice_fusion.1
  62.7 1.4 %collective-permute-start.9 = (bf16[384,512]{1,0:T(8,128)(2,1)}, bf16[384,512]{1,0:T(8,128)(2,1)}, u32[]{:S(2)}, u32[]{:S(2)}) collective-permute-start(bf16[384,512]{1,0:T(8,128)(2,1)} %constant_dynamic-slice_fusion.4), channel_id=1, source_target_pairs={{8,16},{10,18},{12,20},{14,22},{16,8},{18,10},{20,12},{22,14},{9,1... | collective-permute-start | bytes 1179656 | tf_op jit(solution)/shard_map/ppermute | solution.py:30
  64.1 2.2 %collective-permute-start.18 = (bf16[384,512]{1,0:T(8,128)(2,1)}, bf16[384,512]{1,0:T(8,128)(2,1)}, u32[]{:S(2)}, u32[]{:S(2)}) collective-permute-start(bf16[384,512]{1,0:T(8,128)(2,1)} %constant_dynamic-slice_fusion.3), channel_id=1, source_target_pairs={{0,8},{2,10},{4,12},{6,14},{8,0},{10,2},{12,4},{14,6},{16,24},{18,... | collective-permute-start | bytes 1179656 | tf_op jit(solution)/shard_map/ppermute | solution.py:30
  66.2 1.4 %collective-permute-start.19 = (bf16[384,512]{1,0:T(8,128)(2,1)}, bf16[384,512]{1,0:T(8,128)(2,1)}, u32[]{:S(2)}, u32[]{:S(2)}) collective-permute-start(bf16[384,512]{1,0:T(8,128)(2,1)} %constant_dynamic-slice_fusion.2), channel_id=1, source_target_pairs={{8,16},{10,18},{12,20},{14,22},{16,8},{18,10},{20,12},{22,14},{9,1... | collective-permute-start | bytes 1179656 | tf_op jit(solution)/shard_map/ppermute | solution.py:30
  67.7 0.8 constant_dynamic-slice_fusion
  68.5 2.0 %collective-permute-start.28 = (bf16[384,512]{1,0:T(8,128)(2,1)}, bf16[384,512]{1,0:T(8,128)(2,1)S(1)}, u32[]{:S(2)}, u32[]{:S(2)}) collective-permute-start(bf16[384,512]{1,0:T(8,128)(2,1)} %constant_dynamic-slice_fusion.1), channel_id=1, source_target_pairs={{0,8},{2,10},{4,12},{6,14},{8,0},{10,2},{12,4},{14,6},{16,24},{18,... | collective-permute-start | bytes 1179656 | tf_op jit(solution)/shard_map/ppermute | solution.py:30
  70.5 0.8 copy-done.8
  71.3 1.4 %collective-permute-start.29 = (bf16[384,512]{1,0:T(8,128)(2,1)}, bf16[384,512]{1,0:T(8,128)(2,1)}, u32[]{:S(2)}, u32[]{:S(2)}) collective-permute-start(bf16[384,512]{1,0:T(8,128)(2,1)} %constant_dynamic-slice_fusion), channel_id=1, source_target_pairs={{8,16},{10,18},{12,20},{14,22},{16,8},{18,10},{20,12},{22,14},{9,1... | collective-permute-start | bytes 1179656 | tf_op jit(solution)/shard_map/ppermute | solution.py:30
  72.9 2.7 %shard_map.96.refs_0_.refs_1_ = bf16[512,1536]{1,0:T(8,128)(2,1)} custom-call(s32[3]{0:T(128)} %pad_add_fusion.place_ref, bf16[128,1536]{1,0:T(8,128)(2,1)} %get-tuple-element.33.refs_0_, bf16[128,1536]{1,0:T(8,128)(2,1)} %copy-done.16, bf16[128,1536]{1,0:T(8,128)(2,1)} %copy-done.17, bf16[128,1536]{1,0:T(8,128)(2,1)} %copy-done.18), custom_call_target="tpu_custom_call" | custom-call | tf_op jit(solution)/shard_map/pallas_call | solution.py:95
  75.7 1.4 %copy-done = bf16[512,1536]{1,0:T(8,128)(2,1)S(1)} copy-done((bf16[512,1536]{1,0:T(8,128)(2,1)S(1)}, bf16[512,1536]{1,0:T(8,128)(2,1)}, u32[]{:S(2)}) %copy-start) | copy-done | bytes 1572888
  77.1 1.0 copy-done.5
  78.1 1.0 copy-done.9
  79.1 5.8 %shard_map.99 = (bf16[128,256]{1,0:T(8,128)(2,1)S(1)}, bf16[128,256]{1,0:T(8,128)(2,1)}, bf16[128,256]{1,0:T(8,128)(2,1)}, bf16[128,256]{1,0:T(8,128)(2,1)}, f32[8,128]{1,0:T(8,128)S(1)}) custom-call(s32[3]{0:T(128)S(1)} %copy-done.10, s32[1,4]{1,0:T(1,128)S(1)} %copy-done.15, s32[1,16]{1,0:T(1,128)S(1)} %copy-done.14, f32[4]{0:T(128)S(1)} %select_reduce_fusion.weight_ref, ...), custom_call_target="tpu_custom_call" | custom-call | flops 536870912 | bytes 3407872 | tf_op jit(solution)/shard_map/pallas_call | solution.py:216
  84.9 0.6 copy-done.11
  85.6 1.5 %collective-permute-start.11 = (bf16[128,256]{1,0:T(8,128)(2,1)}, bf16[128,256]{1,0:T(8,128)(2,1)S(1)}, u32[]{:S(2)}, u32[]{:S(2)}) collective-permute-start(bf16[128,256]{1,0:T(8,128)(2,1)} %get-tuple-element.43), channel_id=1, source_target_pairs={{0,4},{2,6},{4,0},{6,2},{8,12},{10,14},{12,8},{14,10},{16,20},{18,... | collective-permute-start | bytes 196616 | tf_op jit(solution)/shard_map/ppermute | solution.py:249
  87.4 5.3 %shard_map.102 = (bf16[128,256]{1,0:T(8,128)(2,1)S(1)}, bf16[128,256]{1,0:T(8,128)(2,1)S(1)}, bf16[128,256]{1,0:T(8,128)(2,1)S(1)}, bf16[128,256]{1,0:T(8,128)(2,1)S(1)}, f32[8,128]{1,0:T(8,128)S(1)}) custom-call(s32[3]{0:T(128)S(1)} %copy-done.10, s32[1,4]{1,0:T(1,128)S(1)} %copy-done.15, s32[1,16]{1,0:T(1,128)S(1)} %copy-done.14, ...), custom_call_target="tpu_custom_call" | custom-call | flops 536870912 | bytes 3407872 | tf_op jit(solution)/shard_map/pallas_call | solution.py:216
  93.7 5.9 %shard_map.104 = (bf16[128,256]{1,0:T(8,128)(2,1)S(1)}, bf16[128,256]{1,0:T(8,128)(2,1)S(1)}, bf16[128,256]{1,0:T(8,128)(2,1)S(1)}, bf16[128,256]{1,0:T(8,128)(2,1)S(1)}, f32[32,128]{1,0:T(8,128)}) custom-call(s32[3]{0:T(128)S(1)} %copy-done.10, s32[1,4]{1,0:T(1,128)S(1)} %copy-done.15, s32[1,16]{1,0:T(1,128)S(1)} %copy-done.14, ...), custom_call_target="tpu_custom_call" | custom-call | flops 536870912 | bytes 3407872 | tf_op jit(solution)/shard_map/pallas_call | solution.py:216
  99.5 0.6 copy-done.13
  100.2 6.4 %all-to-all-start = ((f32[32,1,128]{2,1,0:T(1,128)}), f32[32,1,128]{2,1,0:T(1,128)S(1)}, u32[]{:S(2)}, u32[]{:S(2)}) async-start(f32[32,1,128]{2,1,0:T(1,128)} %bitcast.14), calls=%async_computation | async-start | bytes 32768 | tf_op jit(solution)/shard_map/all_to_all | solution.py:301
  106.6 1.8 %collective-permute-start.21 = (bf16[128,256]{1,0:T(8,128)(2,1)S(1)}, bf16[128,256]{1,0:T(8,128)(2,1)S(1)}, u32[]{:S(2)}, u32[]{:S(2)}) collective-permute-start(bf16[128,256]{1,0:T(8,128)(2,1)S(1)} %get-tuple-element.52), channel_id=1, source_target_pairs={{0,4},{2,6},{4,0},{6,2},{8,12},{10,14},{12,8},{14,10},{16,20},{18,... | collective-permute-start | bytes 196616 | tf_op jit(solution)/shard_map/ppermute | solution.py:249
  108.8 1.8 %collective-permute-start.31 = (bf16[128,256]{1,0:T(8,128)(2,1)S(1)}, bf16[128,256]{1,0:T(8,128)(2,1)S(1)}, u32[]{:S(2)}, u32[]{:S(2)}) collective-permute-start(bf16[128,256]{1,0:T(8,128)(2,1)S(1)} %get-tuple-element.61), channel_id=1, source_target_pairs={{0,4},{2,6},{4,0},{6,2},{8,12},{10,14},{12,8},{14,10},{16,20},{18,... | collective-permute-start | bytes 196616 | tf_op jit(solution)/shard_map/ppermute | solution.py:249
  110.6 3.2 %all-to-all-done = f32[32,1,128]{2,1,0:T(1,128)S(1)} async-done(((f32[32,1,128]{2,1,0:T(1,128)}), f32[32,1,128]{2,1,0:T(1,128)S(1)}, u32[]{:S(2)}, u32[]{:S(2)}) %all-to-all-start) | async-done | bytes 16416 | tf_op jit(solution)/shard_map/all_to_all | solution.py:301
  114.5 1.2 %collective-permute-done.32.refs_11_ = bf16[128,256]{1,0:T(8,128)(2,1)S(1)} collective-permute-done((bf16[128,256]{1,0:T(8,128)(2,1)S(1)}, bf16[128,256]{1,0:T(8,128)(2,1)S(1)}, u32[]{:S(2)}, u32[]{:S(2)}) %collective-permute-start.32) | collective-permute-done | bytes 65568 | tf_op jit(solution)/shard_map/ppermute | solution.py:249
  116.3 2.1 %unpack.1 = bf16[1,128,3072]{2,1,0:T(8,128)(2,1)} custom-call(s32[3]{0:T(128)} %pad_add_fusion.place_ref, bf16[128,256]{1,0:T(8,128)(2,1)} %copy-done.11, bf16[128,256]{1,0:T(8,128)(2,1)} %copy-done.28, bf16[128,256]{1,0:T(8,128)(2,1)} %copy-done.29, bf16[128,256]{1,0:T(8,128)(2,1)} %collective-permute-done.12.refs_3_, bf16[128,256]{1,0:T(8,128)(2,1)} %copy-done.12, ...), custom_call_target="tpu_custom_call" | custom-call | tf_op jit(solution)/shard_map/unpack/pallas_call | solution.py:114
  (136 shorter events, 6.1 us)
Async XLA Ops:
  1.2 11.1 %copy-start.15 = (s32[1,4]{1,0:T(1,128)S(1)}, s32[1,4]{1,0:T(1,128)}, u32[]{:S(2)}) copy-start(s32[1,4]{1,0:T(1,128)} %clip_ref.5) | copy-start | bytes 52
  1.2 11.5 %copy-start.38 = (f32[1,4]{1,0:T(1,128)S(1)}, f32[1,4]{1,0:T(1,128)}, u32[]{:S(2)}) copy-start(f32[1,4]{1,0:T(1,128)} %param.15) | copy-start | bytes 52
  1.2 11.5 %copy-start.41 = (s32[1,4]{1,0:T(1,128)S(1)}, s32[1,4]{1,0:T(1,128)}, u32[]{:S(2)}) copy-start(s32[1,4]{1,0:T(1,128)} %param.14) | copy-start | bytes 52
  3.9 8.6 %collective-permute-start.3 = (bf16[128,512]{1,0:T(8,128)(2,1)}, bf16[128,512]{1,0:T(8,128)(2,1)S(1)}, u32[]{:S(2)}, u32[]{:S(2)}) collective-permute-start(bf16[128,512]{1,0:T(8,128)(2,1)} %get-tuple-element.38), channel_id=1, source_target_pairs={{0,2},{2,0},{4,6},{6,4},{8,10},{10,8},{12,14},{14,12},{16,18},{18,... | collective-permute-start | bytes 393224 | tf_op jit(solution)/shard_map/ppermute | solution.py:249
  4.5 8.1 %collective-permute-start.4 = (bf16[128,512]{1,0:T(8,128)(2,1)}, bf16[128,512]{1,0:T(8,128)(2,1)S(1)}, u32[]{:S(2)}, u32[]{:S(2)}) collective-permute-start(bf16[128,512]{1,0:T(8,128)(2,1)} %get-tuple-element.39), channel_id=1, source_target_pairs={{0,4},{2,6},{4,0},{6,2},{8,12},{10,14},{12,8},{14,10},{16,20},{18,... | collective-permute-start | bytes 393224 | tf_op jit(solution)/shard_map/ppermute | solution.py:249
  7.1 7.0 %collective-permute-start.5 = (bf16[128,512]{1,0:T(8,128)(2,1)}, bf16[128,512]{1,0:T(8,128)(2,1)S(1)}, u32[]{:S(2)}, u32[]{:S(2)}) collective-permute-start(bf16[128,512]{1,0:T(8,128)(2,1)} %get-tuple-element.40), channel_id=1, source_target_pairs={{0,6},{2,4},{4,2},{6,0},{8,14},{10,12},{12,10},{14,8},{16,22},{18,... | collective-permute-start | bytes 393224 | tf_op jit(solution)/shard_map/ppermute | solution.py:249
  10.2 7.1 %collective-permute-start.13 = (bf16[128,512]{1,0:T(8,128)(2,1)}, bf16[128,512]{1,0:T(8,128)(2,1)S(1)}, u32[]{:S(2)}, u32[]{:S(2)}) collective-permute-start(bf16[128,512]{1,0:T(8,128)(2,1)} %get-tuple-element.47), channel_id=1, source_target_pairs={{0,2},{2,0},{4,6},{6,4},{8,10},{10,8},{12,14},{14,12},{16,18},{18,... | collective-permute-start | bytes 393224 | tf_op jit(solution)/shard_map/ppermute | solution.py:249
  10.4 8.1 %collective-permute-start.14 = (bf16[128,512]{1,0:T(8,128)(2,1)}, bf16[128,512]{1,0:T(8,128)(2,1)S(1)}, u32[]{:S(2)}, u32[]{:S(2)}) collective-permute-start(bf16[128,512]{1,0:T(8,128)(2,1)} %get-tuple-element.48), channel_id=1, source_target_pairs={{0,4},{2,6},{4,0},{6,2},{8,12},{10,14},{12,8},{14,10},{16,20},{18,... | collective-permute-start | bytes 393224 | tf_op jit(solution)/shard_map/ppermute | solution.py:249
  12.5 7.5 %collective-permute-start.15 = (bf16[128,512]{1,0:T(8,128)(2,1)}, bf16[128,512]{1,0:T(8,128)(2,1)S(1)}, u32[]{:S(2)}, u32[]{:S(2)}) collective-permute-start(bf16[128,512]{1,0:T(8,128)(2,1)} %get-tuple-element.49), channel_id=1, source_target_pairs={{0,6},{2,4},{4,2},{6,0},{8,14},{10,12},{12,10},{14,8},{16,22},{18,... | collective-permute-start | bytes 393224 | tf_op jit(solution)/shard_map/ppermute | solution.py:249
  12.6 10.1 %collective-permute-start.23 = (bf16[128,512]{1,0:T(8,128)(2,1)}, bf16[128,512]{1,0:T(8,128)(2,1)S(1)}, u32[]{:S(2)}, u32[]{:S(2)}) collective-permute-start(bf16[128,512]{1,0:T(8,128)(2,1)} %get-tuple-element.56), channel_id=1, source_target_pairs={{0,2},{2,0},{4,6},{6,4},{8,10},{10,8},{12,14},{14,12},{16,18},{18,... | collective-permute-start | bytes 393224 | tf_op jit(solution)/shard_map/ppermute | solution.py:249
  12.8 24.0 %copy-start.36 = (s32[4]{0:T(128)}, s32[4]{0:T(128)S(1)}, u32[]{:S(2)}) copy-start(s32[4]{0:T(128)S(1)} %fusion.1) | copy-start | bytes 52
  14.1 9.4 %collective-permute-start.24 = (bf16[128,512]{1,0:T(8,128)(2,1)}, bf16[128,512]{1,0:T(8,128)(2,1)S(1)}, u32[]{:S(2)}, u32[]{:S(2)}) collective-permute-start(bf16[128,512]{1,0:T(8,128)(2,1)} %get-tuple-element.57), channel_id=1, source_target_pairs={{0,4},{2,6},{4,0},{6,2},{8,12},{10,14},{12,8},{14,10},{16,20},{18,... | collective-permute-start | bytes 393224 | tf_op jit(solution)/shard_map/ppermute | solution.py:249
  17.3 11.9 %collective-permute-start.25 = (bf16[128,512]{1,0:T(8,128)(2,1)}, bf16[128,512]{1,0:T(8,128)(2,1)S(1)}, u32[]{:S(2)}, u32[]{:S(2)}) collective-permute-start(bf16[128,512]{1,0:T(8,128)(2,1)} %get-tuple-element.58), channel_id=1, source_target_pairs={{0,6},{2,4},{4,2},{6,0},{8,14},{10,12},{12,10},{14,8},{16,22},{18,... | collective-permute-start | bytes 393224 | tf_op jit(solution)/shard_map/ppermute | solution.py:249
  18.5 21.8 %collective-permute-start.6 = (bf16[512,512]{1,0:T(8,128)(2,1)}, bf16[512,512]{1,0:T(8,128)(2,1)S(1)}, u32[]{:S(2)}, u32[]{:S(2)}) collective-permute-start(bf16[512,512]{1,0:T(8,128)(2,1)} %shard_map.98.refs_1_), channel_id=1, source_target_pairs={{0,8},{2,10},{4,12},{6,14},{8,0},{10,2},{12,4},{14,6},{16,24},{18,... | collective-permute-start | bytes 1572872 | tf_op jit(solution)/shard_map/ppermute | solution.py:30
  20.1 16.9 %collective-permute-start.7 = (bf16[512,512]{1,0:T(8,128)(2,1)}, bf16[512,512]{1,0:T(8,128)(2,1)S(1)}, u32[]{:S(2)}, u32[]{:S(2)}) collective-permute-start(bf16[512,512]{1,0:T(8,128)(2,1)} %shard_map.98.refs_1_), channel_id=1, source_target_pairs={{8,16},{10,18},{12,20},{14,22},{16,8},{18,10},{20,12},{22,14},{9,1... | collective-permute-start | bytes 1572872 | tf_op jit(solution)/shard_map/ppermute | solution.py:30
  22.7 13.8 %copy-start.42 = (s32[1,4]{1,0:T(1,128)S(1)}, s32[1,4]{1,0:T(1,128)}, u32[]{:S(2)}) copy-start(s32[1,4]{1,0:T(1,128)} %param.14) | copy-start | bytes 52
  22.7 14.0 %copy-start.14 = (s32[1,16]{1,0:T(1,128)S(1)}, s32[1,16]{1,0:T(1,128)}, u32[]{:S(2)}) copy-start(s32[1,16]{1,0:T(1,128)} %valid_ref.5) | copy-start | bytes 196
  22.7 17.6 %collective-permute-start.17 = (bf16[512,512]{1,0:T(8,128)(2,1)}, bf16[512,512]{1,0:T(8,128)(2,1)S(1)}, u32[]{:S(2)}, u32[]{:S(2)}) collective-permute-start(bf16[512,512]{1,0:T(8,128)(2,1)} %shard_map.101.refs_2_), channel_id=1, source_target_pairs={{8,16},{10,18},{12,20},{14,22},{16,8},{18,10},{20,12},{22,14},{9,1... | collective-permute-start | bytes 1572872 | tf_op jit(solution)/shard_map/ppermute | solution.py:30
  23.5 21.2 %collective-permute-start.16 = (bf16[512,512]{1,0:T(8,128)(2,1)}, bf16[512,512]{1,0:T(8,128)(2,1)S(1)}, u32[]{:S(2)}, u32[]{:S(2)}) collective-permute-start(bf16[512,512]{1,0:T(8,128)(2,1)} %shard_map.101.refs_2_), channel_id=1, source_target_pairs={{0,8},{2,10},{4,12},{6,14},{8,0},{10,2},{12,4},{14,6},{16,24},{18,... | collective-permute-start | bytes 1572872 | tf_op jit(solution)/shard_map/ppermute | solution.py:30
  31.8 13.0 %collective-permute-start.27 = (bf16[512,512]{1,0:T(8,128)(2,1)}, bf16[512,512]{1,0:T(8,128)(2,1)S(1)}, u32[]{:S(2)}, u32[]{:S(2)}) collective-permute-start(bf16[512,512]{1,0:T(8,128)(2,1)} %shard_map.103.refs_2_), channel_id=1, source_target_pairs={{8,16},{10,18},{12,20},{14,22},{16,8},{18,10},{20,12},{22,14},{9,1... | collective-permute-start | bytes 1572872 | tf_op jit(solution)/shard_map/ppermute | solution.py:30
  36.6 8.2 %copy-start.43 = (bf16[128,1536]{1,0:T(8,128)(2,1)S(1)}, bf16[128,1536]{1,0:T(8,128)(2,1)}, u32[]{:S(2)}) copy-start(bf16[128,1536]{1,0:T(8,128)(2,1)} %get-tuple-element.36) | copy-start | bytes 1179652
  37.0 24.9 %copy-start.4 = (bf16[512,512]{1,0:T(8,128)(2,1)}, bf16[512,512]{1,0:T(8,128)(2,1)S(1)}, u32[]{:S(2)}) copy-start(bf16[512,512]{1,0:T(8,128)(2,1)S(1)} %collective-permute-done.7.refs_3_) | copy-start | bytes 1572868
  37.0 29.3 %collective-permute-start.26 = (bf16[512,512]{1,0:T(8,128)(2,1)S(1)}, bf16[512,512]{1,0:T(8,128)(2,1)S(1)}, u32[]{:S(2)}, u32[]{:S(2)}) collective-permute-start(bf16[512,512]{1,0:T(8,128)(2,1)S(1)} %copy-done.3), channel_id=1, source_target_pairs={{0,8},{2,10},{4,12},{6,14},{8,0},{10,2},{12,4},{14,6},{16,24},{18,... | collective-permute-start | bytes 1572872 | tf_op jit(solution)/shard_map/ppermute | solution.py:30
  40.2 22.4 %collective-permute-start = (bf16[128,1536]{1,0:T(8,128)(2,1)}, bf16[128,1536]{1,0:T(8,128)(2,1)S(1)}, u32[]{:S(2)}, u32[]{:S(2)}) collective-permute-start(bf16[128,1536]{1,0:T(8,128)(2,1)} %get-tuple-element.34), channel_id=1, source_target_pairs={{0,2},{2,0},{4,6},{6,4},{8,10},{10,8},{12,14},{14,12},{16,18},{18,... | collective-permute-start | bytes 1179656 | tf_op jit(solution)/shard_map/ppermute | solution.py:249
  40.3 23.7 %collective-permute-start.1 = (bf16[128,1536]{1,0:T(8,128)(2,1)}, bf16[128,1536]{1,0:T(8,128)(2,1)S(1)}, u32[]{:S(2)}, u32[]{:S(2)}) collective-permute-start(bf16[128,1536]{1,0:T(8,128)(2,1)} %get-tuple-element.35), channel_id=1, source_target_pairs={{0,4},{2,6},{4,0},{6,2},{8,12},{10,14},{12,8},{14,10},{16,20},{18,... | collective-permute-start | bytes 1179656 | tf_op jit(solution)/shard_map/ppermute | solution.py:249
  44.7 28.0 %copy-start.39 = (f32[1,4]{1,0:T(1,128)S(1)}, f32[1,4]{1,0:T(1,128)}, u32[]{:S(2)}) copy-start(f32[1,4]{1,0:T(1,128)} %param.15) | copy-start | bytes 52
  44.7 28.0 %copy-start.37 = (s32[4]{0:T(128)S(1)}, s32[4]{0:T(128)}, u32[]{:S(2)}) copy-start(s32[4]{0:T(128)} %copy-done.36) | copy-start | bytes 52
  44.7 28.0 %copy-start.40 = (s32[4]{0:T(128)S(1)}, s32[4]{0:T(128)}, u32[]{:S(2)}) copy-start(s32[4]{0:T(128)} %iota_add_fusion) | copy-start | bytes 52
  44.7 23.8 %collective-permute-start.2 = (bf16[128,1536]{1,0:T(8,128)(2,1)S(1)}, bf16[128,1536]{1,0:T(8,128)(2,1)S(1)}, u32[]{:S(2)}, u32[]{:S(2)}) collective-permute-start(bf16[128,1536]{1,0:T(8,128)(2,1)S(1)} %copy-done.43), channel_id=1, source_target_pairs={{0,6},{2,4},{4,2},{6,0},{8,14},{10,12},{12,10},{14,8},{16,22},{18,... | collective-permute-start | bytes 1179656 | tf_op jit(solution)/shard_map/ppermute | solution.py:249
  44.8 25.7 %collective-permute-start.8 = (bf16[384,512]{1,0:T(8,128)(2,1)S(1)}, bf16[384,512]{1,0:T(8,128)(2,1)S(1)}, u32[]{:S(2)}, u32[]{:S(2)}) collective-permute-start(bf16[384,512]{1,0:T(8,128)(2,1)S(1)} %constant_dynamic-slice_fusion.5), channel_id=1, source_target_pairs={{0,8},{2,10},{4,12},{6,14},{8,0},{10,2},{12,4},{14,6},{16,24},{18,... | collective-permute-start | bytes 1179656 | tf_op jit(solution)/shard_map/ppermute | solution.py:30
  62.7 13.0 %collective-permute-start.9 = (bf16[384,512]{1,0:T(8,128)(2,1)}, bf16[384,512]{1,0:T(8,128)(2,1)}, u32[]{:S(2)}, u32[]{:S(2)}) collective-permute-start(bf16[384,512]{1,0:T(8,128)(2,1)} %constant_dynamic-slice_fusion.4), channel_id=1, source_target_pairs={{8,16},{10,18},{12,20},{14,22},{16,8},{18,10},{20,12},{22,14},{9,1... | collective-permute-start | bytes 1179656 | tf_op jit(solution)/shard_map/ppermute | solution.py:30
  64.1 8.8 %copy-start.17 = (bf16[128,1536]{1,0:T(8,128)(2,1)}, bf16[128,1536]{1,0:T(8,128)(2,1)S(1)}, u32[]{:S(2)}) copy-start(bf16[128,1536]{1,0:T(8,128)(2,1)S(1)} %collective-permute-done.1.refs_2_) | copy-start | bytes 1179652
  64.1 21.5 %collective-permute-start.18 = (bf16[384,512]{1,0:T(8,128)(2,1)}, bf16[384,512]{1,0:T(8,128)(2,1)}, u32[]{:S(2)}, u32[]{:S(2)}) collective-permute-start(bf16[384,512]{1,0:T(8,128)(2,1)} %constant_dynamic-slice_fusion.3), channel_id=1, source_target_pairs={{0,8},{2,10},{4,12},{6,14},{8,0},{10,2},{12,4},{14,6},{16,24},{18,... | collective-permute-start | bytes 1179656 | tf_op jit(solution)/shard_map/ppermute | solution.py:30
  66.2 20.8 %collective-permute-start.19 = (bf16[384,512]{1,0:T(8,128)(2,1)}, bf16[384,512]{1,0:T(8,128)(2,1)}, u32[]{:S(2)}, u32[]{:S(2)}) collective-permute-start(bf16[384,512]{1,0:T(8,128)(2,1)} %constant_dynamic-slice_fusion.2), channel_id=1, source_target_pairs={{8,16},{10,18},{12,20},{14,22},{16,8},{18,10},{20,12},{22,14},{9,1... | collective-permute-start | bytes 1179656 | tf_op jit(solution)/shard_map/ppermute | solution.py:30
  68.5 24.9 %collective-permute-start.28 = (bf16[384,512]{1,0:T(8,128)(2,1)}, bf16[384,512]{1,0:T(8,128)(2,1)S(1)}, u32[]{:S(2)}, u32[]{:S(2)}) collective-permute-start(bf16[384,512]{1,0:T(8,128)(2,1)} %constant_dynamic-slice_fusion.1), channel_id=1, source_target_pairs={{0,8},{2,10},{4,12},{6,14},{8,0},{10,2},{12,4},{14,6},{16,24},{18,... | collective-permute-start | bytes 1179656 | tf_op jit(solution)/shard_map/ppermute | solution.py:30
  71.3 22.4 %collective-permute-start.29 = (bf16[384,512]{1,0:T(8,128)(2,1)}, bf16[384,512]{1,0:T(8,128)(2,1)}, u32[]{:S(2)}, u32[]{:S(2)}) collective-permute-start(bf16[384,512]{1,0:T(8,128)(2,1)} %constant_dynamic-slice_fusion), channel_id=1, source_target_pairs={{8,16},{10,18},{12,20},{14,22},{16,8},{18,10},{20,12},{22,14},{9,1... | collective-permute-start | bytes 1179656 | tf_op jit(solution)/shard_map/ppermute | solution.py:30
  79.1 8.3 %copy-start.1 = (bf16[512,512]{1,0:T(8,128)(2,1)S(1)}, bf16[512,512]{1,0:T(8,128)(2,1)}, u32[]{:S(2)}) copy-start(bf16[512,512]{1,0:T(8,128)(2,1)} %shard_map.101.refs_2_) | copy-start | bytes 1572868
  85.5 22.9 %collective-permute-start.10 = (bf16[128,256]{1,0:T(8,128)(2,1)}, bf16[128,256]{1,0:T(8,128)(2,1)S(1)}, u32[]{:S(2)}, u32[]{:S(2)}) collective-permute-start(bf16[128,256]{1,0:T(8,128)(2,1)} %get-tuple-element.42), channel_id=1, source_target_pairs={{0,2},{2,0},{4,6},{6,4},{8,10},{10,8},{12,14},{14,12},{16,18},{18,... | collective-permute-start | bytes 196616 | tf_op jit(solution)/shard_map/ppermute | solution.py:249
  85.6 22.9 %collective-permute-start.11 = (bf16[128,256]{1,0:T(8,128)(2,1)}, bf16[128,256]{1,0:T(8,128)(2,1)S(1)}, u32[]{:S(2)}, u32[]{:S(2)}) collective-permute-start(bf16[128,256]{1,0:T(8,128)(2,1)} %get-tuple-element.43), channel_id=1, source_target_pairs={{0,4},{2,6},{4,0},{6,2},{8,12},{10,14},{12,8},{14,10},{16,20},{18,... | collective-permute-start | bytes 196616 | tf_op jit(solution)/shard_map/ppermute | solution.py:249
  87.0 21.7 %collective-permute-start.12 = (bf16[128,256]{1,0:T(8,128)(2,1)}, bf16[128,256]{1,0:T(8,128)(2,1)}, u32[]{:S(2)}, u32[]{:S(2)}) collective-permute-start(bf16[128,256]{1,0:T(8,128)(2,1)} %get-tuple-element.44), channel_id=1, source_target_pairs={{0,6},{2,4},{4,2},{6,0},{8,14},{10,12},{12,10},{14,8},{16,22},{18,... | collective-permute-start | bytes 196616 | tf_op jit(solution)/shard_map/ppermute | solution.py:249
  93.4 17.2 %collective-permute-start.20 = (bf16[128,256]{1,0:T(8,128)(2,1)S(1)}, bf16[128,256]{1,0:T(8,128)(2,1)S(1)}, u32[]{:S(2)}, u32[]{:S(2)}) collective-permute-start(bf16[128,256]{1,0:T(8,128)(2,1)S(1)} %get-tuple-element.51), channel_id=1, source_target_pairs={{0,2},{2,0},{4,6},{6,4},{8,10},{10,8},{12,14},{14,12},{16,18},{18,... | collective-permute-start | bytes 196616 | tf_op jit(solution)/shard_map/ppermute | solution.py:249
  100.2 13.6 %all-to-all-start = ((f32[32,1,128]{2,1,0:T(1,128)}), f32[32,1,128]{2,1,0:T(1,128)S(1)}, u32[]{:S(2)}, u32[]{:S(2)}) async-start(f32[32,1,128]{2,1,0:T(1,128)} %bitcast.14), calls=%async_computation | async-start | bytes 32768 | tf_op jit(solution)/shard_map/all_to_all | solution.py:301
  106.6 7.8 %collective-permute-start.21 = (bf16[128,256]{1,0:T(8,128)(2,1)S(1)}, bf16[128,256]{1,0:T(8,128)(2,1)S(1)}, u32[]{:S(2)}, u32[]{:S(2)}) collective-permute-start(bf16[128,256]{1,0:T(8,128)(2,1)S(1)} %get-tuple-element.52), channel_id=1, source_target_pairs={{0,4},{2,6},{4,0},{6,2},{8,12},{10,14},{12,8},{14,10},{16,20},{18,... | collective-permute-start | bytes 196616 | tf_op jit(solution)/shard_map/ppermute | solution.py:249
  108.4 7.3 %copy-start.28 = (bf16[128,256]{1,0:T(8,128)(2,1)}, bf16[128,256]{1,0:T(8,128)(2,1)S(1)}, u32[]{:S(2)}) copy-start(bf16[128,256]{1,0:T(8,128)(2,1)S(1)} %collective-permute-done.10.refs_1_) | copy-start | bytes 196612
  108.4 6.0 %collective-permute-start.22 = (bf16[128,256]{1,0:T(8,128)(2,1)S(1)}, bf16[128,256]{1,0:T(8,128)(2,1)S(1)}, u32[]{:S(2)}, u32[]{:S(2)}) collective-permute-start(bf16[128,256]{1,0:T(8,128)(2,1)S(1)} %get-tuple-element.53), channel_id=1, source_target_pairs={{0,6},{2,4},{4,2},{6,0},{8,14},{10,12},{12,10},{14,8},{16,22},{18,... | collective-permute-start | bytes 196616 | tf_op jit(solution)/shard_map/ppermute | solution.py:249
  108.4 6.0 %collective-permute-start.30 = (bf16[128,256]{1,0:T(8,128)(2,1)S(1)}, bf16[128,256]{1,0:T(8,128)(2,1)S(1)}, u32[]{:S(2)}, u32[]{:S(2)}) collective-permute-start(bf16[128,256]{1,0:T(8,128)(2,1)S(1)} %get-tuple-element.60), channel_id=1, source_target_pairs={{0,2},{2,0},{4,6},{6,4},{8,10},{10,8},{12,14},{14,12},{16,18},{18,... | collective-permute-start | bytes 196616 | tf_op jit(solution)/shard_map/ppermute | solution.py:249
  108.8 5.7 %collective-permute-start.31 = (bf16[128,256]{1,0:T(8,128)(2,1)S(1)}, bf16[128,256]{1,0:T(8,128)(2,1)S(1)}, u32[]{:S(2)}, u32[]{:S(2)}) collective-permute-start(bf16[128,256]{1,0:T(8,128)(2,1)S(1)} %get-tuple-element.61), channel_id=1, source_target_pairs={{0,4},{2,6},{4,0},{6,2},{8,12},{10,14},{12,8},{14,10},{16,20},{18,... | collective-permute-start | bytes 196616 | tf_op jit(solution)/shard_map/ppermute | solution.py:249
  110.6 5.1 %collective-permute-start.32 = (bf16[128,256]{1,0:T(8,128)(2,1)S(1)}, bf16[128,256]{1,0:T(8,128)(2,1)S(1)}, u32[]{:S(2)}, u32[]{:S(2)}) collective-permute-start(bf16[128,256]{1,0:T(8,128)(2,1)S(1)} %get-tuple-element.62), channel_id=1, source_target_pairs={{0,6},{2,4},{4,2},{6,0},{8,14},{10,12},{12,10},{14,8},{16,22},{18,... | collective-permute-start | bytes 196616 | tf_op jit(solution)/shard_map/ppermute | solution.py:249
  (30 other events, 84.1 us)

commit v5 on v4

--- a/solution.py
+++ b/solution.py
@@ -19,6 +19,7 @@
 
 
 masked_score = -1e30
+small_grant = pltpu.CompilerParams(vmem_limit_bytes=6 * 1024 * 1024)
 
 
 def level_swap(value, axis, odd):
@@ -79,6 +80,7 @@
         in_specs=[pl.BlockSpec(memory_space=pltpu.SMEM), hbm, hbm],
         out_specs=[pl.BlockSpec(memory_space=pltpu.VMEM)] * len(shapes),
         scratch_shapes=[pltpu.SemaphoreType.DMA((2 * len(shapes),))],
+        compiler_params=small_grant,
     )(place, first, second)
     return [found[first : first + LEVEL] for first in range(0, len(shapes), LEVEL)]
 
@@ -97,6 +99,7 @@
         out_shape=jax.ShapeDtypeStruct((len(parts) * rows, width), parts[0].dtype),
         in_specs=[pl.BlockSpec(memory_space=pltpu.SMEM)] + [vmem] * len(parts),
         out_specs=vmem,
+        compiler_params=small_grant,
     )(place, *parts)
 
 
@@ -116,6 +119,7 @@
         out_shape=jax.ShapeDtypeStruct((1, outs[0].shape[0], width), outs[0].dtype),
         in_specs=[pl.BlockSpec(memory_space=pltpu.SMEM)] + [vmem] * len(outs),
         out_specs=vmem,
+        compiler_params=small_grant,
         name="unpack",
     )(place, *outs)
 
@@ -123,10 +127,10 @@
 def kernel_body(heads, first_head, earlier, place_ref, clip_ref, valid_ref, weight_ref, *refs):
     earlier, refs = refs[:earlier], refs[earlier:]
     width = heads * HEAD
-    qn_ref, kv_parts = refs[0], refs[1:6]
-    out_refs = refs[6 : 6 + LEVEL]
-    err_ref, kv_buf = refs[6 + LEVEL :]
-    half = qn_ref.shape[1] // 2
+    qn_refs, kv_parts = refs[:LEVEL], refs[LEVEL : LEVEL + 5]
+    out_refs = refs[LEVEL + 5 : 2 * LEVEL + 5]
+    err_ref, kv_buf = refs[2 * LEVEL + 5 :]
+    half = qn_refs[0].shape[1] // 2
     level_first, own, odd = place_ref[0], place_ref[1], place_ref[2]
     sides = (REACH + LEVEL, REACH - LEVEL)
     ends = (REACH + 2 * LEVEL, 0)
@@ -162,7 +166,6 @@
         window_first = clip_start - (level_first - REACH)
         blocks.append(
             (
-                pl.ds(pl.multiple_of(block * BLK, BLK), BLK),
                 pl.ds(pl.multiple_of(window_first * BLK, BLK), MAXB * BLK),
                 jnp.concatenate(bias, axis=1),
                 valid_ref[0, own_id],
@@ -178,9 +181,9 @@
             rows = pl.ds(pl.multiple_of(first * BLK, BLK), ref.shape[0])
             kv_buf[rows, columns] = ref[:, columns]
             kv_buf[rows, other] = ref[:, other]
-        for step, (rows, window, bias, live, weight) in enumerate(blocks):
+        for step, (window, bias, live, weight) in enumerate(blocks):
             scores = lax.dot_general(
-                qn_ref[rows, own_columns],
+                qn_refs[step][:, own_columns],
                 kv_buf[window, columns],
                 (((1,), (1,)), ((), ())),
                 preferred_element_type=jnp.float32,
@@ -198,7 +201,7 @@
             own_live = lax.broadcasted_iota(jnp.int32, (BLK, HEAD), 0) < live
             result = jnp.where(own_live, mixed, 0.0).astype(jnp.bfloat16)
             out_refs[step][:, columns] = result
-            diff = qn_ref[rows, own_other].astype(jnp.float32) - result.astype(jnp.float32)
+            diff = qn_refs[step][:, own_other].astype(jnp.float32) - result.astype(jnp.float32)
             block_err = jnp.where(own_live, diff * diff, 0.0)
             err = err + weight * jnp.sum(block_err.reshape(BLK // 8, 8, HEAD), axis=0)
     if err_ref.shape[0] != err.shape[0]:
@@ -217,7 +220,7 @@
         functools.partial(kernel_body, heads, first_head, len(earlier)),
         out_shape=[jax.ShapeDtypeStruct((BLK, width), jnp.bfloat16)] * LEVEL
         + [jax.ShapeDtypeStruct((spread, HEAD), jnp.float32)],
-        in_specs=[smem] * len(tables) + [vmem] * (len(earlier) + 1 + len(kv_parts)),
+        in_specs=[smem] * len(tables) + [vmem] * (len(earlier) + len(qn) + len(kv_parts)),
         out_specs=[vmem] * (LEVEL + 1),
         scratch_shapes=[
             pltpu.VMEM((total, 2 * width), jnp.bfloat16),
@@ -225,10 +228,10 @@
         cost_estimate=pl.CostEstimate(
             flops=units * 4 * BLK * MAXB * BLK * HEAD,
             transcendentals=units * BLK * MAXB * BLK,
-            bytes_accessed=4 * (total + 2 * qn.shape[0]) * width,
+            bytes_accessed=4 * (total + 2 * LEVEL * BLK) * width,
         ),
-        compiler_params=pltpu.CompilerParams(vmem_limit_bytes=24 * 1024 * 1024),
-    )(*tables, *earlier, qn, *kv_parts)
+        compiler_params=pltpu.CompilerParams(vmem_limit_bytes=12 * 1024 * 1024),
+    )(*tables, *earlier, *qn, *kv_parts)
 
 
 def step(queries, keys, values, next_latent, clip_blocks, valid_counts, group_ids, rewards):
@@ -257,12 +260,13 @@
     def gathered(own):
         reached = (REACH - LEVEL) * BLK
         upper = LEVEL * BLK - reached
-        first = [level_swap(own, "tok", side) for side in (0, 1)]
-        starts = (jnp.where(odd == 0, upper, 0), jnp.where(odd == 1, upper, 0))
-        second = [
-            level_swap(lax.dynamic_slice_in_dim(value, start, reached, 0), "tok", side)
-            for side, (value, start) in enumerate(zip(first[::-1], starts))
-        ]
+        first, second = [], []
+        for side in (0, 1):
+            first.append(level_swap(own, "tok", side))
+        for side in (0, 1):
+            start = jnp.where(odd == side, upper, 0)
+            passed = lax.dynamic_slice_in_dim(first[1 - side], start, reached, 0)
+            second.append(level_swap(passed, "tok", side))
         return [own, *first, *second]
 
     own_kv = []
@@ -272,8 +276,7 @@
         parts = swapped(parts)
         own_kv.append(joined(place, parts))
     (parts,) = packed(place, queries, next_latent, [(0, share)])
-    parts = swapped(parts)
-    qn = joined(place, parts)
+    qn = swapped(parts)
 
     valid_row = valid_counts[0]
     clip_row = clip_blocks[0]

time: 119 us -> 111 us (0.933)
  Pallas kernels: 36.8 us -> 21.5 us
  waiting for transfers between devices: 8.17 us -> 16.6 us
  local copies, waits for them, and re-layouts: 11.3 us -> 8.02 us
  starting transfers between devices: 58.4 us -> 61.3 us
    pallas_call x4 -> x3, Pallas kernels: 8.52 us -> 1.74 us  [joined(): pl.pallas_call(join_body, out_shape=jax.ShapeDtypeStruct((len(parts) * ro...]
    pallas_call x3, Pallas kernels: 9.16 us -> 2.46 us  [packed(): pl.pallas_call(functools.partial(pack_body, spans), out_shape=shapes, in_...]
    ppermute x12, waiting for transfers between devices: 2.46 us -> 8.46 us  [level_swap(): lax.ppermute(value, axis, [pair for pair in partners if 0 <= pair[1] < co...]
    ppermute x21, waiting for transfers between devices: 2.47 us -> 5.01 us  [swapped(): found.append(lax.ppermute(parts[step], 'tok', partners))]
    ppermute x12, starting transfers between devices: 36.7 us -> 38.4 us  [level_swap(): lax.ppermute(value, axis, [pair for pair in partners if 0 <= pair[1] < co...]
    dynamic_slice x6, local copies, waits for them, and re-layouts: 3.89 us -> 2.17 us  [gathered(): passed = lax.dynamic_slice_in_dim(first[1 - side], start, reached, 0)]
    all_to_all x1, starting transfers between devices: 6.4 us -> 8.08 us  [step(): lax.all_to_all(errs[-1], ('tok', 'grp'), 0, 0, tiled=True)[:, 0]]
    unnamed x88 -> x16, local copies, waits for them, and re-layouts: 7.43 us -> 5.85 us
  transfers between devices with their start and end apart: 34 -> 34, of which waited for: 4 -> 11; matrix products, arithmetic and copies ran while one was open for 5% -> 3% of each run, Pallas kernels for 27% -> 18%
where the time goes in v5:
time: 111 us; the launch traced here: 110 us
  starting transfers between devices  61.3 us (55%)
  Pallas kernels  21.5 us (19%)
  waiting for transfers between devices  16.6 us (15%)
  local copies, waits for them, and re-layouts  8.02 us (7%)
  other arithmetic  1.51 us (1%)
    ppermute x12, starting transfers between devices, level_swap(): lax.ppermute(value, axis, [pair for pair in partners if 0 <= pair[1] < co...  38.4 us
    pallas_call x3, Pallas kernels, attend(): pl.pallas_call(functools.partial(kernel_body, heads, first_head, len(earl...  15.8 us
    ppermute x21, starting transfers between devices, swapped(): found.append(lax.ppermute(parts[step], 'tok', partners))  14.8 us
    ppermute x12, waiting for transfers between devices, level_swap(): lax.ppermute(value, axis, [pair for pair in partners if 0 <= pair[1] < co...  8.46 us
    all_to_all x1, starting transfers between devices, step(): lax.all_to_all(errs[-1], ('tok', 'grp'), 0, 0, tiled=True)[:, 0]  8.08 us
    unnamed x16, local copies, waits for them, and re-layouts  5.85 us
    ppermute x21, waiting for transfers between devices, swapped(): found.append(lax.ppermute(parts[step], 'tok', partners))  5.01 us
    all_to_all x1, waiting for transfers between devices, step(): lax.all_to_all(errs[-1], ('tok', 'grp'), 0, 0, tiled=True)[:, 0]  3.16 us
  transfers between devices with their start and end apart: 34, of which 11 were waited for; matrix products, arithmetic and copies ran while one was open for 3% of the time, Pallas kernels for 18%

profile of v5, /device:TPU:0, one launch (start us, length us, event | category | flops | bytes accessed | tf_op | source)
XLA Modules:
  0.0 109.9 jit_solution(17265488484866902532)
XLA Ops:
  0.7 1.1 %copy-done = bf16[1,128,3072]{2,1,0:T(8,128)(2,1)S(1)} copy-done((bf16[1,128,3072]{2,1,0:T(8,128)(2,1)S(1)}, bf16[1,128,3072]{2,1,0:T(8,128)(2,1)}, u32[]{:S(2)}) %copy-start) | copy-done | bytes 786456
  1.9 1.1 %copy-done.1 = bf16[1,128,3072]{2,1,0:T(8,128)(2,1)S(1)} copy-done((bf16[1,128,3072]{2,1,0:T(8,128)(2,1)S(1)}, bf16[1,128,3072]{2,1,0:T(8,128)(2,1)}, u32[]{:S(2)}) %copy-start.1) | copy-done | bytes 786456
  3.0 0.7 shard_map.96
  4.3 2.6 %collective-permute-start.4 = (bf16[128,512]{1,0:T(8,128)(2,1)S(1)}, bf16[128,512]{1,0:T(8,128)(2,1)S(1)}, u32[]{:S(2)}, u32[]{:S(2)}) collective-permute-start(bf16[128,512]{1,0:T(8,128)(2,1)S(1)} %get-tuple-element.39), channel_id=1, source_target_pairs={{0,4},{2,6},{4,0},{6,2},{8,12},{10,14},{12,8},{14,10},{16,20},{18,... | collective-permute-start | bytes 393224 | tf_op jit(solution)/shard_map/ppermute | solution.py:252
  6.9 0.9 shard_map.99
  8.0 1.9 %collective-permute-start.14 = (bf16[128,512]{1,0:T(8,128)(2,1)S(1)}, bf16[128,512]{1,0:T(8,128)(2,1)S(1)}, u32[]{:S(2)}, u32[]{:S(2)}) collective-permute-start(bf16[128,512]{1,0:T(8,128)(2,1)S(1)} %get-tuple-element.48), channel_id=1, source_target_pairs={{0,4},{2,6},{4,0},{6,2},{8,12},{10,14},{12,8},{14,10},{16,20},{18,... | collective-permute-start | bytes 393224 | tf_op jit(solution)/shard_map/ppermute | solution.py:252
  10.5 0.7 collective-permute-done.4.refs_2_
  11.2 0.6 copy-done.6
  12.0 1.6 %collective-permute-done.5.refs_3_ = bf16[128,512]{1,0:T(8,128)(2,1)S(1)} collective-permute-done((bf16[128,512]{1,0:T(8,128)(2,1)S(1)}, bf16[128,512]{1,0:T(8,128)(2,1)S(1)}, u32[]{:S(2)}, u32[]{:S(2)}) %collective-permute-start.5) | collective-permute-done | bytes 131104 | tf_op jit(solution)/shard_map/ppermute | solution.py:252
  13.5 1.4 %collective-permute-start.24 = (bf16[128,512]{1,0:T(8,128)(2,1)S(1)}, bf16[128,512]{1,0:T(8,128)(2,1)S(1)}, u32[]{:S(2)}, u32[]{:S(2)}) collective-permute-start(bf16[128,512]{1,0:T(8,128)(2,1)S(1)} %get-tuple-element.57), channel_id=1, source_target_pairs={{0,4},{2,6},{4,0},{6,2},{8,12},{10,14},{12,8},{14,10},{16,20},{18,... | collective-permute-start | bytes 393224 | tf_op jit(solution)/shard_map/ppermute | solution.py:252
  14.9 0.6 shard_map.97.refs_4_
  16.1 0.7 collective-permute-done.14.refs_2_
  16.8 2.1 %collective-permute-start.6 = (bf16[512,512]{1,0:T(8,128)(2,1)S(1)}, bf16[512,512]{1,0:T(8,128)(2,1)S(1)}, u32[]{:S(2)}, u32[]{:S(2)}) collective-permute-start(bf16[512,512]{1,0:T(8,128)(2,1)S(1)} %shard_map.97.refs_4_), channel_id=1, source_target_pairs={{0,8},{2,10},{4,12},{6,14},{8,0},{10,2},{12,4},{14,6},{16,24},{18,... | collective-permute-start | bytes 1572872 | tf_op jit(solution)/shard_map/ppermute | solution.py:31
  19.2 1.5 %collective-permute-start.7 = (bf16[512,512]{1,0:T(8,128)(2,1)S(1)}, bf16[512,512]{1,0:T(8,128)(2,1)}, u32[]{:S(2)}, u32[]{:S(2)}) collective-permute-start(bf16[512,512]{1,0:T(8,128)(2,1)S(1)} %shard_map.97.refs_4_), channel_id=1, source_target_pairs={{8,16},{10,18},{12,20},{14,22},{16,8},{18,10},{20,12},{22,14},{9,1... | collective-permute-start | bytes 1572872 | tf_op jit(solution)/shard_map/ppermute | solution.py:31
  20.6 0.6 shard_map.100.refs_5_
  21.2 0.7 collective-permute-start.17
  22.4 4.8 %collective-permute-start.16 = (bf16[512,512]{1,0:T(8,128)(2,1)S(1)}, bf16[512,512]{1,0:T(8,128)(2,1)}, u32[]{:S(2)}, u32[]{:S(2)}) collective-permute-start(bf16[512,512]{1,0:T(8,128)(2,1)S(1)} %shard_map.100.refs_5_), channel_id=1, source_target_pairs={{0,8},{2,10},{4,12},{6,14},{8,0},{10,2},{12,4},{14,6},{16,24},{18,... | collective-permute-start | bytes 1572872 | tf_op jit(solution)/shard_map/ppermute | solution.py:31
  27.3 0.6 shard_map.102.refs_5_
  27.9 0.7 collective-permute-start.27
  28.6 1.1 %copy-done.2 = bf16[1,128,3072]{2,1,0:T(8,128)(2,1)S(1)} copy-done((bf16[1,128,3072]{2,1,0:T(8,128)(2,1)S(1)}, bf16[1,128,3072]{2,1,0:T(8,128)(2,1)}, u32[]{:S(2)}) %copy-start.2) | copy-done | bytes 786456
  29.7 1.1 %copy-done.3 = bf16[1,128,3072]{2,1,0:T(8,128)(2,1)S(1)} copy-done((bf16[1,128,3072]{2,1,0:T(8,128)(2,1)S(1)}, bf16[1,128,3072]{2,1,0:T(8,128)(2,1)}, u32[]{:S(2)}) %copy-start.3) | copy-done | bytes 786456
  30.9 0.9 shard_map.95
  31.9 0.7 copy-done.4
  32.8 4.8 %collective-permute-start.26 = (bf16[512,512]{1,0:T(8,128)(2,1)S(1)}, bf16[512,512]{1,0:T(8,128)(2,1)S(1)}, u32[]{:S(2)}, u32[]{:S(2)}) collective-permute-start(bf16[512,512]{1,0:T(8,128)(2,1)S(1)} %shard_map.102.refs_5_), channel_id=1, source_target_pairs={{0,8},{2,10},{4,12},{6,14},{8,0},{10,2},{12,4},{14,6},{16,24},{18,... | collective-permute-start | bytes 1572872 | tf_op jit(solution)/shard_map/ppermute | solution.py:31
  37.5 1.0 constant_dynamic-slice_fusion.5
  38.6 1.5 %collective-permute-start.1 = (bf16[128,1536]{1,0:T(8,128)(2,1)S(1)}, bf16[128,1536]{1,0:T(8,128)(2,1)S(1)}, u32[]{:S(2)}, u32[]{:S(2)}) collective-permute-start(bf16[128,1536]{1,0:T(8,128)(2,1)S(1)} %get-tuple-element.35), channel_id=1, source_target_pairs={{0,4},{2,6},{4,0},{6,2},{8,12},{10,14},{12,8},{14,10},{16,20},{18,... | collective-permute-start | bytes 1179656 | tf_op jit(solution)/shard_map/ppermute | solution.py:252
  40.1 2.9 %collective-permute-done.16.refs_6_ = bf16[512,512]{1,0:T(8,128)(2,1)} collective-permute-done((bf16[512,512]{1,0:T(8,128)(2,1)S(1)}, bf16[512,512]{1,0:T(8,128)(2,1)}, u32[]{:S(2)}, u32[]{:S(2)}) %collective-permute-start.16) | collective-permute-done | bytes 524320 | tf_op jit(solution)/shard_map/ppermute | solution.py:31
  43.0 16.7 %collective-permute-start.8 = (bf16[384,512]{1,0:T(8,128)(2,1)S(1)}, bf16[384,512]{1,0:T(8,128)(2,1)S(1)}, u32[]{:S(2)}, u32[]{:S(2)}) collective-permute-start(bf16[384,512]{1,0:T(8,128)(2,1)S(1)} %constant_dynamic-slice_fusion.5), channel_id=1, source_target_pairs={{0,8},{2,10},{4,12},{6,14},{8,0},{10,2},{12,4},{14,6},{16,24},{18,... | collective-permute-start | bytes 1179656 | tf_op jit(solution)/shard_map/ppermute | solution.py:31
  59.8 1.0 constant_dynamic-slice_fusion.2
  60.8 0.7 collective-permute-start.9
  61.5 2.9 %collective-permute-start.18 = (bf16[384,512]{1,0:T(8,128)(2,1)S(1)}, bf16[384,512]{1,0:T(8,128)(2,1)S(1)}, u32[]{:S(2)}, u32[]{:S(2)}) collective-permute-start(bf16[384,512]{1,0:T(8,128)(2,1)S(1)} %constant_dynamic-slice_fusion.3), channel_id=1, source_target_pairs={{0,8},{2,10},{4,12},{6,14},{8,0},{10,2},{12,4},{14,6},{16,24},{18,... | collective-permute-start | bytes 1179656 | tf_op jit(solution)/shard_map/ppermute | solution.py:31
  64.4 0.7 collective-permute-start.19
  65.2 2.1 %collective-permute-start.28 = (bf16[384,512]{1,0:T(8,128)(2,1)S(1)}, bf16[384,512]{1,0:T(8,128)(2,1)S(1)}, u32[]{:S(2)}, u32[]{:S(2)}) collective-permute-start(bf16[384,512]{1,0:T(8,128)(2,1)S(1)} %constant_dynamic-slice_fusion.1), channel_id=1, source_target_pairs={{0,8},{2,10},{4,12},{6,14},{8,0},{10,2},{12,4},{14,6},{16,24},{18,... | collective-permute-start | bytes 1179656 | tf_op jit(solution)/shard_map/ppermute | solution.py:31
  67.2 2.4 %collective-permute-done.8.refs_7_ = bf16[384,512]{1,0:T(8,128)(2,1)S(1)} collective-permute-done((bf16[384,512]{1,0:T(8,128)(2,1)S(1)}, bf16[384,512]{1,0:T(8,128)(2,1)S(1)}, u32[]{:S(2)}, u32[]{:S(2)}) %collective-permute-start.8) | collective-permute-done | bytes 393248 | tf_op jit(solution)/shard_map/ppermute | solution.py:31
  69.7 0.9 collective-permute-start.29
  70.8 5.2 %shard_map.98 = (bf16[128,256]{1,0:T(8,128)(2,1)S(1)}, bf16[128,256]{1,0:T(8,128)(2,1)S(1)}, bf16[128,256]{1,0:T(8,128)(2,1)S(1)}, bf16[128,256]{1,0:T(8,128)(2,1)S(1)}, f32[8,128]{1,0:T(8,128)S(1)}) custom-call(s32[3]{0:T(128)S(1)} %pad_add_fusion.place_ref, s32[1,4]{1,0:T(1,128)S(1)} %copy-done.5, s32[1,16]{1,0:T(1,128)S(1)} %copy-done.4, ...), custom_call_target="tpu_custom_call" | custom-call | flops 536870912 | bytes 3407872 | tf_op jit(solution)/shard_map/pallas_call | solution.py:219
  76.0 2.1 %collective-permute-done.18.refs_8_ = bf16[384,512]{1,0:T(8,128)(2,1)S(1)} collective-permute-done((bf16[384,512]{1,0:T(8,128)(2,1)S(1)}, bf16[384,512]{1,0:T(8,128)(2,1)S(1)}, u32[]{:S(2)}, u32[]{:S(2)}) %collective-permute-start.18) | collective-permute-done | bytes 393248 | tf_op jit(solution)/shard_map/ppermute | solution.py:31
  78.1 1.5 %collective-permute-start.11 = (bf16[128,256]{1,0:T(8,128)(2,1)S(1)}, bf16[128,256]{1,0:T(8,128)(2,1)S(1)}, u32[]{:S(2)}, u32[]{:S(2)}) collective-permute-start(bf16[128,256]{1,0:T(8,128)(2,1)S(1)} %get-tuple-element.43), channel_id=1, source_target_pairs={{0,4},{2,6},{4,0},{6,2},{8,12},{10,14},{12,8},{14,10},{16,20},{18,... | collective-permute-start | bytes 196616 | tf_op jit(solution)/shard_map/ppermute | solution.py:252
  79.6 5.2 %shard_map.101 = (bf16[128,256]{1,0:T(8,128)(2,1)S(1)}, bf16[128,256]{1,0:T(8,128)(2,1)S(1)}, bf16[128,256]{1,0:T(8,128)(2,1)S(1)}, bf16[128,256]{1,0:T(8,128)(2,1)S(1)}, f32[8,128]{1,0:T(8,128)S(1)}) custom-call(s32[3]{0:T(128)S(1)} %pad_add_fusion.place_ref, s32[1,4]{1,0:T(1,128)S(1)} %copy-done.5, s32[1,16]{1,0:T(1,128)S(1)} %copy-done.4, ...), custom_call_target="tpu_custom_call" | custom-call | flops 536870912 | bytes 3407872 | tf_op jit(solution)/shard_map/pallas_call | solution.py:219
  84.8 1.0 collective-permute-done.28.refs_8_
  85.8 5.4 %shard_map.103 = (bf16[128,256]{1,0:T(8,128)(2,1)S(1)}, bf16[128,256]{1,0:T(8,128)(2,1)S(1)}, bf16[128,256]{1,0:T(8,128)(2,1)S(1)}, bf16[128,256]{1,0:T(8,128)(2,1)S(1)}, f32[32,128]{1,0:T(8,128)}) custom-call(s32[3]{0:T(128)S(1)} %pad_add_fusion.place_ref, s32[1,4]{1,0:T(1,128)S(1)} %copy-done.5, s32[1,16]{1,0:T(1,128)S(1)} %copy-done.4, ...), custom_call_target="tpu_custom_call" | custom-call | flops 536870912 | bytes 3407872 | tf_op jit(solution)/shard_map/pallas_call | solution.py:219
  91.2 8.1 %all-to-all-start = ((f32[32,1,128]{2,1,0:T(1,128)}), f32[32,1,128]{2,1,0:T(1,128)S(1)}, u32[]{:S(2)}, u32[]{:S(2)}) async-start(f32[32,1,128]{2,1,0:T(1,128)} %bitcast.14), calls=%async_computation | async-start | bytes 32768 | tf_op jit(solution)/shard_map/all_to_all | solution.py:304
  99.3 1.8 %collective-permute-start.21 = (bf16[128,256]{1,0:T(8,128)(2,1)S(1)}, bf16[128,256]{1,0:T(8,128)(2,1)S(1)}, u32[]{:S(2)}, u32[]{:S(2)}) collective-permute-start(bf16[128,256]{1,0:T(8,128)(2,1)S(1)} %get-tuple-element.52), channel_id=1, source_target_pairs={{0,4},{2,6},{4,0},{6,2},{8,12},{10,14},{12,8},{14,10},{16,20},{18,... | collective-permute-start | bytes 196616 | tf_op jit(solution)/shard_map/ppermute | solution.py:252
  101.5 1.8 %collective-permute-start.31 = (bf16[128,256]{1,0:T(8,128)(2,1)S(1)}, bf16[128,256]{1,0:T(8,128)(2,1)S(1)}, u32[]{:S(2)}, u32[]{:S(2)}) collective-permute-start(bf16[128,256]{1,0:T(8,128)(2,1)S(1)} %get-tuple-element.61), channel_id=1, source_target_pairs={{0,4},{2,6},{4,0},{6,2},{8,12},{10,14},{12,8},{14,10},{16,20},{18,... | collective-permute-start | bytes 196616 | tf_op jit(solution)/shard_map/ppermute | solution.py:252
  103.3 3.2 %all-to-all-done = f32[32,1,128]{2,1,0:T(1,128)S(1)} async-done(((f32[32,1,128]{2,1,0:T(1,128)}), f32[32,1,128]{2,1,0:T(1,128)S(1)}, u32[]{:S(2)}, u32[]{:S(2)}) %all-to-all-start) | async-done | bytes 16416 | tf_op jit(solution)/shard_map/all_to_all | solution.py:304
  106.5 0.6 slice_reduce_fusion
  107.1 1.3 %collective-permute-done.32.refs_11_ = bf16[128,256]{1,0:T(8,128)(2,1)S(1)} collective-permute-done((bf16[128,256]{1,0:T(8,128)(2,1)S(1)}, bf16[128,256]{1,0:T(8,128)(2,1)S(1)}, u32[]{:S(2)}, u32[]{:S(2)}) %collective-permute-start.32) | collective-permute-done | bytes 65568 | tf_op jit(solution)/shard_map/ppermute | solution.py:252
  108.4 1.5 %unpack.1 = bf16[1,128,3072]{2,1,0:T(8,128)(2,1)} custom-call(s32[3]{0:T(128)S(1)} %pad_add_fusion.place_ref, bf16[128,256]{1,0:T(8,128)(2,1)S(1)} %get-tuple-element.41.refs_0_, bf16[128,256]{1,0:T(8,128)(2,1)S(1)} %collective-permute-done.10.refs_1_, bf16[128,256]{1,0:T(8,128)(2,1)S(1)} %collective-permute-done.11.refs_2_, ...), custom_call_target="tpu_custom_call" | custom-call | tf_op jit(solution)/shard_map/unpack/pallas_call | solution.py:117
  (63 shorter events, 4.2 us)
Async XLA Ops:
  0.7 1.1 %copy-start = (bf16[1,128,3072]{2,1,0:T(8,128)(2,1)S(1)}, bf16[1,128,3072]{2,1,0:T(8,128)(2,1)}, u32[]{:S(2)}) copy-start(bf16[1,128,3072]{2,1,0:T(8,128)(2,1)} %first_ref.5) | copy-start | bytes 2359300
  1.9 1.1 %copy-start.1 = (bf16[1,128,3072]{2,1,0:T(8,128)(2,1)S(1)}, bf16[1,128,3072]{2,1,0:T(8,128)(2,1)}, u32[]{:S(2)}) copy-start(bf16[1,128,3072]{2,1,0:T(8,128)(2,1)} %second_ref.5) | copy-start | bytes 2359300
  3.7 6.4 %collective-permute-start.3 = (bf16[128,512]{1,0:T(8,128)(2,1)S(1)}, bf16[128,512]{1,0:T(8,128)(2,1)S(1)}, u32[]{:S(2)}, u32[]{:S(2)}) collective-permute-start(bf16[128,512]{1,0:T(8,128)(2,1)S(1)} %get-tuple-element.38), channel_id=1, source_target_pairs={{0,2},{2,0},{4,6},{6,4},{8,10},{10,8},{12,14},{14,12},{16,18},{18,... | collective-permute-start | bytes 393224 | tf_op jit(solution)/shard_map/ppermute | solution.py:252
  4.3 6.9 %collective-permute-start.4 = (bf16[128,512]{1,0:T(8,128)(2,1)S(1)}, bf16[128,512]{1,0:T(8,128)(2,1)S(1)}, u32[]{:S(2)}, u32[]{:S(2)}) collective-permute-start(bf16[128,512]{1,0:T(8,128)(2,1)S(1)} %get-tuple-element.39), channel_id=1, source_target_pairs={{0,4},{2,6},{4,0},{6,2},{8,12},{10,14},{12,8},{14,10},{16,20},{18,... | collective-permute-start | bytes 393224 | tf_op jit(solution)/shard_map/ppermute | solution.py:252
  6.8 6.7 %collective-permute-start.5 = (bf16[128,512]{1,0:T(8,128)(2,1)S(1)}, bf16[128,512]{1,0:T(8,128)(2,1)S(1)}, u32[]{:S(2)}, u32[]{:S(2)}) collective-permute-start(bf16[128,512]{1,0:T(8,128)(2,1)S(1)} %get-tuple-element.40), channel_id=1, source_target_pairs={{0,6},{2,4},{4,2},{6,0},{8,14},{10,12},{12,10},{14,8},{16,22},{18,... | collective-permute-start | bytes 393224 | tf_op jit(solution)/shard_map/ppermute | solution.py:252
  7.8 7.8 %collective-permute-start.13 = (bf16[128,512]{1,0:T(8,128)(2,1)S(1)}, bf16[128,512]{1,0:T(8,128)(2,1)S(1)}, u32[]{:S(2)}, u32[]{:S(2)}) collective-permute-start(bf16[128,512]{1,0:T(8,128)(2,1)S(1)} %get-tuple-element.47), channel_id=1, source_target_pairs={{0,2},{2,0},{4,6},{6,4},{8,10},{10,8},{12,14},{14,12},{16,18},{18,... | collective-permute-start | bytes 393224 | tf_op jit(solution)/shard_map/ppermute | solution.py:252
  8.0 2.0 %copy-start.5 = (s32[1,4]{1,0:T(1,128)S(1)}, s32[1,4]{1,0:T(1,128)}, u32[]{:S(2)}) copy-start(s32[1,4]{1,0:T(1,128)} %clip_ref.5) | copy-start | bytes 52
  8.0 8.8 %collective-permute-start.14 = (bf16[128,512]{1,0:T(8,128)(2,1)S(1)}, bf16[128,512]{1,0:T(8,128)(2,1)S(1)}, u32[]{:S(2)}, u32[]{:S(2)}) collective-permute-start(bf16[128,512]{1,0:T(8,128)(2,1)S(1)} %get-tuple-element.48), channel_id=1, source_target_pairs={{0,4},{2,6},{4,0},{6,2},{8,12},{10,14},{12,8},{14,10},{16,20},{18,... | collective-permute-start | bytes 393224 | tf_op jit(solution)/shard_map/ppermute | solution.py:252
  10.1 9.0 %collective-permute-start.15 = (bf16[128,512]{1,0:T(8,128)(2,1)S(1)}, bf16[128,512]{1,0:T(8,128)(2,1)S(1)}, u32[]{:S(2)}, u32[]{:S(2)}) collective-permute-start(bf16[128,512]{1,0:T(8,128)(2,1)S(1)} %get-tuple-element.49), channel_id=1, source_target_pairs={{0,6},{2,4},{4,2},{6,0},{8,14},{10,12},{12,10},{14,8},{16,22},{18,... | collective-permute-start | bytes 393224 | tf_op jit(solution)/shard_map/ppermute | solution.py:252
  11.2 10.0 %collective-permute-start.23 = (bf16[128,512]{1,0:T(8,128)(2,1)S(1)}, bf16[128,512]{1,0:T(8,128)(2,1)S(1)}, u32[]{:S(2)}, u32[]{:S(2)}) collective-permute-start(bf16[128,512]{1,0:T(8,128)(2,1)S(1)} %get-tuple-element.56), channel_id=1, source_target_pairs={{0,2},{2,0},{4,6},{6,4},{8,10},{10,8},{12,14},{14,12},{16,18},{18,... | collective-permute-start | bytes 393224 | tf_op jit(solution)/shard_map/ppermute | solution.py:252
  11.2 0.7 copy-start.6
  11.2 0.7 copy-start.7
  13.5 8.9 %collective-permute-start.24 = (bf16[128,512]{1,0:T(8,128)(2,1)S(1)}, bf16[128,512]{1,0:T(8,128)(2,1)S(1)}, u32[]{:S(2)}, u32[]{:S(2)}) collective-permute-start(bf16[128,512]{1,0:T(8,128)(2,1)S(1)} %get-tuple-element.57), channel_id=1, source_target_pairs={{0,4},{2,6},{4,0},{6,2},{8,12},{10,14},{12,8},{14,10},{16,20},{18,... | collective-permute-start | bytes 393224 | tf_op jit(solution)/shard_map/ppermute | solution.py:252
  15.5 11.7 %collective-permute-start.25 = (bf16[128,512]{1,0:T(8,128)(2,1)S(1)}, bf16[128,512]{1,0:T(8,128)(2,1)S(1)}, u32[]{:S(2)}, u32[]{:S(2)}) collective-permute-start(bf16[128,512]{1,0:T(8,128)(2,1)S(1)} %get-tuple-element.58), channel_id=1, source_target_pairs={{0,6},{2,4},{4,2},{6,0},{8,14},{10,12},{12,10},{14,8},{16,22},{18,... | collective-permute-start | bytes 393224 | tf_op jit(solution)/shard_map/ppermute | solution.py:252
  16.8 21.7 %collective-permute-start.6 = (bf16[512,512]{1,0:T(8,128)(2,1)S(1)}, bf16[512,512]{1,0:T(8,128)(2,1)S(1)}, u32[]{:S(2)}, u32[]{:S(2)}) collective-permute-start(bf16[512,512]{1,0:T(8,128)(2,1)S(1)} %shard_map.97.refs_4_), channel_id=1, source_target_pairs={{0,8},{2,10},{4,12},{6,14},{8,0},{10,2},{12,4},{14,6},{16,24},{18,... | collective-permute-start | bytes 1572872 | tf_op jit(solution)/shard_map/ppermute | solution.py:31
  19.2 13.6 %collective-permute-start.7 = (bf16[512,512]{1,0:T(8,128)(2,1)S(1)}, bf16[512,512]{1,0:T(8,128)(2,1)}, u32[]{:S(2)}, u32[]{:S(2)}) collective-permute-start(bf16[512,512]{1,0:T(8,128)(2,1)S(1)} %shard_map.97.refs_4_), channel_id=1, source_target_pairs={{8,16},{10,18},{12,20},{14,22},{16,8},{18,10},{20,12},{22,14},{9,1... | collective-permute-start | bytes 1572872 | tf_op jit(solution)/shard_map/ppermute | solution.py:31
  21.2 17.4 %collective-permute-start.17 = (bf16[512,512]{1,0:T(8,128)(2,1)S(1)}, bf16[512,512]{1,0:T(8,128)(2,1)S(1)}, u32[]{:S(2)}, u32[]{:S(2)}) collective-permute-start(bf16[512,512]{1,0:T(8,128)(2,1)S(1)} %shard_map.100.refs_5_), channel_id=1, source_target_pairs={{8,16},{10,18},{12,20},{14,22},{16,8},{18,10},{20,12},{22,14},{9,1... | collective-permute-start | bytes 1572872 | tf_op jit(solution)/shard_map/ppermute | solution.py:31
  22.4 20.6 %collective-permute-start.16 = (bf16[512,512]{1,0:T(8,128)(2,1)S(1)}, bf16[512,512]{1,0:T(8,128)(2,1)}, u32[]{:S(2)}, u32[]{:S(2)}) collective-permute-start(bf16[512,512]{1,0:T(8,128)(2,1)S(1)} %shard_map.100.refs_5_), channel_id=1, source_target_pairs={{0,8},{2,10},{4,12},{6,14},{8,0},{10,2},{12,4},{14,6},{16,24},{18,... | collective-permute-start | bytes 1572872 | tf_op jit(solution)/shard_map/ppermute | solution.py:31
  27.9 15.2 %collective-permute-start.27 = (bf16[512,512]{1,0:T(8,128)(2,1)S(1)}, bf16[512,512]{1,0:T(8,128)(2,1)S(1)}, u32[]{:S(2)}, u32[]{:S(2)}) collective-permute-start(bf16[512,512]{1,0:T(8,128)(2,1)S(1)} %shard_map.102.refs_5_), channel_id=1, source_target_pairs={{8,16},{10,18},{12,20},{14,22},{16,8},{18,10},{20,12},{22,14},{9,1... | collective-permute-start | bytes 1572872 | tf_op jit(solution)/shard_map/ppermute | solution.py:31
  28.6 1.1 %copy-start.2 = (bf16[1,128,3072]{2,1,0:T(8,128)(2,1)S(1)}, bf16[1,128,3072]{2,1,0:T(8,128)(2,1)}, u32[]{:S(2)}) copy-start(bf16[1,128,3072]{2,1,0:T(8,128)(2,1)} %first_ref.3) | copy-start | bytes 2359300
  29.7 1.1 %copy-start.3 = (bf16[1,128,3072]{2,1,0:T(8,128)(2,1)S(1)}, bf16[1,128,3072]{2,1,0:T(8,128)(2,1)}, u32[]{:S(2)}) copy-start(bf16[1,128,3072]{2,1,0:T(8,128)(2,1)} %second_ref.3) | copy-start | bytes 2359300
  31.9 0.7 copy-start.4
  32.8 31.7 %collective-permute-start.26 = (bf16[512,512]{1,0:T(8,128)(2,1)S(1)}, bf16[512,512]{1,0:T(8,128)(2,1)S(1)}, u32[]{:S(2)}, u32[]{:S(2)}) collective-permute-start(bf16[512,512]{1,0:T(8,128)(2,1)S(1)} %shard_map.102.refs_5_), channel_id=1, source_target_pairs={{0,8},{2,10},{4,12},{6,14},{8,0},{10,2},{12,4},{14,6},{16,24},{18,... | collective-permute-start | bytes 1572872 | tf_op jit(solution)/shard_map/ppermute | solution.py:31
  38.6 22.3 %collective-permute-start = (bf16[128,1536]{1,0:T(8,128)(2,1)S(1)}, bf16[128,1536]{1,0:T(8,128)(2,1)S(1)}, u32[]{:S(2)}, u32[]{:S(2)}) collective-permute-start(bf16[128,1536]{1,0:T(8,128)(2,1)S(1)} %get-tuple-element.34), channel_id=1, source_target_pairs={{0,2},{2,0},{4,6},{6,4},{8,10},{10,8},{12,14},{14,12},{16,18},{18,... | collective-permute-start | bytes 1179656 | tf_op jit(solution)/shard_map/ppermute | solution.py:252
  38.6 22.9 %collective-permute-start.1 = (bf16[128,1536]{1,0:T(8,128)(2,1)S(1)}, bf16[128,1536]{1,0:T(8,128)(2,1)S(1)}, u32[]{:S(2)}, u32[]{:S(2)}) collective-permute-start(bf16[128,1536]{1,0:T(8,128)(2,1)S(1)} %get-tuple-element.35), channel_id=1, source_target_pairs={{0,4},{2,6},{4,0},{6,2},{8,12},{10,14},{12,8},{14,10},{16,20},{18,... | collective-permute-start | bytes 1179656 | tf_op jit(solution)/shard_map/ppermute | solution.py:252
  43.0 22.1 %collective-permute-start.2 = (bf16[128,1536]{1,0:T(8,128)(2,1)S(1)}, bf16[128,1536]{1,0:T(8,128)(2,1)S(1)}, u32[]{:S(2)}, u32[]{:S(2)}) collective-permute-start(bf16[128,1536]{1,0:T(8,128)(2,1)S(1)} %get-tuple-element.36), channel_id=1, source_target_pairs={{0,6},{2,4},{4,2},{6,0},{8,14},{10,12},{12,10},{14,8},{16,22},{18,... | collective-permute-start | bytes 1179656 | tf_op jit(solution)/shard_map/ppermute | solution.py:252
  43.0 26.7 %collective-permute-start.8 = (bf16[384,512]{1,0:T(8,128)(2,1)S(1)}, bf16[384,512]{1,0:T(8,128)(2,1)S(1)}, u32[]{:S(2)}, u32[]{:S(2)}) collective-permute-start(bf16[384,512]{1,0:T(8,128)(2,1)S(1)} %constant_dynamic-slice_fusion.5), channel_id=1, source_target_pairs={{0,8},{2,10},{4,12},{6,14},{8,0},{10,2},{12,4},{14,6},{16,24},{18,... | collective-permute-start | bytes 1179656 | tf_op jit(solution)/shard_map/ppermute | solution.py:31
  60.8 9.9 %collective-permute-start.9 = (bf16[384,512]{1,0:T(8,128)(2,1)S(1)}, bf16[384,512]{1,0:T(8,128)(2,1)S(1)}, u32[]{:S(2)}, u32[]{:S(2)}) collective-permute-start(bf16[384,512]{1,0:T(8,128)(2,1)S(1)} %constant_dynamic-slice_fusion.4), channel_id=1, source_target_pairs={{8,16},{10,18},{12,20},{14,22},{16,8},{18,10},{20,12},{22,14},{9,1... | collective-permute-start | bytes 1179656 | tf_op jit(solution)/shard_map/ppermute | solution.py:31
  61.5 16.6 %collective-permute-start.18 = (bf16[384,512]{1,0:T(8,128)(2,1)S(1)}, bf16[384,512]{1,0:T(8,128)(2,1)S(1)}, u32[]{:S(2)}, u32[]{:S(2)}) collective-permute-start(bf16[384,512]{1,0:T(8,128)(2,1)S(1)} %constant_dynamic-slice_fusion.3), channel_id=1, source_target_pairs={{0,8},{2,10},{4,12},{6,14},{8,0},{10,2},{12,4},{14,6},{16,24},{18,... | collective-permute-start | bytes 1179656 | tf_op jit(solution)/shard_map/ppermute | solution.py:31
  64.4 15.2 %collective-permute-start.19 = (bf16[384,512]{1,0:T(8,128)(2,1)S(1)}, bf16[384,512]{1,0:T(8,128)(2,1)S(1)}, u32[]{:S(2)}, u32[]{:S(2)}) collective-permute-start(bf16[384,512]{1,0:T(8,128)(2,1)S(1)} %constant_dynamic-slice_fusion.2), channel_id=1, source_target_pairs={{8,16},{10,18},{12,20},{14,22},{16,8},{18,10},{20,12},{22,14},{9,1... | collective-permute-start | bytes 1179656 | tf_op jit(solution)/shard_map/ppermute | solution.py:31
  65.2 20.7 %collective-permute-start.28 = (bf16[384,512]{1,0:T(8,128)(2,1)S(1)}, bf16[384,512]{1,0:T(8,128)(2,1)S(1)}, u32[]{:S(2)}, u32[]{:S(2)}) collective-permute-start(bf16[384,512]{1,0:T(8,128)(2,1)S(1)} %constant_dynamic-slice_fusion.1), channel_id=1, source_target_pairs={{0,8},{2,10},{4,12},{6,14},{8,0},{10,2},{12,4},{14,6},{16,24},{18,... | collective-permute-start | bytes 1179656 | tf_op jit(solution)/shard_map/ppermute | solution.py:31
  69.7 16.1 %collective-permute-start.29 = (bf16[384,512]{1,0:T(8,128)(2,1)S(1)}, bf16[384,512]{1,0:T(8,128)(2,1)S(1)}, u32[]{:S(2)}, u32[]{:S(2)}) collective-permute-start(bf16[384,512]{1,0:T(8,128)(2,1)S(1)} %constant_dynamic-slice_fusion), channel_id=1, source_target_pairs={{8,16},{10,18},{12,20},{14,22},{16,8},{18,10},{20,12},{22,14},{9,1... | collective-permute-start | bytes 1179656 | tf_op jit(solution)/shard_map/ppermute | solution.py:31
  75.9 25.2 %collective-permute-start.10 = (bf16[128,256]{1,0:T(8,128)(2,1)S(1)}, bf16[128,256]{1,0:T(8,128)(2,1)S(1)}, u32[]{:S(2)}, u32[]{:S(2)}) collective-permute-start(bf16[128,256]{1,0:T(8,128)(2,1)S(1)} %get-tuple-element.42), channel_id=1, source_target_pairs={{0,2},{2,0},{4,6},{6,4},{8,10},{10,8},{12,14},{14,12},{16,18},{18,... | collective-permute-start | bytes 196616 | tf_op jit(solution)/shard_map/ppermute | solution.py:252
  78.1 23.1 %collective-permute-start.11 = (bf16[128,256]{1,0:T(8,128)(2,1)S(1)}, bf16[128,256]{1,0:T(8,128)(2,1)S(1)}, u32[]{:S(2)}, u32[]{:S(2)}) collective-permute-start(bf16[128,256]{1,0:T(8,128)(2,1)S(1)} %get-tuple-element.43), channel_id=1, source_target_pairs={{0,4},{2,6},{4,0},{6,2},{8,12},{10,14},{12,8},{14,10},{16,20},{18,... | collective-permute-start | bytes 196616 | tf_op jit(solution)/shard_map/ppermute | solution.py:252
  79.6 21.9 %collective-permute-start.12 = (bf16[128,256]{1,0:T(8,128)(2,1)S(1)}, bf16[128,256]{1,0:T(8,128)(2,1)S(1)}, u32[]{:S(2)}, u32[]{:S(2)}) collective-permute-start(bf16[128,256]{1,0:T(8,128)(2,1)S(1)} %get-tuple-element.44), channel_id=1, source_target_pairs={{0,6},{2,4},{4,2},{6,0},{8,14},{10,12},{12,10},{14,8},{16,22},{18,... | collective-permute-start | bytes 196616 | tf_op jit(solution)/shard_map/ppermute | solution.py:252
  85.8 17.5 %collective-permute-start.20 = (bf16[128,256]{1,0:T(8,128)(2,1)S(1)}, bf16[128,256]{1,0:T(8,128)(2,1)S(1)}, u32[]{:S(2)}, u32[]{:S(2)}) collective-permute-start(bf16[128,256]{1,0:T(8,128)(2,1)S(1)} %get-tuple-element.51), channel_id=1, source_target_pairs={{0,2},{2,0},{4,6},{6,4},{8,10},{10,8},{12,14},{14,12},{16,18},{18,... | collective-permute-start | bytes 196616 | tf_op jit(solution)/shard_map/ppermute | solution.py:252
  91.2 15.2 %all-to-all-start = ((f32[32,1,128]{2,1,0:T(1,128)}), f32[32,1,128]{2,1,0:T(1,128)S(1)}, u32[]{:S(2)}, u32[]{:S(2)}) async-start(f32[32,1,128]{2,1,0:T(1,128)} %bitcast.14), calls=%async_computation | async-start | bytes 32768 | tf_op jit(solution)/shard_map/all_to_all | solution.py:304
  99.3 7.8 %collective-permute-start.21 = (bf16[128,256]{1,0:T(8,128)(2,1)S(1)}, bf16[128,256]{1,0:T(8,128)(2,1)S(1)}, u32[]{:S(2)}, u32[]{:S(2)}) collective-permute-start(bf16[128,256]{1,0:T(8,128)(2,1)S(1)} %get-tuple-element.52), channel_id=1, source_target_pairs={{0,4},{2,6},{4,0},{6,2},{8,12},{10,14},{12,8},{14,10},{16,20},{18,... | collective-permute-start | bytes 196616 | tf_op jit(solution)/shard_map/ppermute | solution.py:252
  101.2 5.9 %collective-permute-start.22 = (bf16[128,256]{1,0:T(8,128)(2,1)S(1)}, bf16[128,256]{1,0:T(8,128)(2,1)S(1)}, u32[]{:S(2)}, u32[]{:S(2)}) collective-permute-start(bf16[128,256]{1,0:T(8,128)(2,1)S(1)} %get-tuple-element.53), channel_id=1, source_target_pairs={{0,6},{2,4},{4,2},{6,0},{8,14},{10,12},{12,10},{14,8},{16,22},{18,... | collective-permute-start | bytes 196616 | tf_op jit(solution)/shard_map/ppermute | solution.py:252
  101.2 5.9 %collective-permute-start.30 = (bf16[128,256]{1,0:T(8,128)(2,1)S(1)}, bf16[128,256]{1,0:T(8,128)(2,1)S(1)}, u32[]{:S(2)}, u32[]{:S(2)}) collective-permute-start(bf16[128,256]{1,0:T(8,128)(2,1)S(1)} %get-tuple-element.60), channel_id=1, source_target_pairs={{0,2},{2,0},{4,6},{6,4},{8,10},{10,8},{12,14},{14,12},{16,18},{18,... | collective-permute-start | bytes 196616 | tf_op jit(solution)/shard_map/ppermute | solution.py:252
  101.5 5.6 %collective-permute-start.31 = (bf16[128,256]{1,0:T(8,128)(2,1)S(1)}, bf16[128,256]{1,0:T(8,128)(2,1)S(1)}, u32[]{:S(2)}, u32[]{:S(2)}) collective-permute-start(bf16[128,256]{1,0:T(8,128)(2,1)S(1)} %get-tuple-element.61), channel_id=1, source_target_pairs={{0,4},{2,6},{4,0},{6,2},{8,12},{10,14},{12,8},{14,10},{16,20},{18,... | collective-permute-start | bytes 196616 | tf_op jit(solution)/shard_map/ppermute | solution.py:252
  103.3 5.1 %collective-permute-start.32 = (bf16[128,256]{1,0:T(8,128)(2,1)S(1)}, bf16[128,256]{1,0:T(8,128)(2,1)S(1)}, u32[]{:S(2)}, u32[]{:S(2)}) collective-permute-start(bf16[128,256]{1,0:T(8,128)(2,1)S(1)} %get-tuple-element.62), channel_id=1, source_target_pairs={{0,6},{2,4},{4,2},{6,0},{8,14},{10,12},{12,10},{14,8},{16,22},{18,... | collective-permute-start | bytes 196616 | tf_op jit(solution)/shard_map/ppermute | solution.py:252

commit v6 on v5

--- a/solution.py
+++ b/solution.py
@@ -15,7 +15,7 @@
 GROUPS = 4
 LEVEL = MAXB // 2
 REACH = MAXB - 1
-CHUNKS = (1, 1, 1)
+CHUNKS = (1, 2, 2, 1)
 
 
 masked_score = -1e30
@@ -68,7 +68,7 @@
 
 
 def packed(place, first, second, spans):
-    hbm = pl.BlockSpec(memory_space=pl.ANY)
+    hbm = pl.BlockSpec(memory_space=pltpu.HBM)
     shapes = [
         jax.ShapeDtypeStruct((first.shape[1], 2 * (high - low)), first.dtype)
         for low, high in spans
@@ -270,7 +270,8 @@
         return [own, *first, *second]
 
     own_kv = []
-    packs = packed(place, keys, values, spans[:1])
+    in_hbm = [pltpu.with_memory_space_constraint(value, pltpu.HBM) for value in (keys, values)]
+    packs = packed(place, *in_hbm, spans[:1])
     packs += packed(place, keys, values, spans[1:])
     for parts in packs:
         parts = swapped(parts)

time: 111 us -> 119 us (1.072)
  starting transfers between devices: 61.3 us -> 71.1 us
  waiting for transfers between devices: 16.6 us -> 13.5 us
  Pallas kernels: 21.5 us -> 24.5 us
  local copies, waits for them, and re-layouts: 8.02 us -> 6.58 us
    ppermute x12 -> x16, starting transfers between devices: 38.4 us -> 47.5 us  [level_swap(): lax.ppermute(value, axis, [pair for pair in partners if 0 <= pair[1] < co...]
    ppermute x12 -> x16, waiting for transfers between devices: 8.46 us -> 3.37 us  [level_swap(): lax.ppermute(value, axis, [pair for pair in partners if 0 <= pair[1] < co...]
    ppermute x21 -> x27, starting transfers between devices: 14.8 us -> 19.3 us  [swapped(): found.append(lax.ppermute(parts[step], 'tok', partners))]
    all_to_all x1, starting transfers between devices: 8.08 us -> 4.33 us  [step(): lax.all_to_all(errs[-1], ('tok', 'grp'), 0, 0, tiled=True)[:, 0]]
    unnamed x16 -> x20, local copies, waits for them, and re-layouts: 5.85 us -> 3.6 us
    ppermute x21 -> x27, waiting for transfers between devices: 5.01 us -> 6.94 us  [swapped(): found.append(lax.ppermute(parts[step], 'tok', partners))]
    pallas_call x3 -> x4, Pallas kernels: 15.8 us -> 17.2 us  [attend(): pl.pallas_call(functools.partial(kernel_body, heads, first_head, len(earl...]
    dynamic_slice x6 -> x8, local copies, waits for them, and re-layouts: 2.17 us -> 2.98 us  [gathered(): passed = lax.dynamic_slice_in_dim(first[1 - side], start, reached, 0)]
  transfers between devices with their start and end apart: 34 -> 44, of which waited for: 11 -> 5; matrix products, arithmetic and copies ran while one was open for 3% -> 4% of each run, Pallas kernels for 18% -> 18%
where the time goes in v6:
time: 119 us; the launch traced here: 118 us
  starting transfers between devices  71.1 us (60%)
  Pallas kernels  24.5 us (21%)
  waiting for transfers between devices  13.5 us (11%)
  local copies, waits for them, and re-layouts  6.58 us (6%)
  other arithmetic  1.51 us (1%)
    ppermute x16, starting transfers between devices, level_swap(): lax.ppermute(value, axis, [pair for pair in partners if 0 <= pair[1] < co...  47.5 us
    ppermute x27, starting transfers between devices, swapped(): found.append(lax.ppermute(parts[step], 'tok', partners))  19.3 us
    pallas_call x4, Pallas kernels, attend(): pl.pallas_call(functools.partial(kernel_body, heads, first_head, len(earl...  17.2 us
    ppermute x27, waiting for transfers between devices, swapped(): found.append(lax.ppermute(parts[step], 'tok', partners))  6.94 us
    all_to_all x1, starting transfers between devices, step(): lax.all_to_all(errs[-1], ('tok', 'grp'), 0, 0, tiled=True)[:, 0]  4.33 us
    unnamed x20, local copies, waits for them, and re-layouts  3.6 us
    pallas_call x3, Pallas kernels, packed(): pl.pallas_call(functools.partial(pack_body, spans), out_shape=shapes, in_...  3.41 us
    ppermute x16, waiting for transfers between devices, level_swap(): lax.ppermute(value, axis, [pair for pair in partners if 0 <= pair[1] < co...  3.37 us
  transfers between devices with their start and end apart: 44, of which 5 were waited for; matrix products, arithmetic and copies ran while one was open for 4% of the time, Pallas kernels for 18%

profile of v6, /device:TPU:0, one launch (start us, length us, event | category | flops | bytes accessed | tf_op | source)
XLA Modules:
  0.0 118.3 jit_solution(14927758536328198972)
XLA Ops:
  0.7 1.5 %shard_map.96 = (bf16[128,256]{1,0:T(8,128)(2,1)S(1)}, bf16[128,256]{1,0:T(8,128)(2,1)S(1)}, bf16[128,256]{1,0:T(8,128)(2,1)S(1)}, bf16[128,256]{1,0:T(8,128)(2,1)S(1)}) custom-call(s32[3]{0:T(128)S(1)} %pad_add_fusion.place_ref, bf16[1,128,3072]{2,1,0:T(8,128)(2,1)} %first_ref.5, bf16[1,128,3072]{2,1,0:T(8,128)(2,1)} %second_ref.5), custom_call_target="tpu_custom_call" | custom-call | tf_op jit(solution)/shard_map/pallas_call | solution.py:77
  2.8 2.6 %collective-permute-start.4 = (bf16[128,256]{1,0:T(8,128)(2,1)S(1)}, bf16[128,256]{1,0:T(8,128)(2,1)S(1)}, u32[]{:S(2)}, u32[]{:S(2)}) collective-permute-start(bf16[128,256]{1,0:T(8,128)(2,1)S(1)} %get-tuple-element.48), channel_id=1, source_target_pairs={{0,4},{2,6},{4,0},{6,2},{8,12},{10,14},{12,8},{14,10},{16,20},{18,... | collective-permute-start | bytes 196616 | tf_op jit(solution)/shard_map/ppermute | solution.py:252
  5.4 1.1 shard_map.99
  6.7 1.9 %collective-permute-start.34 = (bf16[128,256]{1,0:T(8,128)(2,1)S(1)}, bf16[128,256]{1,0:T(8,128)(2,1)S(1)}, u32[]{:S(2)}, u32[]{:S(2)}) collective-permute-start(bf16[128,256]{1,0:T(8,128)(2,1)S(1)} %get-tuple-element.75), channel_id=1, source_target_pairs={{0,4},{2,6},{4,0},{6,2},{8,12},{10,14},{12,8},{14,10},{16,20},{18,... | collective-permute-start | bytes 196616 | tf_op jit(solution)/shard_map/ppermute | solution.py:252
  9.7 0.8 collective-permute-start.14
  10.5 1.1 collective-permute-start.15
  12.1 0.8 collective-permute-start.35
  12.9 1.6 %collective-permute-start.6 = (bf16[512,256]{1,0:T(8,128)(2,1)S(1)}, bf16[512,256]{1,0:T(8,128)(2,1)}, u32[]{:S(2)}, u32[]{:S(2)}) collective-permute-start(bf16[512,256]{1,0:T(8,128)(2,1)S(1)} %shard_map.97.refs_4_), channel_id=1, source_target_pairs={{0,8},{2,10},{4,12},{6,14},{8,0},{10,2},{12,4},{14,6},{16,24},{18,... | collective-permute-start | bytes 786440 | tf_op jit(solution)/shard_map/ppermute | solution.py:31
  14.4 4.8 %collective-permute-done.35.refs_3_ = bf16[128,256]{1,0:T(8,128)(2,1)S(1)} collective-permute-done((bf16[128,256]{1,0:T(8,128)(2,1)S(1)}, bf16[128,256]{1,0:T(8,128)(2,1)S(1)}, u32[]{:S(2)}, u32[]{:S(2)}) %collective-permute-start.35) | collective-permute-done | bytes 65568 | tf_op jit(solution)/shard_map/ppermute | solution.py:252
  19.2 0.8 collective-permute-start.23
  20.7 0.7 collective-permute-start.25
  22.2 1.4 %collective-permute-start.7 = (bf16[512,256]{1,0:T(8,128)(2,1)S(1)}, bf16[512,256]{1,0:T(8,128)(2,1)}, u32[]{:S(2)}, u32[]{:S(2)}) collective-permute-start(bf16[512,256]{1,0:T(8,128)(2,1)S(1)} %shard_map.97.refs_4_), channel_id=1, source_target_pairs={{8,16},{10,18},{12,20},{14,22},{16,8},{18,10},{20,12},{22,14},{9,1... | collective-permute-start | bytes 786440 | tf_op jit(solution)/shard_map/ppermute | solution.py:31
  24.9 3.8 %collective-permute-start.36 = (bf16[512,256]{1,0:T(8,128)(2,1)S(1)}, bf16[512,256]{1,0:T(8,128)(2,1)S(1)}, u32[]{:S(2)}, u32[]{:S(2)}) collective-permute-start(bf16[512,256]{1,0:T(8,128)(2,1)S(1)} %shard_map.104.refs_5_), channel_id=1, source_target_pairs={{0,8},{2,10},{4,12},{6,14},{8,0},{10,2},{12,4},{14,6},{16,24},{18,... | collective-permute-start | bytes 786440 | tf_op jit(solution)/shard_map/ppermute | solution.py:31
  28.7 1.4 %collective-permute-start.37 = (bf16[512,256]{1,0:T(8,128)(2,1)S(1)}, bf16[512,256]{1,0:T(8,128)(2,1)}, u32[]{:S(2)}, u32[]{:S(2)}) collective-permute-start(bf16[512,256]{1,0:T(8,128)(2,1)S(1)} %shard_map.104.refs_5_), channel_id=1, source_target_pairs={{8,16},{10,18},{12,20},{14,22},{16,8},{18,10},{20,12},{22,14},{9,1... | collective-permute-start | bytes 786440 | tf_op jit(solution)/shard_map/ppermute | solution.py:31
  30.1 1.7 %collective-permute-start.16 = (bf16[512,512]{1,0:T(8,128)(2,1)S(1)}, bf16[512,512]{1,0:T(8,128)(2,1)S(1)}, u32[]{:S(2)}, u32[]{:S(2)}) collective-permute-start(bf16[512,512]{1,0:T(8,128)(2,1)S(1)} %shard_map.100.refs_5_), channel_id=1, source_target_pairs={{0,8},{2,10},{4,12},{6,14},{8,0},{10,2},{12,4},{14,6},{16,24},{18,... | collective-permute-start | bytes 1572872 | tf_op jit(solution)/shard_map/ppermute | solution.py:31
  31.7 0.7 collective-permute-start.17
  33.0 0.7 collective-permute-start.27
  33.8 1.1 copy-done.2
  34.9 1.1 copy-done.3
  36.0 0.9 shard_map.95
  37.0 4.9 %collective-permute-start.26 = (bf16[512,512]{1,0:T(8,128)(2,1)S(1)}, bf16[512,512]{1,0:T(8,128)(2,1)S(1)}, u32[]{:S(2)}, u32[]{:S(2)}) collective-permute-start(bf16[512,512]{1,0:T(8,128)(2,1)S(1)} %shard_map.102.refs_5_), channel_id=1, source_target_pairs={{0,8},{2,10},{4,12},{6,14},{8,0},{10,2},{12,4},{14,6},{16,24},{18,... | collective-permute-start | bytes 1572872 | tf_op jit(solution)/shard_map/ppermute | solution.py:31
  41.9 0.9 constant_dynamic-slice_fusion.7
  42.8 0.9 constant_dynamic-slice_fusion.6
  43.8 3.3 %collective-permute-done.16.refs_6_ = bf16[512,512]{1,0:T(8,128)(2,1)S(1)} collective-permute-done((bf16[512,512]{1,0:T(8,128)(2,1)S(1)}, bf16[512,512]{1,0:T(8,128)(2,1)S(1)}, u32[]{:S(2)}, u32[]{:S(2)}) %collective-permute-start.16) | collective-permute-done | bytes 524320 | tf_op jit(solution)/shard_map/ppermute | solution.py:31
  47.1 0.7 collective-permute-start.1
  48.3 3.6 %collective-permute-start.8 = (bf16[384,256]{1,0:T(8,128)(2,1)S(1)}, bf16[384,256]{1,0:T(8,128)(2,1)S(1)}, u32[]{:S(2)}, u32[]{:S(2)}) collective-permute-start(bf16[384,256]{1,0:T(8,128)(2,1)S(1)} %constant_dynamic-slice_fusion.7), channel_id=1, source_target_pairs={{0,8},{2,10},{4,12},{6,14},{8,0},{10,2},{12,4},{14,6},{16,24},{18,... | collective-permute-start | bytes 589832 | tf_op jit(solution)/shard_map/ppermute | solution.py:31
  51.9 10.9 %collective-permute-start.18 = (bf16[384,512]{1,0:T(8,128)(2,1)S(1)}, bf16[384,512]{1,0:T(8,128)(2,1)S(1)}, u32[]{:S(2)}, u32[]{:S(2)}) collective-permute-start(bf16[384,512]{1,0:T(8,128)(2,1)S(1)} %constant_dynamic-slice_fusion.5), channel_id=1, source_target_pairs={{0,8},{2,10},{4,12},{6,14},{8,0},{10,2},{12,4},{14,6},{16,24},{18,... | collective-permute-start | bytes 1179656 | tf_op jit(solution)/shard_map/ppermute | solution.py:31
  62.8 0.7 collective-permute-start.19
  63.6 0.7 collective-permute-start.9
  64.2 0.8 collective-permute-done.2.refs_3_.refs_4_
  65.1 3.7 %collective-permute-start.28 = (bf16[384,512]{1,0:T(8,128)(2,1)S(1)}, bf16[384,512]{1,0:T(8,128)(2,1)S(1)}, u32[]{:S(2)}, u32[]{:S(2)}) collective-permute-start(bf16[384,512]{1,0:T(8,128)(2,1)S(1)} %constant_dynamic-slice_fusion.3), channel_id=1, source_target_pairs={{0,8},{2,10},{4,12},{6,14},{8,0},{10,2},{12,4},{14,6},{16,24},{18,... | collective-permute-start | bytes 1179656 | tf_op jit(solution)/shard_map/ppermute | solution.py:31
  68.8 0.7 collective-permute-start.29
  69.5 0.9 constant_dynamic-slice_fusion.1
  70.5 10.4 %collective-permute-start.38 = (bf16[384,256]{1,0:T(8,128)(2,1)S(1)}, bf16[384,256]{1,0:T(8,128)(2,1)S(1)}, u32[]{:S(2)}, u32[]{:S(2)}) collective-permute-start(bf16[384,256]{1,0:T(8,128)(2,1)S(1)} %constant_dynamic-slice_fusion.1), channel_id=1, source_target_pairs={{0,8},{2,10},{4,12},{6,14},{8,0},{10,2},{12,4},{14,6},{16,24},{18,... | collective-permute-start | bytes 589832 | tf_op jit(solution)/shard_map/ppermute | solution.py:31
  80.9 0.8 collective-permute-start.39
  81.9 3.7 %shard_map.98 = (bf16[128,128]{1,0:T(8,128)(2,1)S(1)}, bf16[128,128]{1,0:T(8,128)(2,1)S(1)}, bf16[128,128]{1,0:T(8,128)(2,1)S(1)}, bf16[128,128]{1,0:T(8,128)(2,1)}, f32[8,128]{1,0:T(8,128)S(1)}) custom-call(s32[3]{0:T(128)S(1)} %pad_add_fusion.place_ref, s32[1,4]{1,0:T(1,128)S(1)} %copy-done.5, s32[1,16]{1,0:T(1,128)S(1)} %copy-done.4, ...), custom_call_target="tpu_custom_call" | custom-call | flops 268435456 | bytes 1703936 | tf_op jit(solution)/shard_map/pallas_call | solution.py:219
  85.6 5.1 %shard_map.101 = (bf16[128,256]{1,0:T(8,128)(2,1)S(1)}, bf16[128,256]{1,0:T(8,128)(2,1)}, bf16[128,256]{1,0:T(8,128)(2,1)S(1)}, bf16[128,256]{1,0:T(8,128)(2,1)S(1)}, f32[8,128]{1,0:T(8,128)S(1)}) custom-call(s32[3]{0:T(128)S(1)} %pad_add_fusion.place_ref, s32[1,4]{1,0:T(1,128)S(1)} %copy-done.5, s32[1,16]{1,0:T(1,128)S(1)} %copy-done.4, ...), custom_call_target="tpu_custom_call" | custom-call | flops 536870912 | bytes 3407872 | tf_op jit(solution)/shard_map/pallas_call | solution.py:219
  91.6 4.7 %shard_map.103 = (bf16[128,256]{1,0:T(8,128)(2,1)S(1)}, bf16[128,256]{1,0:T(8,128)(2,1)S(1)}, bf16[128,256]{1,0:T(8,128)(2,1)S(1)}, bf16[128,256]{1,0:T(8,128)(2,1)S(1)}, f32[8,128]{1,0:T(8,128)S(1)}) custom-call(s32[3]{0:T(128)S(1)} %pad_add_fusion.place_ref, s32[1,4]{1,0:T(1,128)S(1)} %copy-done.5, s32[1,16]{1,0:T(1,128)S(1)} %copy-done.4, ...), custom_call_target="tpu_custom_call" | custom-call | flops 536870912 | bytes 3407872 | tf_op jit(solution)/shard_map/pallas_call | solution.py:219
  96.4 1.3 %collective-permute-start.12 = (bf16[128,128]{1,0:T(8,128)(2,1)}, bf16[128,128]{1,0:T(8,128)(2,1)S(1)}, u32[]{:S(2)}, u32[]{:S(2)}) collective-permute-start(bf16[128,128]{1,0:T(8,128)(2,1)} %get-tuple-element.53), channel_id=1, source_target_pairs={{0,6},{2,4},{4,2},{6,0},{8,14},{10,12},{12,10},{14,8},{16,22},{18,... | collective-permute-start | bytes 98312 | tf_op jit(solution)/shard_map/ppermute | solution.py:252
  97.7 3.7 %shard_map.105 = (bf16[128,128]{1,0:T(8,128)(2,1)S(1)}, bf16[128,128]{1,0:T(8,128)(2,1)S(1)}, bf16[128,128]{1,0:T(8,128)(2,1)S(1)}, bf16[128,128]{1,0:T(8,128)(2,1)S(1)}, f32[32,128]{1,0:T(8,128)}) custom-call(s32[3]{0:T(128)S(1)} %pad_add_fusion.place_ref, s32[1,4]{1,0:T(1,128)S(1)} %copy-done.5, s32[1,16]{1,0:T(1,128)S(1)} %copy-done.4, ...), custom_call_target="tpu_custom_call" | custom-call | flops 268435456 | bytes 1703936 | tf_op jit(solution)/shard_map/pallas_call | solution.py:219
  101.6 0.7 collective-permute-start.41
  102.3 1.0 collective-permute-start.42
  103.3 4.3 %all-to-all-start = ((f32[32,1,128]{2,1,0:T(1,128)}), f32[32,1,128]{2,1,0:T(1,128)S(1)}, u32[]{:S(2)}, u32[]{:S(2)}) async-start(f32[32,1,128]{2,1,0:T(1,128)} %bitcast.14), calls=%async_computation | async-start | bytes 32768 | tf_op jit(solution)/shard_map/all_to_all | solution.py:305
  107.6 1.8 %collective-permute-start.21 = (bf16[128,256]{1,0:T(8,128)(2,1)S(1)}, bf16[128,256]{1,0:T(8,128)(2,1)S(1)}, u32[]{:S(2)}, u32[]{:S(2)}) collective-permute-start(bf16[128,256]{1,0:T(8,128)(2,1)S(1)} %copy-done.7), channel_id=1, source_target_pairs={{0,4},{2,6},{4,0},{6,2},{8,12},{10,14},{12,8},{14,10},{16,20},{18,... | collective-permute-start | bytes 196616 | tf_op jit(solution)/shard_map/ppermute | solution.py:252
  109.9 1.8 %collective-permute-start.31 = (bf16[128,256]{1,0:T(8,128)(2,1)S(1)}, bf16[128,256]{1,0:T(8,128)(2,1)S(1)}, u32[]{:S(2)}, u32[]{:S(2)}) collective-permute-start(bf16[128,256]{1,0:T(8,128)(2,1)S(1)} %get-tuple-element.70), channel_id=1, source_target_pairs={{0,4},{2,6},{4,0},{6,2},{8,12},{10,14},{12,8},{14,10},{16,20},{18,... | collective-permute-start | bytes 196616 | tf_op jit(solution)/shard_map/ppermute | solution.py:252
  111.6 3.2 %all-to-all-done = f32[32,1,128]{2,1,0:T(1,128)S(1)} async-done(((f32[32,1,128]{2,1,0:T(1,128)}), f32[32,1,128]{2,1,0:T(1,128)S(1)}, u32[]{:S(2)}, u32[]{:S(2)}) %all-to-all-start) | async-done | bytes 16416 | tf_op jit(solution)/shard_map/all_to_all | solution.py:305
  115.5 1.3 %collective-permute-done.32.refs_11_ = bf16[128,256]{1,0:T(8,128)(2,1)S(1)} collective-permute-done((bf16[128,256]{1,0:T(8,128)(2,1)S(1)}, bf16[128,256]{1,0:T(8,128)(2,1)S(1)}, u32[]{:S(2)}, u32[]{:S(2)}) %collective-permute-start.32) | collective-permute-done | bytes 65568 | tf_op jit(solution)/shard_map/ppermute | solution.py:252
  116.7 1.5 %unpack.1 = bf16[1,128,3072]{2,1,0:T(8,128)(2,1)} custom-call(s32[3]{0:T(128)S(1)} %pad_add_fusion.place_ref, bf16[128,128]{1,0:T(8,128)(2,1)S(1)} %get-tuple-element.50.refs_0_, bf16[128,128]{1,0:T(8,128)(2,1)S(1)} %collective-permute-done.10.refs_1_, bf16[128,128]{1,0:T(8,128)(2,1)S(1)} %collective-permute-done.11.refs_2_, ...), custom_call_target="tpu_custom_call" | custom-call | tf_op jit(solution)/shard_map/unpack/pallas_call | solution.py:117
  (91 shorter events, 8.9 us)
Async XLA Ops:
  0.7 4.7 %copy-start = (bf16[1,128,3072]{2,1,0:T(8,128)(2,1)S(1)}, bf16[1,128,3072]{2,1,0:T(8,128)(2,1)}, u32[]{:S(2)}) copy-start(bf16[1,128,3072]{2,1,0:T(8,128)(2,1)} %first_ref.5) | copy-start | bytes 2359300
  0.7 4.7 %copy-start.1 = (bf16[1,128,3072]{2,1,0:T(8,128)(2,1)S(1)}, bf16[1,128,3072]{2,1,0:T(8,128)(2,1)}, u32[]{:S(2)}) copy-start(bf16[1,128,3072]{2,1,0:T(8,128)(2,1)} %second_ref.5) | copy-start | bytes 2359300
  2.2 7.3 %collective-permute-start.3 = (bf16[128,256]{1,0:T(8,128)(2,1)S(1)}, bf16[128,256]{1,0:T(8,128)(2,1)S(1)}, u32[]{:S(2)}, u32[]{:S(2)}) collective-permute-start(bf16[128,256]{1,0:T(8,128)(2,1)S(1)} %get-tuple-element.47), channel_id=1, source_target_pairs={{0,2},{2,0},{4,6},{6,4},{8,10},{10,8},{12,14},{14,12},{16,18},{18,... | collective-permute-start | bytes 196616 | tf_op jit(solution)/shard_map/ppermute | solution.py:252
  2.8 6.9 %collective-permute-start.4 = (bf16[128,256]{1,0:T(8,128)(2,1)S(1)}, bf16[128,256]{1,0:T(8,128)(2,1)S(1)}, u32[]{:S(2)}, u32[]{:S(2)}) collective-permute-start(bf16[128,256]{1,0:T(8,128)(2,1)S(1)} %get-tuple-element.48), channel_id=1, source_target_pairs={{0,4},{2,6},{4,0},{6,2},{8,12},{10,14},{12,8},{14,10},{16,20},{18,... | collective-permute-start | bytes 196616 | tf_op jit(solution)/shard_map/ppermute | solution.py:252
  5.4 5.1 %collective-permute-start.5 = (bf16[128,256]{1,0:T(8,128)(2,1)S(1)}, bf16[128,256]{1,0:T(8,128)(2,1)S(1)}, u32[]{:S(2)}, u32[]{:S(2)}) collective-permute-start(bf16[128,256]{1,0:T(8,128)(2,1)S(1)} %get-tuple-element.49), channel_id=1, source_target_pairs={{0,6},{2,4},{4,2},{6,0},{8,14},{10,12},{12,10},{14,8},{16,22},{18,... | collective-permute-start | bytes 196616 | tf_op jit(solution)/shard_map/ppermute | solution.py:252
  6.5 5.6 %collective-permute-start.33 = (bf16[128,256]{1,0:T(8,128)(2,1)S(1)}, bf16[128,256]{1,0:T(8,128)(2,1)S(1)}, u32[]{:S(2)}, u32[]{:S(2)}) collective-permute-start(bf16[128,256]{1,0:T(8,128)(2,1)S(1)} %get-tuple-element.74), channel_id=1, source_target_pairs={{0,2},{2,0},{4,6},{6,4},{8,10},{10,8},{12,14},{14,12},{16,18},{18,... | collective-permute-start | bytes 196616 | tf_op jit(solution)/shard_map/ppermute | solution.py:252
  6.7 6.2 %collective-permute-start.34 = (bf16[128,256]{1,0:T(8,128)(2,1)S(1)}, bf16[128,256]{1,0:T(8,128)(2,1)S(1)}, u32[]{:S(2)}, u32[]{:S(2)}) collective-permute-start(bf16[128,256]{1,0:T(8,128)(2,1)S(1)} %get-tuple-element.75), channel_id=1, source_target_pairs={{0,4},{2,6},{4,0},{6,2},{8,12},{10,14},{12,8},{14,10},{16,20},{18,... | collective-permute-start | bytes 196616 | tf_op jit(solution)/shard_map/ppermute | solution.py:252
  9.6 10.4 %collective-permute-start.13 = (bf16[128,512]{1,0:T(8,128)(2,1)S(1)}, bf16[128,512]{1,0:T(8,128)(2,1)S(1)}, u32[]{:S(2)}, u32[]{:S(2)}) collective-permute-start(bf16[128,512]{1,0:T(8,128)(2,1)S(1)} %get-tuple-element.56), channel_id=1, source_target_pairs={{0,2},{2,0},{4,6},{6,4},{8,10},{10,8},{12,14},{14,12},{16,18},{18,... | collective-permute-start | bytes 393224 | tf_op jit(solution)/shard_map/ppermute | solution.py:252
  9.7 11.0 %collective-permute-start.14 = (bf16[128,512]{1,0:T(8,128)(2,1)S(1)}, bf16[128,512]{1,0:T(8,128)(2,1)S(1)}, u32[]{:S(2)}, u32[]{:S(2)}) collective-permute-start(bf16[128,512]{1,0:T(8,128)(2,1)S(1)} %get-tuple-element.57), channel_id=1, source_target_pairs={{0,4},{2,6},{4,0},{6,2},{8,12},{10,14},{12,8},{14,10},{16,20},{18,... | collective-permute-start | bytes 393224 | tf_op jit(solution)/shard_map/ppermute | solution.py:252
  10.5 11.7 %collective-permute-start.15 = (bf16[128,512]{1,0:T(8,128)(2,1)S(1)}, bf16[128,512]{1,0:T(8,128)(2,1)S(1)}, u32[]{:S(2)}, u32[]{:S(2)}) collective-permute-start(bf16[128,512]{1,0:T(8,128)(2,1)S(1)} %get-tuple-element.58), channel_id=1, source_target_pairs={{0,6},{2,4},{4,2},{6,0},{8,14},{10,12},{12,10},{14,8},{16,22},{18,... | collective-permute-start | bytes 393224 | tf_op jit(solution)/shard_map/ppermute | solution.py:252
  12.1 7.1 %collective-permute-start.35 = (bf16[128,256]{1,0:T(8,128)(2,1)S(1)}, bf16[128,256]{1,0:T(8,128)(2,1)S(1)}, u32[]{:S(2)}, u32[]{:S(2)}) collective-permute-start(bf16[128,256]{1,0:T(8,128)(2,1)S(1)} %get-tuple-element.76), channel_id=1, source_target_pairs={{0,6},{2,4},{4,2},{6,0},{8,14},{10,12},{12,10},{14,8},{16,22},{18,... | collective-permute-start | bytes 196616 | tf_op jit(solution)/shard_map/ppermute | solution.py:252
  12.9 18.9 %collective-permute-start.6 = (bf16[512,256]{1,0:T(8,128)(2,1)S(1)}, bf16[512,256]{1,0:T(8,128)(2,1)}, u32[]{:S(2)}, u32[]{:S(2)}) collective-permute-start(bf16[512,256]{1,0:T(8,128)(2,1)S(1)} %shard_map.97.refs_4_), channel_id=1, source_target_pairs={{0,8},{2,10},{4,12},{6,14},{8,0},{10,2},{12,4},{14,6},{16,24},{18,... | collective-permute-start | bytes 786440 | tf_op jit(solution)/shard_map/ppermute | solution.py:31
  19.2 5.7 %collective-permute-start.23 = (bf16[128,512]{1,0:T(8,128)(2,1)S(1)}, bf16[128,512]{1,0:T(8,128)(2,1)S(1)}, u32[]{:S(2)}, u32[]{:S(2)}) collective-permute-start(bf16[128,512]{1,0:T(8,128)(2,1)S(1)} %get-tuple-element.65), channel_id=1, source_target_pairs={{0,2},{2,0},{4,6},{6,4},{8,10},{10,8},{12,14},{14,12},{16,18},{18,... | collective-permute-start | bytes 393224 | tf_op jit(solution)/shard_map/ppermute | solution.py:252
  20.0 8.7 %collective-permute-start.24 = (bf16[128,512]{1,0:T(8,128)(2,1)S(1)}, bf16[128,512]{1,0:T(8,128)(2,1)S(1)}, u32[]{:S(2)}, u32[]{:S(2)}) collective-permute-start(bf16[128,512]{1,0:T(8,128)(2,1)S(1)} %get-tuple-element.66), channel_id=1, source_target_pairs={{0,4},{2,6},{4,0},{6,2},{8,12},{10,14},{12,8},{14,10},{16,20},{18,... | collective-permute-start | bytes 393224 | tf_op jit(solution)/shard_map/ppermute | solution.py:252
  20.7 9.4 %collective-permute-start.25 = (bf16[128,512]{1,0:T(8,128)(2,1)S(1)}, bf16[128,512]{1,0:T(8,128)(2,1)S(1)}, u32[]{:S(2)}, u32[]{:S(2)}) collective-permute-start(bf16[128,512]{1,0:T(8,128)(2,1)S(1)} %get-tuple-element.67), channel_id=1, source_target_pairs={{0,6},{2,4},{4,2},{6,0},{8,14},{10,12},{12,10},{14,8},{16,22},{18,... | collective-permute-start | bytes 393224 | tf_op jit(solution)/shard_map/ppermute | solution.py:252
  22.2 10.8 %collective-permute-start.7 = (bf16[512,256]{1,0:T(8,128)(2,1)S(1)}, bf16[512,256]{1,0:T(8,128)(2,1)}, u32[]{:S(2)}, u32[]{:S(2)}) collective-permute-start(bf16[512,256]{1,0:T(8,128)(2,1)S(1)} %shard_map.97.refs_4_), channel_id=1, source_target_pairs={{8,16},{10,18},{12,20},{14,22},{16,8},{18,10},{20,12},{22,14},{9,1... | collective-permute-start | bytes 786440 | tf_op jit(solution)/shard_map/ppermute | solution.py:31
  24.9 12.0 %collective-permute-start.36 = (bf16[512,256]{1,0:T(8,128)(2,1)S(1)}, bf16[512,256]{1,0:T(8,128)(2,1)S(1)}, u32[]{:S(2)}, u32[]{:S(2)}) collective-permute-start(bf16[512,256]{1,0:T(8,128)(2,1)S(1)} %shard_map.104.refs_5_), channel_id=1, source_target_pairs={{0,8},{2,10},{4,12},{6,14},{8,0},{10,2},{12,4},{14,6},{16,24},{18,... | collective-permute-start | bytes 786440 | tf_op jit(solution)/shard_map/ppermute | solution.py:31
  28.7 8.3 %collective-permute-start.37 = (bf16[512,256]{1,0:T(8,128)(2,1)S(1)}, bf16[512,256]{1,0:T(8,128)(2,1)}, u32[]{:S(2)}, u32[]{:S(2)}) collective-permute-start(bf16[512,256]{1,0:T(8,128)(2,1)S(1)} %shard_map.104.refs_5_), channel_id=1, source_target_pairs={{8,16},{10,18},{12,20},{14,22},{16,8},{18,10},{20,12},{22,14},{9,1... | collective-permute-start | bytes 786440 | tf_op jit(solution)/shard_map/ppermute | solution.py:31
  30.1 17.0 %collective-permute-start.16 = (bf16[512,512]{1,0:T(8,128)(2,1)S(1)}, bf16[512,512]{1,0:T(8,128)(2,1)S(1)}, u32[]{:S(2)}, u32[]{:S(2)}) collective-permute-start(bf16[512,512]{1,0:T(8,128)(2,1)S(1)} %shard_map.100.refs_5_), channel_id=1, source_target_pairs={{0,8},{2,10},{4,12},{6,14},{8,0},{10,2},{12,4},{14,6},{16,24},{18,... | collective-permute-start | bytes 1572872 | tf_op jit(solution)/shard_map/ppermute | solution.py:31
  31.7 16.0 %collective-permute-start.17 = (bf16[512,512]{1,0:T(8,128)(2,1)S(1)}, bf16[512,512]{1,0:T(8,128)(2,1)S(1)}, u32[]{:S(2)}, u32[]{:S(2)}) collective-permute-start(bf16[512,512]{1,0:T(8,128)(2,1)S(1)} %shard_map.100.refs_5_), channel_id=1, source_target_pairs={{8,16},{10,18},{12,20},{14,22},{16,8},{18,10},{20,12},{22,14},{9,1... | collective-permute-start | bytes 1572872 | tf_op jit(solution)/shard_map/ppermute | solution.py:31
  33.0 18.8 %collective-permute-start.27 = (bf16[512,512]{1,0:T(8,128)(2,1)S(1)}, bf16[512,512]{1,0:T(8,128)(2,1)S(1)}, u32[]{:S(2)}, u32[]{:S(2)}) collective-permute-start(bf16[512,512]{1,0:T(8,128)(2,1)S(1)} %shard_map.102.refs_5_), channel_id=1, source_target_pairs={{8,16},{10,18},{12,20},{14,22},{16,8},{18,10},{20,12},{22,14},{9,1... | collective-permute-start | bytes 1572872 | tf_op jit(solution)/shard_map/ppermute | solution.py:31
  36.9 11.4 %collective-permute-start = (bf16[128,1536]{1,0:T(8,128)(2,1)S(1)}, bf16[128,1536]{1,0:T(8,128)(2,1)S(1)}, u32[]{:S(2)}, u32[]{:S(2)}) collective-permute-start(bf16[128,1536]{1,0:T(8,128)(2,1)S(1)} %get-tuple-element.43), channel_id=1, source_target_pairs={{0,2},{2,0},{4,6},{6,4},{8,10},{10,8},{12,14},{14,12},{16,18},{18,... | collective-permute-start | bytes 1179656 | tf_op jit(solution)/shard_map/ppermute | solution.py:252
  37.0 25.8 %collective-permute-start.26 = (bf16[512,512]{1,0:T(8,128)(2,1)S(1)}, bf16[512,512]{1,0:T(8,128)(2,1)S(1)}, u32[]{:S(2)}, u32[]{:S(2)}) collective-permute-start(bf16[512,512]{1,0:T(8,128)(2,1)S(1)} %shard_map.102.refs_5_), channel_id=1, source_target_pairs={{0,8},{2,10},{4,12},{6,14},{8,0},{10,2},{12,4},{14,6},{16,24},{18,... | collective-permute-start | bytes 1572872 | tf_op jit(solution)/shard_map/ppermute | solution.py:31
  47.1 16.5 %collective-permute-start.1 = (bf16[128,1536]{1,0:T(8,128)(2,1)S(1)}, bf16[128,1536]{1,0:T(8,128)(2,1)S(1)}, u32[]{:S(2)}, u32[]{:S(2)}) collective-permute-start(bf16[128,1536]{1,0:T(8,128)(2,1)S(1)} %get-tuple-element.44), channel_id=1, source_target_pairs={{0,4},{2,6},{4,0},{6,2},{8,12},{10,14},{12,8},{14,10},{16,20},{18,... | collective-permute-start | bytes 1179656 | tf_op jit(solution)/shard_map/ppermute | solution.py:252
  47.8 17.3 %collective-permute-start.2 = (bf16[128,1536]{1,0:T(8,128)(2,1)S(1)}, bf16[128,1536]{1,0:T(8,128)(2,1)S(1)}, u32[]{:S(2)}, u32[]{:S(2)}) collective-permute-start(bf16[128,1536]{1,0:T(8,128)(2,1)S(1)} %get-tuple-element.45), channel_id=1, source_target_pairs={{0,6},{2,4},{4,2},{6,0},{8,14},{10,12},{12,10},{14,8},{16,22},{18,... | collective-permute-start | bytes 1179656 | tf_op jit(solution)/shard_map/ppermute | solution.py:252
  48.3 20.5 %collective-permute-start.8 = (bf16[384,256]{1,0:T(8,128)(2,1)S(1)}, bf16[384,256]{1,0:T(8,128)(2,1)S(1)}, u32[]{:S(2)}, u32[]{:S(2)}) collective-permute-start(bf16[384,256]{1,0:T(8,128)(2,1)S(1)} %constant_dynamic-slice_fusion.7), channel_id=1, source_target_pairs={{0,8},{2,10},{4,12},{6,14},{8,0},{10,2},{12,4},{14,6},{16,24},{18,... | collective-permute-start | bytes 589832 | tf_op jit(solution)/shard_map/ppermute | solution.py:31
  51.9 29.0 %collective-permute-start.18 = (bf16[384,512]{1,0:T(8,128)(2,1)S(1)}, bf16[384,512]{1,0:T(8,128)(2,1)S(1)}, u32[]{:S(2)}, u32[]{:S(2)}) collective-permute-start(bf16[384,512]{1,0:T(8,128)(2,1)S(1)} %constant_dynamic-slice_fusion.5), channel_id=1, source_target_pairs={{0,8},{2,10},{4,12},{6,14},{8,0},{10,2},{12,4},{14,6},{16,24},{18,... | collective-permute-start | bytes 1179656 | tf_op jit(solution)/shard_map/ppermute | solution.py:31
  62.8 22.8 %collective-permute-start.19 = (bf16[384,512]{1,0:T(8,128)(2,1)S(1)}, bf16[384,512]{1,0:T(8,128)(2,1)S(1)}, u32[]{:S(2)}, u32[]{:S(2)}) collective-permute-start(bf16[384,512]{1,0:T(8,128)(2,1)S(1)} %constant_dynamic-slice_fusion.4), channel_id=1, source_target_pairs={{8,16},{10,18},{12,20},{14,22},{16,8},{18,10},{20,12},{22,14},{9,1... | collective-permute-start | bytes 1179656 | tf_op jit(solution)/shard_map/ppermute | solution.py:31
  63.6 6.9 %collective-permute-start.9 = (bf16[384,256]{1,0:T(8,128)(2,1)S(1)}, bf16[384,256]{1,0:T(8,128)(2,1)S(1)}, u32[]{:S(2)}, u32[]{:S(2)}) collective-permute-start(bf16[384,256]{1,0:T(8,128)(2,1)S(1)} %constant_dynamic-slice_fusion.6), channel_id=1, source_target_pairs={{8,16},{10,18},{12,20},{14,22},{16,8},{18,10},{20,12},{22,14},{9,1... | collective-permute-start | bytes 589832 | tf_op jit(solution)/shard_map/ppermute | solution.py:31
  65.1 25.7 %collective-permute-start.28 = (bf16[384,512]{1,0:T(8,128)(2,1)S(1)}, bf16[384,512]{1,0:T(8,128)(2,1)S(1)}, u32[]{:S(2)}, u32[]{:S(2)}) collective-permute-start(bf16[384,512]{1,0:T(8,128)(2,1)S(1)} %constant_dynamic-slice_fusion.3), channel_id=1, source_target_pairs={{0,8},{2,10},{4,12},{6,14},{8,0},{10,2},{12,4},{14,6},{16,24},{18,... | collective-permute-start | bytes 1179656 | tf_op jit(solution)/shard_map/ppermute | solution.py:31
  68.8 22.6 %collective-permute-start.29 = (bf16[384,512]{1,0:T(8,128)(2,1)S(1)}, bf16[384,512]{1,0:T(8,128)(2,1)S(1)}, u32[]{:S(2)}, u32[]{:S(2)}) collective-permute-start(bf16[384,512]{1,0:T(8,128)(2,1)S(1)} %constant_dynamic-slice_fusion.2), channel_id=1, source_target_pairs={{8,16},{10,18},{12,20},{14,22},{16,8},{18,10},{20,12},{22,14},{9,1... | collective-permute-start | bytes 1179656 | tf_op jit(solution)/shard_map/ppermute | solution.py:31
  70.5 25.9 %collective-permute-start.38 = (bf16[384,256]{1,0:T(8,128)(2,1)S(1)}, bf16[384,256]{1,0:T(8,128)(2,1)S(1)}, u32[]{:S(2)}, u32[]{:S(2)}) collective-permute-start(bf16[384,256]{1,0:T(8,128)(2,1)S(1)} %constant_dynamic-slice_fusion.1), channel_id=1, source_target_pairs={{0,8},{2,10},{4,12},{6,14},{8,0},{10,2},{12,4},{14,6},{16,24},{18,... | collective-permute-start | bytes 589832 | tf_op jit(solution)/shard_map/ppermute | solution.py:31
  80.9 16.8 %collective-permute-start.39 = (bf16[384,256]{1,0:T(8,128)(2,1)S(1)}, bf16[384,256]{1,0:T(8,128)(2,1)S(1)}, u32[]{:S(2)}, u32[]{:S(2)}) collective-permute-start(bf16[384,256]{1,0:T(8,128)(2,1)S(1)} %constant_dynamic-slice_fusion), channel_id=1, source_target_pairs={{8,16},{10,18},{12,20},{14,22},{16,8},{18,10},{20,12},{22,14},{9,1... | collective-permute-start | bytes 589832 | tf_op jit(solution)/shard_map/ppermute | solution.py:31
  85.6 16.0 %collective-permute-start.10 = (bf16[128,128]{1,0:T(8,128)(2,1)S(1)}, bf16[128,128]{1,0:T(8,128)(2,1)S(1)}, u32[]{:S(2)}, u32[]{:S(2)}) collective-permute-start(bf16[128,128]{1,0:T(8,128)(2,1)S(1)} %get-tuple-element.51), channel_id=1, source_target_pairs={{0,2},{2,0},{4,6},{6,4},{8,10},{10,8},{12,14},{14,12},{16,18},{18,... | collective-permute-start | bytes 98312 | tf_op jit(solution)/shard_map/ppermute | solution.py:252
  90.8 5.6 %copy-start.6 = (bf16[128,256]{1,0:T(8,128)(2,1)}, bf16[128,256]{1,0:T(8,128)(2,1)S(1)}, u32[]{:S(2)}) copy-start(bf16[128,256]{1,0:T(8,128)(2,1)S(1)} %get-tuple-element.61) | copy-start | bytes 196612
  90.8 11.5 %collective-permute-start.11 = (bf16[128,128]{1,0:T(8,128)(2,1)S(1)}, bf16[128,128]{1,0:T(8,128)(2,1)S(1)}, u32[]{:S(2)}, u32[]{:S(2)}) collective-permute-start(bf16[128,128]{1,0:T(8,128)(2,1)S(1)} %get-tuple-element.52), channel_id=1, source_target_pairs={{0,4},{2,6},{4,0},{6,2},{8,12},{10,14},{12,8},{14,10},{16,20},{18,... | collective-permute-start | bytes 98312 | tf_op jit(solution)/shard_map/ppermute | solution.py:252
  91.4 20.2 %collective-permute-start.20 = (bf16[128,256]{1,0:T(8,128)(2,1)}, bf16[128,256]{1,0:T(8,128)(2,1)S(1)}, u32[]{:S(2)}, u32[]{:S(2)}) collective-permute-start(bf16[128,256]{1,0:T(8,128)(2,1)} %get-tuple-element.60), channel_id=1, source_target_pairs={{0,2},{2,0},{4,6},{6,4},{8,10},{10,8},{12,14},{14,12},{16,18},{18,... | collective-permute-start | bytes 196616 | tf_op jit(solution)/shard_map/ppermute | solution.py:252
  96.4 11.3 %collective-permute-start.12 = (bf16[128,128]{1,0:T(8,128)(2,1)}, bf16[128,128]{1,0:T(8,128)(2,1)S(1)}, u32[]{:S(2)}, u32[]{:S(2)}) collective-permute-start(bf16[128,128]{1,0:T(8,128)(2,1)} %get-tuple-element.53), channel_id=1, source_target_pairs={{0,6},{2,4},{4,2},{6,0},{8,14},{10,12},{12,10},{14,8},{16,22},{18,... | collective-permute-start | bytes 98312 | tf_op jit(solution)/shard_map/ppermute | solution.py:252
  97.7 9.9 %copy-start.7 = (bf16[128,256]{1,0:T(8,128)(2,1)S(1)}, bf16[128,256]{1,0:T(8,128)(2,1)}, u32[]{:S(2)}) copy-start(bf16[128,256]{1,0:T(8,128)(2,1)} %copy-done.6) | copy-start | bytes 196612
  101.4 8.1 %collective-permute-start.40 = (bf16[128,128]{1,0:T(8,128)(2,1)S(1)}, bf16[128,128]{1,0:T(8,128)(2,1)S(1)}, u32[]{:S(2)}, u32[]{:S(2)}) collective-permute-start(bf16[128,128]{1,0:T(8,128)(2,1)S(1)} %get-tuple-element.78), channel_id=1, source_target_pairs={{0,2},{2,0},{4,6},{6,4},{8,10},{10,8},{12,14},{14,12},{16,18},{18,... | collective-permute-start | bytes 98312 | tf_op jit(solution)/shard_map/ppermute | solution.py:252
  101.6 7.8 %collective-permute-start.41 = (bf16[128,128]{1,0:T(8,128)(2,1)S(1)}, bf16[128,128]{1,0:T(8,128)(2,1)S(1)}, u32[]{:S(2)}, u32[]{:S(2)}) collective-permute-start(bf16[128,128]{1,0:T(8,128)(2,1)S(1)} %get-tuple-element.79), channel_id=1, source_target_pairs={{0,4},{2,6},{4,0},{6,2},{8,12},{10,14},{12,8},{14,10},{16,20},{18,... | collective-permute-start | bytes 98312 | tf_op jit(solution)/shard_map/ppermute | solution.py:252
  102.3 7.6 %collective-permute-start.42 = (bf16[128,128]{1,0:T(8,128)(2,1)S(1)}, bf16[128,128]{1,0:T(8,128)(2,1)S(1)}, u32[]{:S(2)}, u32[]{:S(2)}) collective-permute-start(bf16[128,128]{1,0:T(8,128)(2,1)S(1)} %get-tuple-element.80), channel_id=1, source_target_pairs={{0,6},{2,4},{4,2},{6,0},{8,14},{10,12},{12,10},{14,8},{16,22},{18,... | collective-permute-start | bytes 98312 | tf_op jit(solution)/shard_map/ppermute | solution.py:252
  103.3 11.6 %all-to-all-start = ((f32[32,1,128]{2,1,0:T(1,128)}), f32[32,1,128]{2,1,0:T(1,128)S(1)}, u32[]{:S(2)}, u32[]{:S(2)}) async-start(f32[32,1,128]{2,1,0:T(1,128)} %bitcast.14), calls=%async_computation | async-start | bytes 32768 | tf_op jit(solution)/shard_map/all_to_all | solution.py:305
  107.6 7.8 %collective-permute-start.21 = (bf16[128,256]{1,0:T(8,128)(2,1)S(1)}, bf16[128,256]{1,0:T(8,128)(2,1)S(1)}, u32[]{:S(2)}, u32[]{:S(2)}) collective-permute-start(bf16[128,256]{1,0:T(8,128)(2,1)S(1)} %copy-done.7), channel_id=1, source_target_pairs={{0,4},{2,6},{4,0},{6,2},{8,12},{10,14},{12,8},{14,10},{16,20},{18,... | collective-permute-start | bytes 196616 | tf_op jit(solution)/shard_map/ppermute | solution.py:252
  109.5 6.0 %collective-permute-start.22 = (bf16[128,256]{1,0:T(8,128)(2,1)S(1)}, bf16[128,256]{1,0:T(8,128)(2,1)S(1)}, u32[]{:S(2)}, u32[]{:S(2)}) collective-permute-start(bf16[128,256]{1,0:T(8,128)(2,1)S(1)} %get-tuple-element.62), channel_id=1, source_target_pairs={{0,6},{2,4},{4,2},{6,0},{8,14},{10,12},{12,10},{14,8},{16,22},{18,... | collective-permute-start | bytes 196616 | tf_op jit(solution)/shard_map/ppermute | solution.py:252
  109.5 6.0 %collective-permute-start.30 = (bf16[128,256]{1,0:T(8,128)(2,1)S(1)}, bf16[128,256]{1,0:T(8,128)(2,1)S(1)}, u32[]{:S(2)}, u32[]{:S(2)}) collective-permute-start(bf16[128,256]{1,0:T(8,128)(2,1)S(1)} %get-tuple-element.69), channel_id=1, source_target_pairs={{0,2},{2,0},{4,6},{6,4},{8,10},{10,8},{12,14},{14,12},{16,18},{18,... | collective-permute-start | bytes 196616 | tf_op jit(solution)/shard_map/ppermute | solution.py:252
  109.9 5.6 %collective-permute-start.31 = (bf16[128,256]{1,0:T(8,128)(2,1)S(1)}, bf16[128,256]{1,0:T(8,128)(2,1)S(1)}, u32[]{:S(2)}, u32[]{:S(2)}) collective-permute-start(bf16[128,256]{1,0:T(8,128)(2,1)S(1)} %get-tuple-element.70), channel_id=1, source_target_pairs={{0,4},{2,6},{4,0},{6,2},{8,12},{10,14},{12,8},{14,10},{16,20},{18,... | collective-permute-start | bytes 196616 | tf_op jit(solution)/shard_map/ppermute | solution.py:252
  111.6 5.1 %collective-permute-start.32 = (bf16[128,256]{1,0:T(8,128)(2,1)S(1)}, bf16[128,256]{1,0:T(8,128)(2,1)S(1)}, u32[]{:S(2)}, u32[]{:S(2)}) collective-permute-start(bf16[128,256]{1,0:T(8,128)(2,1)S(1)} %get-tuple-element.71), channel_id=1, source_target_pairs={{0,6},{2,4},{4,2},{6,0},{8,14},{10,12},{12,10},{14,8},{16,22},{18,... | collective-permute-start | bytes 196616 | tf_op jit(solution)/shard_map/ppermute | solution.py:252
  (6 other events, 6.2 us)
